TPU v7x, 32 devices: a whole 2x2x4 slice. The times are simulated.
32 devices in a mesh: tm: 4 (over y, core), lev: 8 (over z, x).
Axes of the slice: x: 2, y: 2, z: 4, core: 2. Of those that a mesh axis runs over, the one named last changes fastest.
Arguments:
- obs_cell: int32 [4, 16384], P('tm'), may hold values from 0 to 65535
- innovation: float32 [4, 64, 16384], P('tm', 'lev'), may hold values from -8 to 8
- tangent: float32 [4, 64, 128, 512], P('tm', 'lev'), may hold values from -0.45 to 0.45
- damping: float32 [4, 64, 128], P('tm'), may hold values from 0.05 to 0.95
- spread: float32 [64, 128], replicated, may hold values from 0.5 to 2
- vertical: float32 [64, 64], replicated, may hold values from -0.75 to 0.75
Outputs:
- gradient: float32 [64, 128, 2, 128], P(None, 'lev', None, 'tm')
All inputs are finite; a program needn't handle non-finite values.
Results may differ from a plain program's by a relative error of at most 0.0003.
Values sent between devices are 32-bit elements; how exact they have to be, the bound alone decides.
No kernel may reach another device: no remote copies, remote signals or barrier semaphores. Data moves between devices by JAX's collectives and lax.ppermute only.
A program may use at most 128 MiB of HBM per device.

v0:
```python
import math

import jax
import jax.numpy as jnp
from jax import lax
from jax.sharding import PartitionSpec as P

PRECISE = lax.Precision.HIGHEST
HALF_GAMMA_LOG = 0.5 * math.log(math.pi) - math.log(2.0)


def fourier_table(lon_count, wave_count):
    longitude = jnp.arange(lon_count, dtype=jnp.int32)[:, None]
    wavenumber = jnp.arange(wave_count, dtype=jnp.int32)[None, :]
    angles = (longitude * wavenumber % lon_count).astype(jnp.float32) * (2.0 * math.pi / lon_count)
    norm_factor = math.sqrt(2.0 / lon_count)
    columns = jnp.stack([jnp.cos(angles), jnp.sin(angles)], axis=2) * norm_factor
    return columns.reshape(lon_count, 2 * wave_count)


def legendre_table(first_wave, wave_block, lat_count, wave_count):
    orders = (first_wave + jnp.arange(wave_block, dtype=jnp.int32)).astype(jnp.float32)[:, None]
    row_index = jnp.arange(lat_count, dtype=jnp.float32)
    latitude = (row_index + 0.5) * (math.pi / lat_count) - 0.5 * math.pi
    sine_lat = jnp.sin(latitude)[None, :]
    cosine = jnp.cos(latitude)[None, :]
    logdiag = (
        -0.5 * math.log(2.0)
        + 0.5
        * (
            jax.scipy.special.gammaln(orders + 1.5)
            - HALF_GAMMA_LOG
            - jax.scipy.special.gammaln(orders + 1.0)
        )
        + orders * jnp.log(cosine)
    )
    diagonal = jnp.exp(logdiag)

    def advance(state_pair, degree):
        prev_one, prev_two = state_pair
        upward = jnp.sqrt(
            jnp.maximum(4.0 * degree * degree - 1.0, 1.0)
            / jnp.maximum(degree * degree - orders * orders, 1.0)
        )
        lower = degree - 1.0
        downward = jnp.sqrt(
            jnp.maximum(lower * lower - orders * orders, 0.0)
            / jnp.maximum(4.0 * lower * lower - 1.0, 1.0)
        )
        recurred = upward * (sine_lat * prev_one - downward * prev_two)
        current = jnp.where(degree < orders, 0.0, jnp.where(degree == orders, diagonal, recurred))
        return ((current, prev_one), current)

    zero_rows = jnp.zeros((wave_block, lat_count), jnp.float32)
    degrees = jnp.arange(wave_count, dtype=jnp.float32)
    _, values = lax.scan(advance, (zero_rows, zero_rows), degrees, unroll=16)
    weight = jnp.sqrt(math.pi / lat_count * cosine)
    return values * weight[None]


def forcing_field(cell_ids, innov_rows, lat_count, lon_count):
    flat_field = jnp.zeros((innov_rows.shape[0], lat_count * lon_count), jnp.float32)
    flat_field = flat_field.at[:, cell_ids].add(innov_rows)
    return flat_field.reshape(innov_rows.shape[0], lat_count, lon_count)


def shards(obs_cell, innovation, tangent, damping, spread, vertical):
    sections = lax.axis_size("tm")
    groups = lax.axis_size("lev")
    my_section = lax.axis_index("tm")
    lev_dev = tangent.shape[1]
    lat_rows = tangent.shape[2]
    lon_cols = tangent.shape[3]
    levels = damping.shape[1]
    wave_count = damping.shape[2]
    block_waves = wave_count // groups
    fourier = fourier_table(lon_cols, wave_count)
    legendre = legendre_table(
        lax.axis_index("lev") * block_waves, block_waves, lat_rows, wave_count
    )
    forcing = forcing_field(obs_cell[0], innovation[0], lat_rows, lon_cols)
    lat_block = lat_rows // sections
    level_block = levels // sections
    stacked = jnp.stack([tangent[0], forcing], axis=0)[None]
    received = lax.all_to_all(stacked, "tm", split_axis=3, concat_axis=0, tiled=True)
    damp_every = lax.all_gather(damping, "tm", axis=0, tiled=True)
    damp_mine = lax.dynamic_slice_in_dim(damp_every, my_section * level_block, level_block, 1)

    def sweep_step(step_index, carry):
        adjoint, total = carry
        time_now = sections - 1 - step_index
        fields = lax.dynamic_index_in_dim(received, time_now, 0, keepdims=False)
        forced = adjoint + fields[1]
        coeffs = jnp.einsum("klx,xc->klc", forced, fourier, precision=PRECISE)
        by_wave = lax.all_to_all(coeffs, "lev", split_axis=2, concat_axis=0, tiled=True)
        by_level = lax.all_to_all(by_wave, "tm", split_axis=0, concat_axis=1, tiled=True)
        by_level = by_level.reshape(level_block, lat_rows, block_waves, 2)
        spectral = jnp.einsum("klmp,nml->kmpn", by_level, legendre, precision=PRECISE)
        total = total + spectral
        rates = lax.dynamic_index_in_dim(damp_mine, time_now, 0, keepdims=False)
        filtered = spectral * rates[:, None, None, :]
        synthesized = jnp.einsum("kmpn,nml->klmp", filtered, legendre, precision=PRECISE)
        synthesized = synthesized.reshape(level_block, lat_rows, 2 * block_waves)
        back_rows = lax.all_to_all(synthesized, "tm", split_axis=1, concat_axis=0, tiled=True)
        back_waves = lax.all_to_all(back_rows, "lev", split_axis=0, concat_axis=2, tiled=True)
        gridded = jnp.einsum("klc,xc->klx", back_waves, fourier, precision=PRECISE)
        adjoint = fields[0] * forced + gridded
        return (adjoint, total)

    start_state = jnp.zeros((lev_dev, lat_block, lon_cols), jnp.float32)
    start_total = jnp.zeros((level_block, block_waves, 2, wave_count), jnp.float32)
    _, total = lax.fori_loop(0, sections, sweep_step, (start_state, start_total))
    spread_rows = lax.dynamic_slice_in_dim(spread, my_section * level_block, level_block, 0)
    vertical_rows = lax.dynamic_slice_in_dim(vertical, my_section * level_block, level_block, 0)
    scaled = total * spread_rows[:, None, None, :]
    partial_grad = jnp.einsum("kj,kmpn->jmpn", vertical_rows, scaled, precision=PRECISE)
    return lax.psum_scatter(partial_grad, "tm", scatter_dimension=3, tiled=True)


def solution(mesh):
    placed = (
        P("tm", None),
        P("tm", "lev", None),
        P("tm", "lev", None, None),
        P("tm", None, None),
        P(),
        P(),
    )
    return jax.shard_map(
        shards, mesh=mesh, in_specs=placed, out_specs=P(None, "lev", None, "tm"), check_vma=False
    )
```

profile of v0, /device:TPU:0, one launch (start us, length us, event | category | flops | bytes accessed | tf_op | source)
XLA Modules:
  0.0 1015.6 jit_solution(16356142913365503621)
XLA Ops:
  7.6 5.7 copy.49
  13.3 100.8 %scatter_custom_fusion = f32[8,65536]{0,1:T(8,128)} fusion(s32[16384]{0:T(1024)S(1)} %bitcast.447, f32[16384,8]{1,0:T(8,128)} %copy.49, f32[]{:T(128)} %constant.212.clone.1), kind=kCustom, calls=%fused_computation.145 | custom fusion | flops 131072 | bytes 2097664 | tf_op jit(solution)/shard_map/scatter-add | solution.py:63
  114.1 17.7 %copy.51 = f32[1,8,128,512]{3,1,0,2:T(8,128)S(1)} copy(f32[1,8,128,512]{1,3,2,0:T(8,128)} %bitcast.434) | data formatting | bytes 4194304 | tf_op jit(solution)/shard_map/stack;reshape | solution.py:84
  131.8 4.2 copy.50
  136.0 4.2 maximum_bitcast_fusion
  140.1 4.8 all-to-all-start.4
  145.2 500.8 %while.40 = (s32[]{:T(128)}, f32[16,128]{1,0:T(8,128)S(1)}, f32[16,128]{1,0:T(8,128)S(1)}, f32[8,16,16,128]{3,2,1,0:T(8,128)}, f32[8,16]{1,0:T(8,128)S(1)}, /*in...) while((s32[]{:T(128)}, f32[16,128]{1,0:T(8,128)S(1)}, ...), condition=%wide.region_2.3_spmd.clone.clone.clone.clone, body=%wide.region_1.2_spmd.clone.clone.clone.clone.sunk | while | flops 614194 | bytes 875717 | solution.py:56
  647.9 6.5 all_gather.3
  655.6 317.7 %while.39 = (s32[]{:T(128)}, f32[8,32,512]{2,1,0:T(8,128)}, f32[16,16,2,128]{3,0,2,1:T(8,128)}, f32[4,2,8,32,512]{4,2,1,3,0:T(8,128)}, f32[512,256]{1,0:T(8,128)...) while((s32[]{:T(128)}, f32[8,32,512]{2,1,0:T(8,128)}, ...), condition=%wide.region_4.5_spmd.clone, body=%wide.region_3.4_spmd.clone.sunk | while | flops 1007616000 | bytes 24142164 | solution.py:112
  659.4 15.4 %all_to_all.204 = f32[8,1,8192]{2,1,0:T(1,128)S(1)} all-to-all(f32[8,1,8192]{2,1,0:T(1,128)S(1)} %reshape.1394), channel_id=1, replica_groups=mesh['tm'=4,'lev'=8] {'lev'}, dimensions={0} | all-to-all | bytes 524288 | tf_op jit(solution)/shard_map/while/body/eval_jaxpr/all_to_all | solution.py:95
  684.2 6.0 all-to-all-done.1
  700.5 8.4 all_to_all.205
  715.5 3.6 all-to-all-start.3
  719.1 8.6 all-to-all-done.3
  740.9 11.9 %all_to_all.204 = f32[8,1,8192]{2,1,0:T(1,128)S(1)} all-to-all(f32[8,1,8192]{2,1,0:T(1,128)S(1)} %reshape.1394), channel_id=1, replica_groups=mesh['tm'=4,'lev'=8] {'lev'}, dimensions={0} | all-to-all | bytes 524288 | tf_op jit(solution)/shard_map/while/body/eval_jaxpr/all_to_all | solution.py:95
  762.2 6.0 all-to-all-done.1
  774.0 3.4 select_add_fusion.2
  779.4 8.4 all_to_all.205
  794.4 3.6 all-to-all-start.3
  798.0 8.6 all-to-all-done.3
  820.0 11.9 %all_to_all.204 = f32[8,1,8192]{2,1,0:T(1,128)S(1)} all-to-all(f32[8,1,8192]{2,1,0:T(1,128)S(1)} %reshape.1394), channel_id=1, replica_groups=mesh['tm'=4,'lev'=8] {'lev'}, dimensions={0} | all-to-all | bytes 524288 | tf_op jit(solution)/shard_map/while/body/eval_jaxpr/all_to_all | solution.py:95
  841.3 6.0 all-to-all-done.1
  858.5 8.4 all_to_all.205
  873.5 3.6 all-to-all-start.3
  877.1 8.6 all-to-all-done.3
  899.0 11.9 %all_to_all.204 = f32[8,1,8192]{2,1,0:T(1,128)S(1)} all-to-all(f32[8,1,8192]{2,1,0:T(1,128)S(1)} %reshape.1394), channel_id=1, replica_groups=mesh['tm'=4,'lev'=8] {'lev'}, dimensions={0} | all-to-all | bytes 524288 | tf_op jit(solution)/shard_map/while/body/eval_jaxpr/all_to_all | solution.py:95
  920.3 6.0 all-to-all-done.1
  937.6 8.4 all_to_all.205
  952.6 3.6 all-to-all-start.3
  956.1 8.6 all-to-all-done.3
  973.3 5.7 fusion.59
  979.1 29.6 %reduce-scatter.2.cloned.1.call-done = f32[64,16,2,32]{0,3,2,1:T(8,128)} async-done(((f32[64,16,2,128]{0,3,2,1:T(8,128)}), f32[64,16,2,32]{0,3,2,1:T(8,128)}) %reduce-scatter.2.cloned.1.call-update) | async-done | bytes 262160 | tf_op jit(solution)/shard_map/reduce_scatter | solution.py:117
  (571 shorter events, 266.6 us)
Async XLA Ops:
  6.5 966.8 %copy-start = (f32[64,64]{1,0:T(8,128)S(1)}, f32[64,64]{1,0:T(8,128)}, u32[]{:S(2)}) copy-start(f32[64,64]{1,0:T(8,128)} %param.15) | copy-start | bytes 49156
  140.1 515.4 %all-to-all-start.4 = ((f32[1,2,8,128,512]{4,2,1,0,3:T(8,128)}), f32[1,2,8,128,512]{4,2,1,0,3:T(8,128)}, u32[]{:S(2)}, u32[]{:S(2)}) async-start(f32[1,2,8,128,512]{4,2,1,0,3:T(8,128)} %maximum_bitcast_fusion), calls=%async_computation.4 | async-start | bytes 8388608 | tf_op jit(solution)/shard_map/all_to_all | solution.py:85
  145.0 863.7 %reduce-scatter.2.cloned.1.call-start = ((), (), s32[]{:S(2)}) async-start(), calls=%async_computation.6 | async-start | bytes 2621440 | tf_op jit(solution)/shard_map/reduce_scatter | solution.py:117
  646.0 1.9 copy-start.2
  646.0 9.2 copy-start.1
  680.8 9.4 all-to-all-start.1
  715.5 12.2 %all-to-all-start.3 = ((f32[8,1,8192]{2,1,0:T(1,128)}), f32[8,1,8192]{2,1,0:T(1,128)S(1)}, u32[]{:S(2)}, u32[]{:S(2)}) async-start(f32[8,1,8192]{2,1,0:T(1,128)} %reshape.1401), calls=%async_computation.3 | async-start | bytes 524288 | tf_op jit(solution)/shard_map/while/body/eval_jaxpr/all_to_all | solution.py:105
  758.8 9.4 all-to-all-start.1
  794.4 12.2 %all-to-all-start.3 = ((f32[8,1,8192]{2,1,0:T(1,128)}), f32[8,1,8192]{2,1,0:T(1,128)S(1)}, u32[]{:S(2)}, u32[]{:S(2)}) async-start(f32[8,1,8192]{2,1,0:T(1,128)} %reshape.1401), calls=%async_computation.3 | async-start | bytes 524288 | tf_op jit(solution)/shard_map/while/body/eval_jaxpr/all_to_all | solution.py:105
  837.8 9.4 all-to-all-start.1
  873.5 12.2 %all-to-all-start.3 = ((f32[8,1,8192]{2,1,0:T(1,128)}), f32[8,1,8192]{2,1,0:T(1,128)S(1)}, u32[]{:S(2)}, u32[]{:S(2)}) async-start(f32[8,1,8192]{2,1,0:T(1,128)} %reshape.1401), calls=%async_computation.3 | async-start | bytes 524288 | tf_op jit(solution)/shard_map/while/body/eval_jaxpr/all_to_all | solution.py:105
  916.9 9.4 all-to-all-start.1
  952.6 12.2 %all-to-all-start.3 = ((f32[8,1,8192]{2,1,0:T(1,128)}), f32[8,1,8192]{2,1,0:T(1,128)S(1)}, u32[]{:S(2)}, u32[]{:S(2)}) async-start(f32[8,1,8192]{2,1,0:T(1,128)} %reshape.1401), calls=%async_computation.3 | async-start | bytes 524288 | tf_op jit(solution)/shard_map/while/body/eval_jaxpr/all_to_all | solution.py:105
Sparse Core Ops, SparseCore 0:
  979.2 29.4 reduce-scatter.1
where the time goes:
time: 1030 us; the launch traced here: 1020 us
  loops' own time  396 us (38%)
  other arithmetic  224 us (22%)
  local copies, waits for them, and re-layouts  129 us (13%)
  blocking collectives  91.1 us (9%)
  waiting for transfers between devices  87.9 us (9%)
  matrix products  41.4 us (4%)
  starting transfers between devices  32.9 us (3%)
  between operations  13.5 us (1%)
    another operation x1, loops' own time, legendre_table(): _, values = lax.scan(advance, (zero_rows, zero_rows), degrees, unroll=16)  395 us
    scatter-add x1, other arithmetic, forcing_field(): flat_field = flat_field.at[:, cell_ids].add(innov_rows)  101 us
    eq x128, other arithmetic, advance(): degree == orders  79.5 us
    all_to_all x4, blocking collectives, sweep_step(): lax.all_to_all(coeffs, 'lev', split_axis=2, concat_axis=0, tiled=True)  51 us
    all_to_all x4, waiting for transfers between devices, sweep_step(): lax.all_to_all(back_rows, 'lev', split_axis=0, concat_axis=2, tiled=True)  34.5 us
    all_to_all x4, blocking collectives, sweep_step(): lax.all_to_all(synthesized, 'tm', split_axis=1, concat_axis=0, tiled=True)  33.6 us
    reduce_scatter x1, waiting for transfers between devices, shards(): return lax.psum_scatter(partial_grad, 'tm', scatter_dimension=3, tiled=True)  29.6 us
    all_to_all x4, waiting for transfers between devices, sweep_step(): lax.all_to_all(by_wave, 'tm', split_axis=0, concat_axis=1, tiled=True)  23.8 us
  transfers between devices with their start and end apart: 10, of which 9 were waited for; matrix products, arithmetic and copies ran while one was open for 11% of the time, Pallas kernels for 0%

commit v1 on v0

v1 whole, which is shorter than its diff:
```python
import math

import numpy as np

import jax
import jax.numpy as jnp
from jax import lax
from jax.experimental import pallas as pl
from jax.experimental.pallas import tpu as pltpu
from jax.sharding import PartitionSpec as P

PRECISE = lax.Precision.HIGHEST
LANES = 128
SUBLANES = 8
ACCUMULATORS = 8
OBS_BLOCK = 128
WAVE_UNROLL = 16
DEGREE_UNROLL = 16


def vmem():
    return pl.BlockSpec(memory_space=pltpu.VMEM)


def smem():
    return pl.BlockSpec(memory_space=pltpu.SMEM)


def fourier_rows(lon_count, wave_count):
    longitude = np.arange(lon_count)[None, :]
    wavenumber = np.arange(wave_count)[:, None]
    angles = (longitude * wavenumber % lon_count) * (2.0 * math.pi / lon_count)
    rows = np.concatenate([np.cos(angles), np.sin(angles)]) * math.sqrt(2.0 / lon_count)
    rows = rows.astype(np.float32)
    high = rows.astype(jnp.bfloat16)
    low = (rows - high.astype(np.float32)).astype(jnp.bfloat16)
    return high, low


def legendre_seeds(lat_count, wave_count):
    orders = np.arange(wave_count, dtype=np.float64)[:, None]
    degrees = np.arange(wave_count, dtype=np.float64)[None, :]
    latitude = (np.arange(lat_count) + 0.5) * (math.pi / lat_count) - 0.5 * math.pi
    sine = np.sin(latitude)[None, :]
    cosine = np.cos(latitude)[None, :]
    gammas = np.array(
        [
            math.lgamma(order + 1.5) - math.lgamma(1.5) - math.lgamma(order + 1.0)
            for order in range(wave_count)
        ]
    )[:, None]
    diagonal = np.exp(-0.5 * math.log(2.0) + 0.5 * gammas + orders * np.log(cosine))
    diagonal = diagonal * np.sqrt(math.pi / lat_count * cosine)
    upward = np.sqrt(
        np.maximum(4.0 * degrees**2 - 1.0, 1.0) / np.maximum(degrees**2 - orders**2, 1.0)
    )
    lower = degrees - 1.0
    downward = np.sqrt(
        np.maximum(lower**2 - orders**2, 0.0) / np.maximum(4.0 * lower**2 - 1.0, 1.0)
    )
    cast = lambda table: table.astype(np.float32)
    return cast(upward), cast(upward * downward), cast(diagonal), cast(sine)


def split_parts(values):
    high = values.astype(jnp.bfloat16)
    low = (values - high.astype(jnp.float32)).astype(jnp.bfloat16)
    return high, low


def dot(left, right, left_dim, right_dim):
    return lax.dot_general(
        left, right, (((left_dim,), (right_dim,)), ((), ())), preferred_element_type=jnp.float32
    )


def legendre_kernel(upward, downward, diagonal, sine, table, up_now, down_now, values):
    waves, lats = diagonal.shape
    pitch = values.shape[0] // waves
    up_now[...] = upward[...]
    down_now[...] = downward[...]
    order = lax.broadcasted_iota(jnp.int32, (waves, lats), 0)
    sine_rows = jnp.broadcast_to(sine[...], (waves, lats))

    def advance(group, state):
        one, two = state
        up = up_now[...]
        down = down_now[...]
        for step in range(DEGREE_UNROLL):
            degree = group * DEGREE_UNROLL + step
            seed = jnp.where(order == degree, diagonal[...], 0.0)
            current = (up[:, step : step + 1] * sine_rows) * one
            current = current - down[:, step : step + 1] * two + seed
            values[pl.ds(pl.multiple_of(degree * pitch, SUBLANES), waves), :] = current
            one, two = current, one
        up_now[...] = pltpu.roll(up, waves - DEGREE_UNROLL, 1)
        down_now[...] = pltpu.roll(down, waves - DEGREE_UNROLL, 1)
        return one, two

    zeros = jnp.zeros((waves, lats), jnp.float32)
    lax.fori_loop(0, waves // DEGREE_UNROLL, advance, (zeros, zeros))

    def emit(wave, carry):
        rows = values[pl.ds(wave, waves, stride=pitch), :]
        high, low = split_parts(rows)
        table[wave, 0:waves, :] = high
        table[wave, waves : 2 * waves, :] = low
        return carry

    lax.fori_loop(0, waves, emit, 0)


def legendre_table(lat_count, wave_count):
    pitch = wave_count + SUBLANES
    return pl.pallas_call(
        legendre_kernel,
        out_shape=jax.ShapeDtypeStruct((wave_count, 2 * wave_count, lat_count), jnp.bfloat16),
        in_specs=[vmem()] * 4,
        out_specs=vmem(),
        scratch_shapes=[
            pltpu.VMEM((wave_count, wave_count), jnp.float32),
            pltpu.VMEM((wave_count, wave_count), jnp.float32),
            pltpu.VMEM((wave_count * pitch, lat_count), jnp.float32),
        ],
        compiler_params=pltpu.CompilerParams(vmem_limit_bytes=40 * 2**20),
        name="legendre",
    )(*legendre_seeds(lat_count, wave_count))


def scatter_kernel(rows, low_lat, innov, damp, field, data, *sums):
    levels, obs = innov.shape
    lats = field.shape[1] - SUBLANES
    lons = field.shape[2]
    span = LANES // levels
    waves = damp.shape[1]
    for part in sums:
        part[...] = jnp.zeros(part.shape, jnp.float32)
    lane = lax.broadcasted_iota(jnp.int32, (levels, LANES), 1)
    level = lax.broadcasted_iota(jnp.int32, (levels, LANES), 0)
    place = (lane // span == level).astype(jnp.float32)
    one_row = jnp.ones((1, LANES), jnp.float32)
    lane_low = (lax.broadcasted_iota(jnp.int32, (OBS_BLOCK, LANES), 1) % span).astype(jnp.float32)

    def spread_out(block, carry):
        start = pl.multiple_of(block * OBS_BLOCK, OBS_BLOCK)
        values = innov[:, pl.ds(start, OBS_BLOCK)]
        expanded = lax.dot_general(
            values,
            place,
            (((0,), (0,)), ((), ())),
            precision=PRECISE,
            preferred_element_type=jnp.float32,
        )
        low = dot(low_lat[:, pl.ds(start, OBS_BLOCK)], one_row, 0, 0)
        data[pl.ds(start, OBS_BLOCK), :] = jnp.where(low == lane_low, expanded, 0.0)
        return carry

    lax.fori_loop(0, obs // OBS_BLOCK, spread_out, 0)

    def scatter(block, carry):
        start = pl.multiple_of(block * OBS_BLOCK, OBS_BLOCK)
        for step in range(OBS_BLOCK):
            part = sums[step % ACCUMULATORS]
            row = rows[start + step]
            part[pl.ds(row, 1), :] = part[pl.ds(row, 1), :] + data[pl.ds(start + step, 1), :]
        return carry

    lax.fori_loop(0, obs // OBS_BLOCK, scatter, 0)

    for high in range(lats // span):
        for west in range(lons // LANES):
            block = pl.ds(high * lons + west * LANES, LANES)
            total = sums[0][block, :]
            for part in sums[1:]:
                total = total + part[block, :]
            turned = total.T
            for k in range(levels):
                field[k, high * span : (high + 1) * span, west * LANES : (west + 1) * LANES] = (
                    turned[k * span : (k + 1) * span, :]
                )
    field[:, lats:, :] = jnp.zeros((levels, SUBLANES, lons), jnp.float32)
    for k in range(levels):
        field[k, lats : lats + 1, 0:waves] = damp[k : k + 1, :]


def forcing_field(cells, innov, damp, lats, lons):
    levels, obs = innov.shape
    span = LANES // levels
    lat = cells // lons
    rows = (lat // span) * lons + cells % lons
    low_lat = (lat % span).astype(jnp.float32)[None, :]
    sum_rows = lats * lons // span
    return pl.pallas_call(
        scatter_kernel,
        out_shape=jax.ShapeDtypeStruct((levels, lats + SUBLANES, lons), jnp.float32),
        in_specs=[smem(), vmem(), vmem(), vmem()],
        out_specs=vmem(),
        scratch_shapes=[pltpu.VMEM((obs, LANES), jnp.float32)]
        + [pltpu.VMEM((sum_rows, LANES), jnp.float32)] * ACCUMULATORS,
        compiler_params=pltpu.CompilerParams(vmem_limit_bytes=50 * 2**20),
        name="scatter",
    )(rows, low_lat, innov, damp)


def sweep_kernel(forcing, tangent, spread, fourier_high, fourier_low, table, out, forced, work, total):
    waves = table.shape[0]
    lats = table.shape[2]
    times = out.shape[0]
    degree_block = waves // times
    kept = forcing.shape[0] // times
    half = 2 * kept
    rows = max(SUBLANES, 2 * half)
    copies = rows // half
    row = lax.broadcasted_iota(jnp.int32, (rows, waves), 0)
    is_high = (row // half) % 2 == 0
    total[...] = jnp.zeros(total.shape, jnp.float32)

    for time in range(times - 1, -1, -1):
        for k in range(kept):
            here = slice(k * lats, (k + 1) * lats)
            if time == times - 1:
                forced[here, :] = forcing[time * kept + k, 0:lats, :]
            else:
                forced[here, :] = forced[here, :] + forcing[time * kept + k, 0:lats, :]
        high, low = split_parts(forced[...])
        coeffs = dot(fourier_high[...], high, 1, 1)
        coeffs = coeffs + dot(fourier_low[...], high, 1, 1)
        coeffs = coeffs + dot(fourier_high[...], low, 1, 1)
        for k in range(kept):
            for p in range(2):
                piece = coeffs[p * waves : (p + 1) * waves, k * lats : (k + 1) * lats]
                piece_high = piece.astype(jnp.bfloat16).astype(jnp.float32)
                piece_low = piece - piece_high
                for copy in range(copies):
                    at = copy * half + 2 * k + p
                    work[pl.ds(at, waves, stride=rows), :] = (
                        piece_high if copy % 2 == 0 else piece_low
                    )
        damp_rows = []
        for k in range(kept):
            damp_row = forcing[time * kept + k, lats : lats + 1, 0:waves]
            damp_rows += [damp_row, damp_row]
        damp = jnp.concatenate(damp_rows * copies, axis=0)

        def per_wave(group, carry):
            for step in range(WAVE_UNROLL):
                wave = group * WAVE_UNROLL + step
                at = pl.ds(pl.multiple_of(wave * rows, rows), rows)
                both = table[wave]
                product = dot(work[at, :].astype(jnp.bfloat16), both, 1, 1)
                product = product[:, 0:waves] + product[:, waves:]
                spectral = product + pltpu.roll(product, half, 0)
                total[at, :] = total[at, :] + spectral
                if time > 0:
                    filtered = spectral * damp
                    part = filtered.astype(jnp.bfloat16).astype(jnp.float32)
                    part = jnp.where(is_high, part, filtered - part).astype(jnp.bfloat16)
                    result = dot(jnp.concatenate([part, part], axis=1), both, 1, 0)
                    work[at, :] = result + pltpu.roll(result, half, 0)
            return carry

        lax.fori_loop(0, waves // WAVE_UNROLL, per_wave, 0)
        if time > 0:
            for k in range(kept):
                parts = [work[pl.ds(2 * k + p, waves, stride=rows), :].T for p in range(2)]
                synth_high, synth_low = split_parts(jnp.concatenate(parts, axis=1))
                gridded = dot(synth_high, fourier_high[...], 1, 0)
                gridded = gridded + dot(synth_high, fourier_low[...], 1, 0)
                gridded = gridded + dot(synth_low, fourier_high[...], 1, 0)
                here = slice(k * lats, (k + 1) * lats)
                forced[here, :] = tangent[time * kept + k] * forced[here, :] + gridded

    scaled = []
    for k in range(kept):
        for p in range(2):
            scaled.append(
                total[pl.ds(2 * k + p, waves, stride=rows), :] * spread[k : k + 1, :]
            )
    for block in range(times):
        cols = slice(block * degree_block, (block + 1) * degree_block)
        out[block] = jnp.concatenate([piece[:, cols] for piece in scaled], axis=1)


def sweep(forcing, tangent, spread, table, times):
    kept = spread.shape[0]
    lats, lons = tangent.shape[1:]
    waves = table.shape[0]
    rows = max(SUBLANES, 4 * kept)
    high, low = fourier_rows(lons, waves)
    return pl.pallas_call(
        sweep_kernel,
        out_shape=jax.ShapeDtypeStruct((times, waves, 2 * kept * waves // times), jnp.float32),
        in_specs=[vmem()] * 6,
        out_specs=vmem(),
        scratch_shapes=[
            pltpu.VMEM((kept * lats, lons), jnp.float32),
            pltpu.VMEM((waves * rows, lats), jnp.float32),
            pltpu.VMEM((waves * rows, waves), jnp.float32),
        ],
        compiler_params=pltpu.CompilerParams(vmem_limit_bytes=50 * 2**20),
        name="sweep",
    )(forcing, tangent, spread, high, low, table)


def shards(obs_cell, innovation, tangent, damping, spread, vertical):
    sections = lax.axis_size("tm")
    groups = lax.axis_size("lev")
    my_section = lax.axis_index("tm")
    my_group = lax.axis_index("lev")
    lev_dev, lat_rows, lon_cols = tangent.shape[1:]
    wave_count = damping.shape[2]
    repeat = max(1, sections // lev_dev)
    kept = max(1, lev_dev // sections)
    my_first = my_group * lev_dev + (my_section // repeat) * kept

    def exchange(field):
        field = jnp.repeat(field, repeat, axis=0) if repeat > 1 else field
        return lax.all_to_all(field, "tm", split_axis=0, concat_axis=0, tiled=True)

    tangent_mine = exchange(tangent[0])
    damp_here = lax.dynamic_slice_in_dim(damping[0], my_group * lev_dev, lev_dev, 0)
    forcing = forcing_field(obs_cell[0], innovation[0], damp_here, lat_rows, lon_cols)
    forcing_mine = exchange(forcing)
    table = legendre_table(lat_rows, wave_count)
    spread_mine = lax.dynamic_slice_in_dim(spread, my_first, kept, 0)
    blocks = sweep(forcing_mine, tangent_mine, spread_mine, table, sections)

    block_waves = wave_count // groups
    block_degrees = wave_count // sections
    blocks = blocks.reshape(sections * groups, block_waves, 2 * kept * block_degrees)
    owned = lax.all_to_all(blocks, ("tm", "lev"), split_axis=0, concat_axis=0, tiled=True)
    owned = owned.reshape(sections, groups, block_waves, kept, 2, block_degrees)[::repeat]
    mixing = vertical.reshape(groups, sections // repeat, kept, vertical.shape[1])
    return jnp.einsum("gukl,ugmkpn->lmpn", mixing, owned, precision=PRECISE)


def solution(mesh):
    placed = (
        P("tm", None),
        P("tm", "lev", None),
        P("tm", "lev", None, None),
        P("tm", None, None),
        P(),
        P(),
    )
    return jax.shard_map(
        shards, mesh=mesh, in_specs=placed, out_specs=P(None, "lev", None, "tm"), check_vma=False
    )
```

time: 1030 us -> 185 us (0.18); the launches traced: 1020 us -> 184 us
  loops' own time: 396 us -> 0 us
  other arithmetic: 224 us -> 0.6 us
  Pallas kernels: 0 us -> 135 us
  local copies, waits for them, and re-layouts: 129 us -> 5.48 us
  blocking collectives: 91.1 us -> 16 us
  waiting for transfers between devices: 87.9 us -> 15 us
  matrix products: 41.4 us -> 2.96 us
  starting transfers between devices: 32.9 us -> 9.07 us
  between operations: 13.5 us -> 0.14 us
    another operation x2 -> x0, loops' own time: 396 us -> none  [the longest x1 395 us: legendre_table(): _, values = lax.scan(advance, (zero_rows, zero_rows), degrees, unroll=16)]
    pallas_call x0 -> x3, Pallas kernels: none -> 135 us  [the longest x1 73.4 us: sweep(): pl.pallas_call(sweep_kernel, out_shape=jax.ShapeDtypeStruct((times, waves...]
    scatter-add x1 -> x0, other arithmetic: 101 us -> none  [forcing_field(): flat_field = flat_field.at[:, cell_ids].add(innov_rows)]
    eq x128 -> x0, other arithmetic: 79.5 us -> none  [advance(): degree == orders]
    all_to_all x8 -> x1, blocking collectives: 84.6 us -> 16 us  [shards(): lax.all_to_all(blocks, ('tm', 'lev'), split_axis=0, concat_axis=0, tiled=...]
    all_to_all x40 -> x0, local copies, waits for them, and re-layouts: 46.8 us -> none  [the longest x12 15 us: sweep_step(): lax.all_to_all(back_rows, 'lev', split_axis=0, concat_axis=2, tiled=True)]
    all_to_all x9 -> x2, waiting for transfers between devices: 58.3 us -> 15 us  [exchange(): return lax.all_to_all(field, 'tm', split_axis=0, concat_axis=0, tiled=True)]
    dot_general x17 -> x1, matrix products: 41.4 us -> 2.96 us  [shards(): return jnp.einsum('gukl,ugmkpn->lmpn', mixing, owned, precision=PRECISE)]
  transfers between devices with their start and end apart: 10 -> 2, of which waited for: 9 -> 1; matrix products, arithmetic and copies ran while one was open for 11% -> 1% of each run, Pallas kernels for 0% -> 33%
where the time goes in v1:
time: 185 us; the launch traced here: 184 us
  Pallas kernels  135 us (73%)
  blocking collectives  16 us (9%)
  waiting for transfers between devices  15 us (8%)
  starting transfers between devices  9.07 us (5%)
  local copies, waits for them, and re-layouts  5.48 us (3%)
  matrix products  2.96 us (2%)
    pallas_call x1, Pallas kernels, sweep(): pl.pallas_call(sweep_kernel, out_shape=jax.ShapeDtypeStruct((times, waves...  73.4 us
    pallas_call x1, Pallas kernels, forcing_field(): pl.pallas_call(scatter_kernel, out_shape=jax.ShapeDtypeStruct((levels, la...  53.5 us
    all_to_all x1, blocking collectives, shards(): lax.all_to_all(blocks, ('tm', 'lev'), split_axis=0, concat_axis=0, tiled=...  16 us
    all_to_all x2, waiting for transfers between devices, exchange(): return lax.all_to_all(field, 'tm', split_axis=0, concat_axis=0, tiled=True)  15 us
    all_to_all x2, starting transfers between devices, exchange(): return lax.all_to_all(field, 'tm', split_axis=0, concat_axis=0, tiled=True)  9.07 us
    pallas_call x1, Pallas kernels, legendre_table(): pl.pallas_call(legendre_kernel, out_shape=jax.ShapeDtypeStruct((wave_coun...  8.2 us
  transfers between devices with their start and end apart: 2, of which 1 were waited for; matrix products, arithmetic and copies ran while one was open for 1% of the time, Pallas kernels for 33%

profile of v1, /device:TPU:0, one launch (start us, length us, event | category | flops | bytes accessed | tf_op | source)
XLA Modules:
  0.0 184.3 jit_solution(1998108971007162092)
XLA Ops:
  0.0 0.0 copy-start
  0.0 0.0 copy-start.9
  0.0 0.0 copy-start.2
  0.0 4.4 %all-to-all-start.1 = ((f32[8,128,512]{2,1,0:T(8,128)}), f32[8,128,512]{2,1,0:T(8,128)S(1)}, u32[]{:S(2)}, u32[]{:S(2)}) async-start(f32[8,128,512]{2,1,0:T(8,128)} %bitcast.18), calls=%async_computation.1 | async-start | bytes 4194304 | tf_op jit(solution)/shard_map/all_to_all | solution.py:318
  4.4 0.0 copy-done.9
  4.4 0.5 fusion.4.low_lat
  4.9 0.7 dynamic-slice_bitcast_fusion.damp
  5.6 0.1 fusion.3.rows
  5.7 0.0 copy-done.2
  5.7 53.5 %scatter.1 = f32[8,136,512]{2,1,0:T(8,128)} custom-call(s32[16384]{0:T(1024)S(1)} %fusion.3.rows, f32[1,16384]{1,0:T(1,128)S(1)} %fusion.4.low_lat, f32[8,16384]{1,0:T(8,128)S(1)} %bitcast.17, f32[8,128]{1,0:T(8,128)S(1)} %dynamic-slice_bitcast_fusion.damp), custom_call_target="tpu_custom_call" | custom-call | tf_op jit(solution)/shard_map/scatter/pallas_call | solution.py:193
  59.2 0.0 copy-start.5
  59.2 0.0 copy-start.7
  59.2 0.0 all-to-all-done.1.tangent
  59.3 4.7 %all-to-all-start = ((f32[8,136,512]{2,1,0:T(8,128)}), f32[8,136,512]{2,1,0:T(8,128)}, u32[]{:S(2)}, u32[]{:S(2)}) async-start(f32[8,136,512]{2,1,0:T(8,128)} %scatter.1), calls=%async_computation | async-start | bytes 4456448 | tf_op jit(solution)/shard_map/all_to_all | solution.py:318
  63.9 0.0 copy-done.5
  63.9 0.0 copy-done.6
  64.0 0.0 copy-done.7
  64.0 0.0 copy-done.8
  64.0 0.0 copy-start.3
  64.0 0.0 copy-start.4
  64.0 8.2 %legendre.1.table = bf16[128,256,128]{2,1,0:T(8,128)(2,1)S(1)} custom-call(f32[128,128]{1,0:T(8,128)S(1)} %copy-done.7, f32[128,128]{1,0:T(8,128)S(1)} %copy-done.6, f32[128,128]{1,0:T(8,128)S(1)} %copy-done.5, f32[1,128]{1,0:T(1,128)S(1)} %copy-done.8), custom_call_target="tpu_custom_call" | custom-call | tf_op jit(solution)/shard_map/legendre/pallas_call | solution.py:115
  72.2 0.0 copy-start.1
  72.2 3.2 %copy-done.1 = bf16[128,256,128]{2,1,0:T(8,128)(2,1)} copy-done((bf16[128,256,128]{2,1,0:T(8,128)(2,1)}, bf16[128,256,128]{2,1,0:T(8,128)(2,1)S(1)}, u32[]{:S(2)}) %copy-start.1) | copy-done | bytes 8388632
  75.4 0.7 constant_dynamic-slice_fusion.spread
  76.1 15.0 %all-to-all-done.forcing = f32[8,136,512]{2,1,0:T(8,128)} async-done(((f32[8,136,512]{2,1,0:T(8,128)}), f32[8,136,512]{2,1,0:T(8,128)}, u32[]{:S(2)}, u32[]{:S(2)}) %all-to-all-start) | async-done | bytes 2228256 | tf_op jit(solution)/shard_map/all_to_all | solution.py:318
  91.1 0.0 copy-done.3
  91.1 0.0 copy-done.4
  91.1 73.4 %sweep.1 = f32[4,128,128]{2,1,0:T(8,128)S(1)} custom-call(f32[8,136,512]{2,1,0:T(8,128)} %all-to-all-done.forcing, f32[8,128,512]{2,1,0:T(8,128)S(1)} %all-to-all-done.1.tangent, f32[2,128]{1,0:T(2,128)S(1)} %constant_dynamic-slice_fusion.spread, bf16[256,512]{1,0:T(8,128)(2,1)S(1)} %copy-done.4, bf16[256,512]{1,0:T(8,128)(2,1)S(1)} %copy-done.3, ...), custom_call_target="tpu_custom_call" | custom-call | tf_op jit(solution)/shard_map/sweep/pallas_call | solution.py:290
  164.5 16.0 %all_to_all.15 = f32[32,16,128]{2,1,0:T(8,128)S(1)} all-to-all(f32[32,16,128]{2,1,0:T(8,128)S(1)} %bitcast.16), channel_id=1, replica_groups=mesh['tm'=4,'lev'=8] {'tm','lev'}, dimensions={0} | all-to-all | bytes 524288 | tf_op jit(solution)/shard_map/all_to_all | solution.py:331
  180.5 0.8 reshape.11
  181.3 0.0 copy-done
  181.3 3.0 %convolution_bitcast_fusion = f32[64,16,2,32]{0,3,2,1:T(8,128)} fusion(f32[4,8,16,2,2,32]{5,4,3,2,1,0:T(2,128)S(1)} %reshape.11, f32[8,4,2,64,1,1]{3,2,1,0,5,4:T(2,128)S(1)} %bitcast.15), kind=kOutput, calls=%fused_computation | convolution fusion | flops 50331648 | bytes 540672 | tf_op jit(solution)/shard_map/gukl,ugmkpn->lmpn/dot_general | solution.py:334
  (2 shorter events, 0.0 us)
Async XLA Ops:
  0.0 181.3 %copy-start = (f32[64,64]{1,0:T(8,128)S(1)}, f32[64,64]{1,0:T(8,128)}, u32[]{:S(2)}) copy-start(f32[64,64]{1,0:T(8,128)} %param.17) | copy-start | bytes 49156
  0.0 4.4 %copy-start.9 = (s32[1,16384]{1,0:T(1,128)S(1)}, s32[1,16384]{1,0:T(1,128)}, u32[]{:S(2)}) copy-start(s32[1,16384]{1,0:T(1,128)} %param.12) | copy-start | bytes 196612
  0.0 5.7 %copy-start.2 = (f32[1,8,16384]{2,1,0:T(8,128)S(1)}, f32[1,8,16384]{2,1,0:T(8,128)}, u32[]{:S(2)}) copy-start(f32[1,8,16384]{2,1,0:T(8,128)} %param.13) | copy-start | bytes 1572868
  0.0 59.2 %all-to-all-start.1 = ((f32[8,128,512]{2,1,0:T(8,128)}), f32[8,128,512]{2,1,0:T(8,128)S(1)}, u32[]{:S(2)}, u32[]{:S(2)}) async-start(f32[8,128,512]{2,1,0:T(8,128)} %bitcast.18), calls=%async_computation.1 | async-start | bytes 4194304 | tf_op jit(solution)/shard_map/all_to_all | solution.py:318
  59.2 4.7 %copy-start.5 = (f32[128,128]{1,0:T(8,128)S(1)}, f32[128,128]{1,0:T(8,128)}, u32[]{:S(2)}) copy-start(f32[128,128]{1,0:T(8,128)} %constant.90.clone.diagonal) | copy-start | bytes 196612
  59.2 4.7 %copy-start.6 = (f32[128,128]{1,0:T(8,128)S(1)}, f32[128,128]{1,0:T(8,128)}, u32[]{:S(2)}) copy-start(f32[128,128]{1,0:T(8,128)} %constant.89.clone.downward) | copy-start | bytes 196612
  59.2 4.7 %copy-start.7 = (f32[128,128]{1,0:T(8,128)S(1)}, f32[128,128]{1,0:T(8,128)}, u32[]{:S(2)}) copy-start(f32[128,128]{1,0:T(8,128)} %constant.88.clone.upward) | copy-start | bytes 196612
  59.2 4.7 %copy-start.8 = (f32[1,128]{1,0:T(1,128)S(1)}, f32[1,128]{1,0:T(1,128)}, u32[]{:S(2)}) copy-start(f32[1,128]{1,0:T(1,128)} %constant.91.clone.sine) | copy-start | bytes 1540
  59.3 31.8 %all-to-all-start = ((f32[8,136,512]{2,1,0:T(8,128)}), f32[8,136,512]{2,1,0:T(8,128)}, u32[]{:S(2)}, u32[]{:S(2)}) async-start(f32[8,136,512]{2,1,0:T(8,128)} %scatter.1), calls=%async_computation | async-start | bytes 4456448 | tf_op jit(solution)/shard_map/all_to_all | solution.py:318
  64.0 27.1 %copy-start.3 = (bf16[256,512]{1,0:T(8,128)(2,1)S(1)}, bf16[256,512]{1,0:T(8,128)(2,1)}, u32[]{:S(2)}) copy-start(bf16[256,512]{1,0:T(8,128)(2,1)} %constant.93.clone.fourier_low) | copy-start | bytes 786436
  64.0 27.1 %copy-start.4 = (bf16[256,512]{1,0:T(8,128)(2,1)S(1)}, bf16[256,512]{1,0:T(8,128)(2,1)}, u32[]{:S(2)}) copy-start(bf16[256,512]{1,0:T(8,128)(2,1)} %constant.92.clone.fourier_high) | copy-start | bytes 786436
  72.2 3.2 %copy-start.1 = (bf16[128,256,128]{2,1,0:T(8,128)(2,1)}, bf16[128,256,128]{2,1,0:T(8,128)(2,1)S(1)}, u32[]{:S(2)}) copy-start(bf16[128,256,128]{2,1,0:T(8,128)(2,1)S(1)} %legendre.1.table) | copy-start | bytes 25165828

commit v2 on v1

--- a/solution.py
+++ b/solution.py
@@ -14,6 +14,7 @@
 SUBLANES = 8
 ACCUMULATORS = 8
 OBS_BLOCK = 128
+SPREAD_BLOCK = 1024
 WAVE_UNROLL = 16
 DEGREE_UNROLL = 16
 
@@ -74,7 +75,9 @@
     )
 
 
-def legendre_kernel(upward, downward, diagonal, sine, table, up_now, down_now, values):
+def legendre_kernel(
+    upward, downward, diagonal, sine, analysis, synthesis, up_now, down_now, values
+):
     waves, lats = diagonal.shape
     pitch = values.shape[0] // waves
     up_now[...] = upward[...]
@@ -102,21 +105,23 @@
 
     def emit(wave, carry):
         rows = values[pl.ds(wave, waves, stride=pitch), :]
-        high, low = split_parts(rows)
-        table[wave, 0:waves, :] = high
-        table[wave, waves : 2 * waves, :] = low
+        analysis[wave] = jnp.concatenate(split_parts(rows.T), axis=1)
+        synthesis[wave] = jnp.concatenate(split_parts(rows), axis=1)
         return carry
 
-    lax.fori_loop(0, waves, emit, 0)
-
-
-def legendre_table(lat_count, wave_count):
+    lax.fori_loop(0, waves, emit, 0, unroll=4)
+
+
+def legendre_tables(lat_count, wave_count):
     pitch = wave_count + SUBLANES
     return pl.pallas_call(
         legendre_kernel,
-        out_shape=jax.ShapeDtypeStruct((wave_count, 2 * wave_count, lat_count), jnp.bfloat16),
+        out_shape=[
+            jax.ShapeDtypeStruct((wave_count, lat_count, 2 * wave_count), jnp.bfloat16),
+            jax.ShapeDtypeStruct((wave_count, wave_count, 2 * lat_count), jnp.bfloat16),
+        ],
         in_specs=[vmem()] * 4,
-        out_specs=vmem(),
+        out_specs=[vmem()] * 2,
         scratch_shapes=[
             pltpu.VMEM((wave_count, wave_count), jnp.float32),
             pltpu.VMEM((wave_count, wave_count), jnp.float32),
@@ -135,27 +140,32 @@
     waves = damp.shape[1]
     for part in sums:
         part[...] = jnp.zeros(part.shape, jnp.float32)
-    lane = lax.broadcasted_iota(jnp.int32, (levels, LANES), 1)
-    level = lax.broadcasted_iota(jnp.int32, (levels, LANES), 0)
-    place = (lane // span == level).astype(jnp.float32)
-    one_row = jnp.ones((1, LANES), jnp.float32)
-    lane_low = (lax.broadcasted_iota(jnp.int32, (OBS_BLOCK, LANES), 1) % span).astype(jnp.float32)
+    row = lax.broadcasted_iota(jnp.int32, (4 * SUBLANES, 2 * LANES), 0)
+    lane = lax.broadcasted_iota(jnp.int32, (4 * SUBLANES, 2 * LANES), 1)
+    values_here = (row < 3 * SUBLANES) & (lane < LANES) & (row % SUBLANES == lane // span)
+    place = (values_here | ((row == 3 * SUBLANES) & (lane >= LANES))).astype(jnp.bfloat16)
+    lane_low = (lax.broadcasted_iota(jnp.int32, (SPREAD_BLOCK, LANES), 1) % span).astype(jnp.float32)
 
     def spread_out(block, carry):
-        start = pl.multiple_of(block * OBS_BLOCK, OBS_BLOCK)
-        values = innov[:, pl.ds(start, OBS_BLOCK)]
-        expanded = lax.dot_general(
-            values,
-            place,
-            (((0,), (0,)), ((), ())),
-            precision=PRECISE,
-            preferred_element_type=jnp.float32,
+        start = pl.multiple_of(block * SPREAD_BLOCK, SPREAD_BLOCK)
+        rest = innov[:, pl.ds(start, SPREAD_BLOCK)]
+        if levels < SUBLANES:
+            fill = jnp.zeros((SUBLANES - levels, SPREAD_BLOCK), jnp.float32)
+            rest = jnp.concatenate([rest, fill], axis=0)
+        parts = []
+        for _ in range(3):
+            parts.append(rest.astype(jnp.bfloat16).astype(jnp.float32))
+            rest = rest - parts[-1]
+        low = low_lat[:, pl.ds(start, SPREAD_BLOCK)]
+        parts.append(jnp.broadcast_to(low, (SUBLANES, SPREAD_BLOCK)))
+        stacked = jnp.concatenate(parts, axis=0).astype(jnp.bfloat16)
+        placed = dot(stacked, place, 0, 0)
+        data[pl.ds(start, SPREAD_BLOCK), :] = jnp.where(
+            placed[:, LANES:] == lane_low, placed[:, :LANES], 0.0
         )
-        low = dot(low_lat[:, pl.ds(start, OBS_BLOCK)], one_row, 0, 0)
-        data[pl.ds(start, OBS_BLOCK), :] = jnp.where(low == lane_low, expanded, 0.0)
         return carry
 
-    lax.fori_loop(0, obs // OBS_BLOCK, spread_out, 0)
+    lax.fori_loop(0, obs // SPREAD_BLOCK, spread_out, 0)
 
     def scatter(block, carry):
         start = pl.multiple_of(block * OBS_BLOCK, OBS_BLOCK)
@@ -202,9 +212,21 @@
     )(rows, low_lat, innov, damp)
 
 
-def sweep_kernel(forcing, tangent, spread, fourier_high, fourier_low, table, out, forced, work, total):
-    waves = table.shape[0]
-    lats = table.shape[2]
+def sweep_kernel(
+    forcing,
+    tangent,
+    spread,
+    fourier_high,
+    fourier_low,
+    analysis,
+    synthesis,
+    out,
+    forced,
+    work,
+    filtered,
+    total,
+):
+    waves, lats = analysis.shape[:2]
     times = out.shape[0]
     degree_block = waves // times
     kept = forcing.shape[0] // times
@@ -242,25 +264,32 @@
             damp_rows += [damp_row, damp_row]
         damp = jnp.concatenate(damp_rows * copies, axis=0)
 
-        def per_wave(group, carry):
+        def analyse(group, carry):
             for step in range(WAVE_UNROLL):
                 wave = group * WAVE_UNROLL + step
                 at = pl.ds(pl.multiple_of(wave * rows, rows), rows)
-                both = table[wave]
-                product = dot(work[at, :].astype(jnp.bfloat16), both, 1, 1)
+                product = dot(work[at, :].astype(jnp.bfloat16), analysis[wave], 1, 0)
                 product = product[:, 0:waves] + product[:, waves:]
                 spectral = product + pltpu.roll(product, half, 0)
                 total[at, :] = total[at, :] + spectral
                 if time > 0:
-                    filtered = spectral * damp
-                    part = filtered.astype(jnp.bfloat16).astype(jnp.float32)
-                    part = jnp.where(is_high, part, filtered - part).astype(jnp.bfloat16)
-                    result = dot(jnp.concatenate([part, part], axis=1), both, 1, 0)
-                    work[at, :] = result + pltpu.roll(result, half, 0)
+                    damped = spectral * damp
+                    part = damped.astype(jnp.bfloat16).astype(jnp.float32)
+                    filtered[at, :] = jnp.where(is_high, part, damped - part)
             return carry
 
-        lax.fori_loop(0, waves // WAVE_UNROLL, per_wave, 0)
+        def synthesise(group, carry):
+            for step in range(WAVE_UNROLL):
+                wave = group * WAVE_UNROLL + step
+                at = pl.ds(pl.multiple_of(wave * rows, rows), rows)
+                result = dot(filtered[at, :].astype(jnp.bfloat16), synthesis[wave], 1, 0)
+                result = result[:, 0:lats] + result[:, lats:]
+                work[at, :] = result + pltpu.roll(result, half, 0)
+            return carry
+
+        lax.fori_loop(0, waves // WAVE_UNROLL, analyse, 0)
         if time > 0:
+            lax.fori_loop(0, waves // WAVE_UNROLL, synthesise, 0)
             for k in range(kept):
                 parts = [work[pl.ds(2 * k + p, waves, stride=rows), :].T for p in range(2)]
                 synth_high, synth_low = split_parts(jnp.concatenate(parts, axis=1))
@@ -281,25 +310,26 @@
         out[block] = jnp.concatenate([piece[:, cols] for piece in scaled], axis=1)
 
 
-def sweep(forcing, tangent, spread, table, times):
+def sweep(forcing, tangent, spread, tables, times):
     kept = spread.shape[0]
     lats, lons = tangent.shape[1:]
-    waves = table.shape[0]
+    waves = tables[0].shape[0]
     rows = max(SUBLANES, 4 * kept)
     high, low = fourier_rows(lons, waves)
     return pl.pallas_call(
         sweep_kernel,
         out_shape=jax.ShapeDtypeStruct((times, waves, 2 * kept * waves // times), jnp.float32),
-        in_specs=[vmem()] * 6,
+        in_specs=[vmem()] * 7,
         out_specs=vmem(),
         scratch_shapes=[
             pltpu.VMEM((kept * lats, lons), jnp.float32),
             pltpu.VMEM((waves * rows, lats), jnp.float32),
             pltpu.VMEM((waves * rows, waves), jnp.float32),
+            pltpu.VMEM((waves * rows, waves), jnp.float32),
         ],
         compiler_params=pltpu.CompilerParams(vmem_limit_bytes=50 * 2**20),
         name="sweep",
-    )(forcing, tangent, spread, high, low, table)
+    )(forcing, tangent, spread, high, low, *tables)
 
 
 def shards(obs_cell, innovation, tangent, damping, spread, vertical):
@@ -321,9 +351,9 @@
     damp_here = lax.dynamic_slice_in_dim(damping[0], my_group * lev_dev, lev_dev, 0)
     forcing = forcing_field(obs_cell[0], innovation[0], damp_here, lat_rows, lon_cols)
     forcing_mine = exchange(forcing)
-    table = legendre_table(lat_rows, wave_count)
+    tables = legendre_tables(lat_rows, wave_count)
     spread_mine = lax.dynamic_slice_in_dim(spread, my_first, kept, 0)
-    blocks = sweep(forcing_mine, tangent_mine, spread_mine, table, sections)
+    blocks = sweep(forcing_mine, tangent_mine, spread_mine, tables, sections)
 
     block_waves = wave_count // groups
     block_degrees = wave_count // sections

time: 185 us -> 106 us (0.57)
  Pallas kernels: 135 us -> 60.7 us
  waiting for transfers between devices: 15 us -> 10.7 us
    pallas_call x1, Pallas kernels: 73.4 us -> 24 us  [sweep(): pl.pallas_call(sweep_kernel, out_shape=jax.ShapeDtypeStruct((times, waves...]
    pallas_call x1, Pallas kernels: 53.5 us -> 23.8 us  [forcing_field(): pl.pallas_call(scatter_kernel, out_shape=jax.ShapeDtypeStruct((levels, la...]
    pallas_call x1, Pallas kernels: 8.2 us -> 12.9 us  [legendre_tables(): pl.pallas_call(legendre_kernel, out_shape=[jax.ShapeDtypeStruct((wave_cou...]
    all_to_all x2, waiting for transfers between devices: 15 us -> 10.7 us  [exchange(): return lax.all_to_all(field, 'tm', split_axis=0, concat_axis=0, tiled=True)]
  transfers between devices with their start and end apart: 2 -> 2, of which waited for: 1 -> 2; matrix products, arithmetic and copies ran while one was open for 1% -> 2% of each run, Pallas kernels for 33% -> 35%
where the time goes in v2:
time: 106 us; the launch traced here: 105 us
  Pallas kernels  60.7 us (57%)
  blocking collectives  15.9 us (15%)
  waiting for transfers between devices  10.7 us (10%)
  starting transfers between devices  8.89 us (8%)
  local copies, waits for them, and re-layouts  5.5 us (5%)
  matrix products  2.96 us (3%)
    pallas_call x1, Pallas kernels, sweep(): pl.pallas_call(sweep_kernel, out_shape=jax.ShapeDtypeStruct((times, waves...  24 us
    pallas_call x1, Pallas kernels, forcing_field(): pl.pallas_call(scatter_kernel, out_shape=jax.ShapeDtypeStruct((levels, la...  23.8 us
    all_to_all x1, blocking collectives, shards(): lax.all_to_all(blocks, ('tm', 'lev'), split_axis=0, concat_axis=0, tiled=...  15.9 us
    pallas_call x1, Pallas kernels, legendre_tables(): pl.pallas_call(legendre_kernel, out_shape=[jax.ShapeDtypeStruct((wave_cou...  12.9 us
    all_to_all x2, waiting for transfers between devices, exchange(): return lax.all_to_all(field, 'tm', split_axis=0, concat_axis=0, tiled=True)  10.7 us
    all_to_all x2, starting transfers between devices, exchange(): return lax.all_to_all(field, 'tm', split_axis=0, concat_axis=0, tiled=True)  8.89 us
    unnamed x20, local copies, waits for them, and re-layouts  3.28 us
    dot_general x1, matrix products, shards(): return jnp.einsum('gukl,ugmkpn->lmpn', mixing, owned, precision=PRECISE)  2.96 us
  transfers between devices with their start and end apart: 2, of which 2 were waited for; matrix products, arithmetic and copies ran while one was open for 2% of the time, Pallas kernels for 35%

profile of v2, /device:TPU:0, one launch (start us, length us, event | category | flops | bytes accessed | tf_op | source)
XLA Modules:
  0.0 105.4 jit_solution(7541739869429365057)
XLA Ops:
  0.0 0.0 copy-start
  0.0 0.0 copy-start.9
  0.0 0.0 copy-start.2
  0.0 4.4 %all-to-all-start.1 = ((f32[8,128,512]{2,1,0:T(8,128)}), f32[8,128,512]{2,1,0:T(8,128)S(1)}, u32[]{:S(2)}, u32[]{:S(2)}) async-start(f32[8,128,512]{2,1,0:T(8,128)} %bitcast.18), calls=%async_computation.1 | async-start | bytes 4194304 | tf_op jit(solution)/shard_map/all_to_all | solution.py:348
  4.4 0.0 copy-done.9
  4.4 0.5 fusion.4.low_lat
  4.9 0.7 dynamic-slice_bitcast_fusion.damp
  5.6 0.1 fusion.3.rows
  5.7 0.0 copy-done.2
  5.7 23.8 %scatter.1 = f32[8,136,512]{2,1,0:T(8,128)} custom-call(s32[16384]{0:T(1024)S(1)} %fusion.3.rows, f32[1,16384]{1,0:T(1,128)S(1)} %fusion.4.low_lat, f32[8,16384]{1,0:T(8,128)S(1)} %bitcast.17, f32[8,128]{1,0:T(8,128)S(1)} %dynamic-slice_bitcast_fusion.damp), custom_call_target="tpu_custom_call" | custom-call | tf_op jit(solution)/shard_map/scatter/pallas_call | solution.py:203
  29.6 0.0 copy-start.5
  29.6 0.0 copy-start.6
  29.6 0.0 copy-start.7
  29.6 0.0 copy-start.3
  29.6 0.0 copy-start.4
  29.6 0.5 all-to-all-done.1.tangent
  30.1 4.5 %all-to-all-start = ((f32[8,136,512]{2,1,0:T(8,128)}), f32[8,136,512]{2,1,0:T(8,128)}, u32[]{:S(2)}, u32[]{:S(2)}) async-start(f32[8,136,512]{2,1,0:T(8,128)} %scatter.1), calls=%async_computation | async-start | bytes 4456448 | tf_op jit(solution)/shard_map/all_to_all | solution.py:348
  34.6 0.0 copy-done.5
  34.6 0.0 copy-done.6
  34.6 0.0 copy-done.7
  34.6 0.0 copy-done.8
  34.6 12.9 %legendre.1 = (bf16[128,128,256]{2,1,0:T(8,128)(2,1)S(1)}, bf16[128,128,256]{2,1,0:T(8,128)(2,1)}) custom-call(f32[128,128]{1,0:T(8,128)S(1)} %copy-done.7, f32[128,128]{1,0:T(8,128)S(1)} %copy-done.6, f32[128,128]{1,0:T(8,128)S(1)} %copy-done.5, f32[1,128]{1,0:T(1,128)S(1)} %copy-done.8), custom_call_target="tpu_custom_call" | custom-call | tf_op jit(solution)/shard_map/legendre/pallas_call | solution.py:117
  47.5 3.2 %copy-done.1 = bf16[128,128,256]{2,1,0:T(8,128)(2,1)} copy-done((bf16[128,128,256]{2,1,0:T(8,128)(2,1)}, bf16[128,128,256]{2,1,0:T(8,128)(2,1)S(1)}, u32[]{:S(2)}) %copy-start.1) | copy-done | bytes 8388632
  50.8 0.7 constant_dynamic-slice_fusion.spread
  51.5 10.2 %all-to-all-done.forcing = f32[8,136,512]{2,1,0:T(8,128)} async-done(((f32[8,136,512]{2,1,0:T(8,128)}), f32[8,136,512]{2,1,0:T(8,128)}, u32[]{:S(2)}, u32[]{:S(2)}) %all-to-all-start) | async-done | bytes 2228256 | tf_op jit(solution)/shard_map/all_to_all | solution.py:348
  61.7 0.0 copy-done.3
  61.7 0.0 copy-done.4
  61.7 24.0 %sweep.1 = f32[4,128,128]{2,1,0:T(8,128)S(1)} custom-call(f32[8,136,512]{2,1,0:T(8,128)} %all-to-all-done.forcing, f32[8,128,512]{2,1,0:T(8,128)S(1)} %all-to-all-done.1.tangent, f32[2,128]{1,0:T(2,128)S(1)} %constant_dynamic-slice_fusion.spread, bf16[256,512]{1,0:T(8,128)(2,1)S(1)} %copy-done.4, bf16[256,512]{1,0:T(8,128)(2,1)S(1)} %copy-done.3, ...), custom_call_target="tpu_custom_call" | custom-call | tf_op jit(solution)/shard_map/sweep/pallas_call | solution.py:319
  85.7 15.9 %all_to_all.15 = f32[32,16,128]{2,1,0:T(8,128)S(1)} all-to-all(f32[32,16,128]{2,1,0:T(8,128)S(1)} %bitcast.16), channel_id=1, replica_groups=mesh['tm'=4,'lev'=8] {'tm','lev'}, dimensions={0} | all-to-all | bytes 524288 | tf_op jit(solution)/shard_map/all_to_all | solution.py:361
  101.6 0.8 reshape.11
  102.5 0.0 copy-done
  102.5 3.0 %convolution_bitcast_fusion = f32[64,16,2,32]{0,3,2,1:T(8,128)} fusion(f32[4,8,16,2,2,32]{5,4,3,2,1,0:T(2,128)S(1)} %reshape.11, f32[8,4,2,64,1,1]{3,2,1,0,5,4:T(2,128)S(1)} %bitcast.15), kind=kOutput, calls=%fused_computation | convolution fusion | flops 50331648 | bytes 540672 | tf_op jit(solution)/shard_map/gukl,ugmkpn->lmpn/dot_general | solution.py:364
  (2 shorter events, 0.0 us)
Async XLA Ops:
  0.0 102.5 %copy-start = (f32[64,64]{1,0:T(8,128)S(1)}, f32[64,64]{1,0:T(8,128)}, u32[]{:S(2)}) copy-start(f32[64,64]{1,0:T(8,128)} %param.17) | copy-start | bytes 49156
  0.0 4.4 %copy-start.9 = (s32[1,16384]{1,0:T(1,128)S(1)}, s32[1,16384]{1,0:T(1,128)}, u32[]{:S(2)}) copy-start(s32[1,16384]{1,0:T(1,128)} %param.12) | copy-start | bytes 196612
  0.0 5.7 %copy-start.2 = (f32[1,8,16384]{2,1,0:T(8,128)S(1)}, f32[1,8,16384]{2,1,0:T(8,128)}, u32[]{:S(2)}) copy-start(f32[1,8,16384]{2,1,0:T(8,128)} %param.13) | copy-start | bytes 1572868
  0.0 30.1 %all-to-all-start.1 = ((f32[8,128,512]{2,1,0:T(8,128)}), f32[8,128,512]{2,1,0:T(8,128)S(1)}, u32[]{:S(2)}, u32[]{:S(2)}) async-start(f32[8,128,512]{2,1,0:T(8,128)} %bitcast.18), calls=%async_computation.1 | async-start | bytes 4194304 | tf_op jit(solution)/shard_map/all_to_all | solution.py:348
  29.6 5.0 %copy-start.5 = (f32[128,128]{1,0:T(8,128)S(1)}, f32[128,128]{1,0:T(8,128)}, u32[]{:S(2)}) copy-start(f32[128,128]{1,0:T(8,128)} %constant.90.clone.diagonal) | copy-start | bytes 196612
  29.6 5.0 %copy-start.6 = (f32[128,128]{1,0:T(8,128)S(1)}, f32[128,128]{1,0:T(8,128)}, u32[]{:S(2)}) copy-start(f32[128,128]{1,0:T(8,128)} %constant.89.clone.downward) | copy-start | bytes 196612
  29.6 5.1 %copy-start.7 = (f32[128,128]{1,0:T(8,128)S(1)}, f32[128,128]{1,0:T(8,128)}, u32[]{:S(2)}) copy-start(f32[128,128]{1,0:T(8,128)} %constant.88.clone.upward) | copy-start | bytes 196612
  29.6 5.1 %copy-start.8 = (f32[1,128]{1,0:T(1,128)S(1)}, f32[1,128]{1,0:T(1,128)}, u32[]{:S(2)}) copy-start(f32[1,128]{1,0:T(1,128)} %constant.91.clone.sine) | copy-start | bytes 1540
  29.6 32.2 %copy-start.3 = (bf16[256,512]{1,0:T(8,128)(2,1)S(1)}, bf16[256,512]{1,0:T(8,128)(2,1)}, u32[]{:S(2)}) copy-start(bf16[256,512]{1,0:T(8,128)(2,1)} %constant.93.clone.fourier_low) | copy-start | bytes 786436
  29.6 32.1 %copy-start.4 = (bf16[256,512]{1,0:T(8,128)(2,1)S(1)}, bf16[256,512]{1,0:T(8,128)(2,1)}, u32[]{:S(2)}) copy-start(bf16[256,512]{1,0:T(8,128)(2,1)} %constant.92.clone.fourier_high) | copy-start | bytes 786436
  30.1 31.6 %all-to-all-start = ((f32[8,136,512]{2,1,0:T(8,128)}), f32[8,136,512]{2,1,0:T(8,128)}, u32[]{:S(2)}, u32[]{:S(2)}) async-start(f32[8,136,512]{2,1,0:T(8,128)} %scatter.1), calls=%async_computation | async-start | bytes 4456448 | tf_op jit(solution)/shard_map/all_to_all | solution.py:348
  47.5 3.2 %copy-start.1 = (bf16[128,128,256]{2,1,0:T(8,128)(2,1)}, bf16[128,128,256]{2,1,0:T(8,128)(2,1)S(1)}, u32[]{:S(2)}) copy-start(bf16[128,128,256]{2,1,0:T(8,128)(2,1)S(1)} %get-tuple-element.7.analysis) | copy-start | bytes 25165828

commit v3 on v2

--- a/solution.py
+++ b/solution.py
@@ -1,3 +1,4 @@
+import functools
 import math
 
 import numpy as np
@@ -9,14 +10,15 @@
 from jax.experimental.pallas import tpu as pltpu
 from jax.sharding import PartitionSpec as P
 
+
 PRECISE = lax.Precision.HIGHEST
 LANES = 128
 SUBLANES = 8
 ACCUMULATORS = 8
-OBS_BLOCK = 128
-SPREAD_BLOCK = 1024
+OBS_BLOCK = 512
 WAVE_UNROLL = 16
 DEGREE_UNROLL = 16
+SWEEP_MIB = 20
 
 
 def vmem():
@@ -25,6 +27,10 @@
 
 def smem():
     return pl.BlockSpec(memory_space=pltpu.SMEM)
+
+
+def in_hbm(*arrays):
+    return [pltpu.with_memory_space_constraint(array, pltpu.HBM) for array in arrays]
 
 
 def fourier_rows(lon_count, wave_count):
@@ -59,8 +65,8 @@
     downward = np.sqrt(
         np.maximum(lower**2 - orders**2, 0.0) / np.maximum(4.0 * lower**2 - 1.0, 1.0)
     )
-    cast = lambda table: table.astype(np.float32)
-    return cast(upward), cast(upward * downward), cast(diagonal), cast(sine)
+    sine = np.broadcast_to(sine, (SUBLANES, lat_count))
+    return np.concatenate([upward, upward * downward, diagonal, sine]).astype(np.float32)
 
 
 def split_parts(values):
@@ -75,15 +81,13 @@
     )
 
 
-def legendre_kernel(
-    upward, downward, diagonal, sine, analysis, synthesis, up_now, down_now, values
-):
-    waves, lats = diagonal.shape
+def legendre_kernel(seeds, analysis, synthesis, up_now, down_now, values):
+    waves, lats = analysis.shape[:2]
     pitch = values.shape[0] // waves
-    up_now[...] = upward[...]
-    down_now[...] = downward[...]
+    up_now[...] = seeds[0:waves, :]
+    down_now[...] = seeds[waves : 2 * waves, :]
     order = lax.broadcasted_iota(jnp.int32, (waves, lats), 0)
-    sine_rows = jnp.broadcast_to(sine[...], (waves, lats))
+    sine_rows = jnp.broadcast_to(seeds[3 * waves : 3 * waves + 1, :], (waves, lats))
 
     def advance(group, state):
         one, two = state
@@ -91,7 +95,7 @@
         down = down_now[...]
         for step in range(DEGREE_UNROLL):
             degree = group * DEGREE_UNROLL + step
-            seed = jnp.where(order == degree, diagonal[...], 0.0)
+            seed = jnp.where(order == degree, seeds[2 * waves : 3 * waves, :], 0.0)
             current = (up[:, step : step + 1] * sine_rows) * one
             current = current - down[:, step : step + 1] * two + seed
             values[pl.ds(pl.multiple_of(degree * pitch, SUBLANES), waves), :] = current
@@ -120,62 +124,69 @@
             jax.ShapeDtypeStruct((wave_count, lat_count, 2 * wave_count), jnp.bfloat16),
             jax.ShapeDtypeStruct((wave_count, wave_count, 2 * lat_count), jnp.bfloat16),
         ],
-        in_specs=[vmem()] * 4,
+        in_specs=[vmem()],
         out_specs=[vmem()] * 2,
         scratch_shapes=[
             pltpu.VMEM((wave_count, wave_count), jnp.float32),
             pltpu.VMEM((wave_count, wave_count), jnp.float32),
             pltpu.VMEM((wave_count * pitch, lat_count), jnp.float32),
         ],
-        compiler_params=pltpu.CompilerParams(vmem_limit_bytes=40 * 2**20),
+        compiler_params=pltpu.CompilerParams(vmem_limit_bytes=12 * 2**20),
         name="legendre",
-    )(*legendre_seeds(lat_count, wave_count))
-
-
-def scatter_kernel(rows, low_lat, innov, damp, field, data, *sums):
+    )(*in_hbm(legendre_seeds(lat_count, wave_count)))
+
+
+def scatter_kernel(rows, cells, innov, damping, *refs, sections):
     levels, obs = innov.shape
+    waves = damping.shape[1]
+    outs = refs[:sections]
+    field, even, odd, sems = refs[sections : sections + 4]
+    sums = refs[sections + 4 :]
     lats = field.shape[1] - SUBLANES
     lons = field.shape[2]
     span = LANES // levels
-    waves = damp.shape[1]
     for part in sums:
         part[...] = jnp.zeros(part.shape, jnp.float32)
     row = lax.broadcasted_iota(jnp.int32, (4 * SUBLANES, 2 * LANES), 0)
     lane = lax.broadcasted_iota(jnp.int32, (4 * SUBLANES, 2 * LANES), 1)
     values_here = (row < 3 * SUBLANES) & (lane < LANES) & (row % SUBLANES == lane // span)
     place = (values_here | ((row == 3 * SUBLANES) & (lane >= LANES))).astype(jnp.bfloat16)
-    lane_low = (lax.broadcasted_iota(jnp.int32, (SPREAD_BLOCK, LANES), 1) % span).astype(jnp.float32)
-
-    def spread_out(block, carry):
-        start = pl.multiple_of(block * SPREAD_BLOCK, SPREAD_BLOCK)
-        rest = innov[:, pl.ds(start, SPREAD_BLOCK)]
+    lane_low = (lax.broadcasted_iota(jnp.int32, (OBS_BLOCK, LANES), 1) % span).astype(jnp.float32)
+
+    def spread_out(block, data):
+        start = pl.multiple_of(block * OBS_BLOCK, OBS_BLOCK)
+        rest = innov[:, pl.ds(start, OBS_BLOCK)]
         if levels < SUBLANES:
-            fill = jnp.zeros((SUBLANES - levels, SPREAD_BLOCK), jnp.float32)
+            fill = jnp.zeros((SUBLANES - levels, OBS_BLOCK), jnp.float32)
             rest = jnp.concatenate([rest, fill], axis=0)
         parts = []
         for _ in range(3):
             parts.append(rest.astype(jnp.bfloat16).astype(jnp.float32))
             rest = rest - parts[-1]
-        low = low_lat[:, pl.ds(start, SPREAD_BLOCK)]
-        parts.append(jnp.broadcast_to(low, (SUBLANES, SPREAD_BLOCK)))
+        low = (cells[:, pl.ds(start, OBS_BLOCK)] // lons % span).astype(jnp.float32)
+        parts.append(jnp.broadcast_to(low, (SUBLANES, OBS_BLOCK)))
         stacked = jnp.concatenate(parts, axis=0).astype(jnp.bfloat16)
         placed = dot(stacked, place, 0, 0)
-        data[pl.ds(start, SPREAD_BLOCK), :] = jnp.where(
-            placed[:, LANES:] == lane_low, placed[:, :LANES], 0.0
-        )
-        return carry
-
-    lax.fori_loop(0, obs // SPREAD_BLOCK, spread_out, 0)
-
-    def scatter(block, carry):
+        data[...] = jnp.where(placed[:, LANES:] == lane_low, placed[:, :LANES], 0.0)
+
+    def add_rows(block, data):
         start = pl.multiple_of(block * OBS_BLOCK, OBS_BLOCK)
         for step in range(OBS_BLOCK):
             part = sums[step % ACCUMULATORS]
-            row = rows[start + step]
-            part[pl.ds(row, 1), :] = part[pl.ds(row, 1), :] + data[pl.ds(start + step, 1), :]
+            at = pl.ds(rows[start + step], 1)
+            part[at, :] = part[at, :] + data[step : step + 1, :]
+
+    blocks = obs // OBS_BLOCK
+    spread_out(0, even)
+
+    def two_blocks(pair, carry):
+        spread_out(2 * pair + 1, odd)
+        add_rows(2 * pair, even)
+        spread_out(jnp.minimum(2 * pair + 2, blocks - 1), even)
+        add_rows(2 * pair + 1, odd)
         return carry
 
-    lax.fori_loop(0, obs // OBS_BLOCK, scatter, 0)
+    lax.fori_loop(0, blocks // 2, two_blocks, 0)
 
     for high in range(lats // span):
         for west in range(lons // LANES):
@@ -189,61 +200,106 @@
                     turned[k * span : (k + 1) * span, :]
                 )
     field[:, lats:, :] = jnp.zeros((levels, SUBLANES, lons), jnp.float32)
+    first = lax.axis_index("lev") * levels
     for k in range(levels):
-        field[k, lats : lats + 1, 0:waves] = damp[k : k + 1, :]
-
-
-def forcing_field(cells, innov, damp, lats, lons):
-    levels, obs = innov.shape
+        field[k, lats : lats + 1, 0:waves] = damping[pl.ds(first + k, 1), :]
+    me = lax.axis_index("tm")
+    chunk = max(1, levels // sections)
+    repeat = max(1, sections // levels)
+    copies = [
+        pltpu.make_async_copy(
+            field.at[pl.ds(((me ^ slot) // repeat) * chunk, chunk)], outs[slot], sems.at[slot]
+        )
+        for slot in range(sections)
+    ]
+    for copy in copies:
+        copy.start()
+    for copy in copies:
+        copy.wait()
+
+
+def cut_kernel(field, *refs, sections):
+    outs, sems = refs[:sections], refs[sections]
+    levels = field.shape[0]
+    me = lax.axis_index("tm")
+    chunk = max(1, levels // sections)
+    repeat = max(1, sections // levels)
+    copies = [
+        pltpu.make_async_copy(
+            field.at[pl.ds(((me ^ slot) // repeat) * chunk, chunk)], outs[slot], sems.at[slot]
+        )
+        for slot in range(sections)
+    ]
+    for copy in copies:
+        copy.start()
+    for copy in copies:
+        copy.wait()
+
+
+def cut_chunks(field, sections):
+    levels, lats, lons = field.shape
+    chunk = max(1, levels // sections)
+    return pl.pallas_call(
+        functools.partial(cut_kernel, sections=sections),
+        out_shape=[jax.ShapeDtypeStruct((chunk, lats, lons), jnp.float32)] * sections,
+        in_specs=[pl.BlockSpec(memory_space=pl.ANY)],
+        out_specs=[vmem()] * sections,
+        scratch_shapes=[pltpu.SemaphoreType.DMA((sections,))],
+        compiler_params=pltpu.CompilerParams(vmem_limit_bytes=4 * 2**20),
+        name="cut",
+    )(field)
+
+
+def forcing_chunks(cells, innov, damping, lats, lons, sections):
+    levels, _ = innov.shape
     span = LANES // levels
-    lat = cells // lons
-    rows = (lat // span) * lons + cells % lons
-    low_lat = (lat % span).astype(jnp.float32)[None, :]
-    sum_rows = lats * lons // span
+    rows = (cells // (lons * span)) * lons + cells % lons
+    chunk = max(1, levels // sections)
     return pl.pallas_call(
-        scatter_kernel,
-        out_shape=jax.ShapeDtypeStruct((levels, lats + SUBLANES, lons), jnp.float32),
+        functools.partial(scatter_kernel, sections=sections),
+        out_shape=[jax.ShapeDtypeStruct((chunk, lats + SUBLANES, lons), jnp.float32)] * sections,
         in_specs=[smem(), vmem(), vmem(), vmem()],
-        out_specs=vmem(),
-        scratch_shapes=[pltpu.VMEM((obs, LANES), jnp.float32)]
-        + [pltpu.VMEM((sum_rows, LANES), jnp.float32)] * ACCUMULATORS,
-        compiler_params=pltpu.CompilerParams(vmem_limit_bytes=50 * 2**20),
+        out_specs=[pl.BlockSpec(memory_space=pl.ANY)] * sections,
+        scratch_shapes=[
+            pltpu.VMEM((levels, lats + SUBLANES, lons), jnp.float32),
+            pltpu.VMEM((OBS_BLOCK, LANES), jnp.float32),
+            pltpu.VMEM((OBS_BLOCK, LANES), jnp.float32),
+            pltpu.SemaphoreType.DMA((sections,)),
+        ]
+        + [pltpu.VMEM((lats * lons // span, LANES), jnp.float32)] * ACCUMULATORS,
+        compiler_params=pltpu.CompilerParams(vmem_limit_bytes=32 * 2**20),
         name="scatter",
-    )(rows, low_lat, innov, damp)
-
-
-def sweep_kernel(
-    forcing,
-    tangent,
-    spread,
-    fourier_high,
-    fourier_low,
-    analysis,
-    synthesis,
-    out,
-    forced,
-    work,
-    filtered,
-    total,
-):
+    )(rows, *in_hbm(cells[None, :], innov, damping))
+
+
+def sweep_kernel(spread, fourier, analysis, synthesis, *refs, sections):
+    chunks, tangents = refs[:sections], refs[sections : 2 * sections]
+    out, forced, work, filtered, total, damp_now = refs[2 * sections :]
+    fourier_high, fourier_low = fourier.at[0], fourier.at[1]
     waves, lats = analysis.shape[:2]
-    times = out.shape[0]
+    times = sections
     degree_block = waves // times
-    kept = forcing.shape[0] // times
+    kept = chunks[0].shape[0]
+    levels = spread.shape[0] // lax.axis_size("lev")
     half = 2 * kept
     rows = max(SUBLANES, 2 * half)
     copies = rows // half
     row = lax.broadcasted_iota(jnp.int32, (rows, waves), 0)
     is_high = (row // half) % 2 == 0
     total[...] = jnp.zeros(total.shape, jnp.float32)
+    forced[...] = jnp.zeros(forced.shape, jnp.float32)
+    me = lax.axis_index("tm")
 
     for time in range(times - 1, -1, -1):
-        for k in range(kept):
-            here = slice(k * lats, (k + 1) * lats)
-            if time == times - 1:
-                forced[here, :] = forcing[time * kept + k, 0:lats, :]
-            else:
-                forced[here, :] = forced[here, :] + forcing[time * kept + k, 0:lats, :]
+        for slot in range(sections):
+
+            @pl.when(me ^ slot == time)
+            def _(chunk=chunks[slot]):
+                for k in range(kept):
+                    here = slice(k * lats, (k + 1) * lats)
+                    forced[here, :] = forced[here, :] + chunk[k, 0:lats, :]
+                    damp_now[k : k + 1, :] = chunk[k, lats : lats + 1, 0:waves]
+
         high, low = split_parts(forced[...])
         coeffs = dot(fourier_high[...], high, 1, 1)
         coeffs = coeffs + dot(fourier_low[...], high, 1, 1)
@@ -260,7 +316,7 @@
                     )
         damp_rows = []
         for k in range(kept):
-            damp_row = forcing[time * kept + k, lats : lats + 1, 0:waves]
+            damp_row = damp_now[k : k + 1, :]
             damp_rows += [damp_row, damp_row]
         damp = jnp.concatenate(damp_rows * copies, axis=0)
 
@@ -289,6 +345,14 @@
 
         lax.fori_loop(0, waves // WAVE_UNROLL, analyse, 0)
         if time > 0:
+            for slot in range(sections):
+
+                @pl.when(me ^ slot == time)
+                def _(factor=tangents[slot]):
+                    for k in range(kept):
+                        here = slice(k * lats, (k + 1) * lats)
+                        forced[here, :] = factor[k] * forced[here, :]
+
             lax.fori_loop(0, waves // WAVE_UNROLL, synthesise, 0)
             for k in range(kept):
                 parts = [work[pl.ds(2 * k + p, waves, stride=rows), :].T for p in range(2)]
@@ -297,63 +361,66 @@
                 gridded = gridded + dot(synth_high, fourier_low[...], 1, 0)
                 gridded = gridded + dot(synth_low, fourier_high[...], 1, 0)
                 here = slice(k * lats, (k + 1) * lats)
-                forced[here, :] = tangent[time * kept + k] * forced[here, :] + gridded
+                forced[here, :] = forced[here, :] + gridded
 
     scaled = []
+    repeat = max(1, sections // levels)
+    first = lax.axis_index("lev") * levels + (me // repeat) * kept
     for k in range(kept):
+        factor = spread[pl.ds(first + k, 1), :]
         for p in range(2):
-            scaled.append(
-                total[pl.ds(2 * k + p, waves, stride=rows), :] * spread[k : k + 1, :]
-            )
+            scaled.append(total[pl.ds(2 * k + p, waves, stride=rows), :] * factor)
     for block in range(times):
         cols = slice(block * degree_block, (block + 1) * degree_block)
         out[block] = jnp.concatenate([piece[:, cols] for piece in scaled], axis=1)
 
 
-def sweep(forcing, tangent, spread, tables, times):
-    kept = spread.shape[0]
-    lats, lons = tangent.shape[1:]
+def sweep(chunks, tangents, spread, tables):
+    sections = len(chunks)
+    kept = chunks[0].shape[0]
+    lats, lons = tangents[0].shape[1:]
     waves = tables[0].shape[0]
     rows = max(SUBLANES, 4 * kept)
-    high, low = fourier_rows(lons, waves)
+    fourier = np.stack(fourier_rows(lons, waves))
     return pl.pallas_call(
-        sweep_kernel,
-        out_shape=jax.ShapeDtypeStruct((times, waves, 2 * kept * waves // times), jnp.float32),
-        in_specs=[vmem()] * 7,
+        functools.partial(sweep_kernel, sections=sections),
+        out_shape=jax.ShapeDtypeStruct(
+            (sections, waves, 2 * kept * waves // sections), jnp.float32
+        ),
+        in_specs=[vmem()] * (4 + 2 * sections),
         out_specs=vmem(),
         scratch_shapes=[
             pltpu.VMEM((kept * lats, lons), jnp.float32),
             pltpu.VMEM((waves * rows, lats), jnp.float32),
             pltpu.VMEM((waves * rows, waves), jnp.float32),
             pltpu.VMEM((waves * rows, waves), jnp.float32),
+            pltpu.VMEM((SUBLANES, waves), jnp.float32),
         ],
-        compiler_params=pltpu.CompilerParams(vmem_limit_bytes=50 * 2**20),
+        compiler_params=pltpu.CompilerParams(vmem_limit_bytes=SWEEP_MIB * 2**20),
         name="sweep",
-    )(forcing, tangent, spread, high, low, *tables)
+    )(*in_hbm(spread, fourier), *tables, *chunks, *tangents)
 
 
 def shards(obs_cell, innovation, tangent, damping, spread, vertical):
     sections = lax.axis_size("tm")
     groups = lax.axis_size("lev")
-    my_section = lax.axis_index("tm")
-    my_group = lax.axis_index("lev")
     lev_dev, lat_rows, lon_cols = tangent.shape[1:]
     wave_count = damping.shape[2]
     repeat = max(1, sections // lev_dev)
     kept = max(1, lev_dev // sections)
-    my_first = my_group * lev_dev + (my_section // repeat) * kept
-
-    def exchange(field):
-        field = jnp.repeat(field, repeat, axis=0) if repeat > 1 else field
-        return lax.all_to_all(field, "tm", split_axis=0, concat_axis=0, tiled=True)
-
-    tangent_mine = exchange(tangent[0])
-    damp_here = lax.dynamic_slice_in_dim(damping[0], my_group * lev_dev, lev_dev, 0)
-    forcing = forcing_field(obs_cell[0], innovation[0], damp_here, lat_rows, lon_cols)
-    forcing_mine = exchange(forcing)
+
+    def exchange(chunks):
+        return [
+            lax.ppermute(chunk, "tm", [(i, i ^ slot) for i in range(sections)]) if slot else chunk
+            for slot, chunk in enumerate(chunks)
+        ]
+
+    cut = cut_chunks(*in_hbm(tangent[0]), sections)
+    tangents = exchange(cut)
+    chunks = forcing_chunks(obs_cell[0], innovation[0], damping[0], lat_rows, lon_cols, sections)
+    chunks = exchange(chunks)
     tables = legendre_tables(lat_rows, wave_count)
-    spread_mine = lax.dynamic_slice_in_dim(spread, my_first, kept, 0)
-    blocks = sweep(forcing_mine, tangent_mine, spread_mine, tables, sections)
+    blocks = sweep(chunks, tangents, spread, tables)
 
     block_waves = wave_count // groups
     block_degrees = wave_count // sections

time: 106 us -> 110 us (1.038)
  waiting for transfers between devices: 10.7 us -> 34.2 us
  Pallas kernels: 60.7 us -> 49.3 us
  local copies, waits for them, and re-layouts: 5.5 us -> 0.84 us
  starting transfers between devices: 8.89 us -> 5.38 us
    ppermute x0 -> x6, waiting for transfers between devices: none -> 34.2 us  [exchange(): lax.ppermute(chunk, 'tm', [(i, i ^ slot) for i in range(sections)])]
    all_to_all x2 -> x0, waiting for transfers between devices: 10.7 us -> none  [exchange(): return lax.all_to_all(field, 'tm', split_axis=0, concat_axis=0, tiled=True)]
    pallas_call x2 -> x3, Pallas kernels: 47.8 us -> 38.5 us  [the longest x1 19.2 us: sweep(): pl.pallas_call(functools.partial(sweep_kernel, sections=sections), out_sh...]
    all_to_all x2 -> x0, starting transfers between devices: 8.89 us -> none  [exchange(): return lax.all_to_all(field, 'tm', split_axis=0, concat_axis=0, tiled=True)]
    ppermute x0 -> x6, starting transfers between devices: none -> 5.38 us  [exchange(): lax.ppermute(chunk, 'tm', [(i, i ^ slot) for i in range(sections)])]
    unnamed x20 -> x2, local copies, waits for them, and re-layouts: 3.28 us -> 0.01 us
    pallas_call x1, Pallas kernels: 12.9 us -> 10.7 us  [legendre_tables(): pl.pallas_call(legendre_kernel, out_shape=[jax.ShapeDtypeStruct((wave_cou...]
    dynamic_slice x2 -> x0, local copies, waits for them, and re-layouts: 1.38 us -> none  [the longest x1 0.69 us: shards(): lax.dynamic_slice_in_dim(damping[0], my_group * lev_dev, lev_dev, 0)]
  transfers between devices with their start and end apart: 2 -> 6, of which waited for: 2 -> 2; matrix products, arithmetic and copies ran while one was open for 2% -> 1% of each run, Pallas kernels for 35% -> 26%
where the time goes in v3:
time: 110 us
  Pallas kernels  49.3 us (45%)
  waiting for transfers between devices  34.2 us (31%)
  blocking collectives  16.3 us (15%)
  starting transfers between devices  5.38 us (5%)
  matrix products  2.96 us (3%)
    ppermute x6, waiting for transfers between devices, exchange(): lax.ppermute(chunk, 'tm', [(i, i ^ slot) for i in range(sections)])  34.2 us
    pallas_call x1, Pallas kernels, sweep(): pl.pallas_call(functools.partial(sweep_kernel, sections=sections), out_sh...  19.2 us
    pallas_call x1, Pallas kernels, forcing_chunks(): pl.pallas_call(functools.partial(scatter_kernel, sections=sections), out_...  17.7 us
    all_to_all x1, blocking collectives, shards(): lax.all_to_all(blocks, ('tm', 'lev'), split_axis=0, concat_axis=0, tiled=...  16.3 us
    pallas_call x1, Pallas kernels, legendre_tables(): pl.pallas_call(legendre_kernel, out_shape=[jax.ShapeDtypeStruct((wave_cou...  10.7 us
    ppermute x6, starting transfers between devices, exchange(): lax.ppermute(chunk, 'tm', [(i, i ^ slot) for i in range(sections)])  5.38 us
    dot_general x1, matrix products, shards(): return jnp.einsum('gukl,ugmkpn->lmpn', mixing, owned, precision=PRECISE)  2.96 us
  transfers between devices with their start and end apart: 6, of which 2 were waited for; matrix products, arithmetic and copies ran while one was open for 1% of the time, Pallas kernels for 26%

profile of v3, /device:TPU:0, one launch (start us, length us, event | category | flops | bytes accessed | tf_op | source)
XLA Modules:
  0.0 109.9 jit_solution(2900970099197497916)
XLA Ops:
  0.0 0.0 copy-start
  0.0 1.6 %cut.1 = (f32[2,128,512]{2,1,0:T(8,128)S(1)}, f32[2,128,512]{2,1,0:T(8,128)S(1)}, f32[2,128,512]{2,1,0:T(8,128)S(1)}, f32[2,128,512]{2,1,0:T(8,128)S(1)}) custom-call(f32[8,128,512]{2,1,0:T(8,128)} %bitcast.16), custom_call_target="tpu_custom_call" | custom-call | tf_op jit(solution)/shard_map/cut/pallas_call | solution.py:242
  1.6 0.6 collective-permute-start.3
  2.1 0.9 fusion.3.rows
  3.0 17.7 %scatter.1 = (f32[2,136,512]{2,1,0:T(8,128)S(1)}, f32[2,136,512]{2,1,0:T(8,128)S(1)}, f32[2,136,512]{2,1,0:T(8,128)S(1)}, f32[2,136,512]{2,1,0:T(8,128)S(1)}) custom-call(s32[16384]{0:T(1024)S(1)} %fusion.3.rows, s32[1,16384]{1,0:T(1,128)} %cells.1, f32[8,16384]{1,0:T(8,128)} %bitcast.17, f32[64,128]{1,0:T(8,128)} %bitcast.19), custom_call_target="tpu_custom_call" | custom-call | tf_op jit(solution)/shard_map/scatter/pallas_call | solution.py:258
  20.8 0.1 collective-permute-start
  20.8 3.0 %collective-permute-start.1 = (f32[2,136,512]{2,1,0:T(8,128)S(1)}, f32[2,136,512]{2,1,0:T(8,128)S(1)}, u32[]{:S(2)}, u32[]{:S(2)}) collective-permute-start(f32[2,136,512]{2,1,0:T(8,128)S(1)} %get-tuple-element.19), channel_id=1, source_target_pairs={{0,16},{8,24},{16,0},{24,8},{1,17},{9,25},{17,1},{25,9},{2,18},{10... | collective-permute-start | bytes 1671176 | tf_op jit(solution)/shard_map/ppermute | solution.py:414
  23.8 0.0 collective-permute-start.2
  23.8 1.4 %collective-permute-start.4 = (f32[2,128,512]{2,1,0:T(8,128)S(1)}, f32[2,128,512]{2,1,0:T(8,128)S(1)}, u32[]{:S(2)}, u32[]{:S(2)}) collective-permute-start(f32[2,128,512]{2,1,0:T(8,128)S(1)} %get-tuple-element.23), channel_id=1, source_target_pairs={{0,16},{8,24},{16,0},{24,8},{1,17},{9,25},{17,1},{25,9},{2,18},{10... | collective-permute-start | bytes 1572872 | tf_op jit(solution)/shard_map/ppermute | solution.py:414
  25.3 0.0 collective-permute-done.3.refs_5_
  25.3 0.3 collective-permute-start.5
  25.6 10.7 %legendre.1 = (bf16[128,128,256]{2,1,0:T(8,128)(2,1)S(1)}, bf16[128,128,256]{2,1,0:T(8,128)(2,1)S(1)}) custom-call(f32[392,128]{1,0:T(8,128)} %constant.35.clone.seeds), custom_call_target="tpu_custom_call" | custom-call | tf_op jit(solution)/shard_map/legendre/pallas_call | solution.py:121
  36.3 24.1 %collective-permute-done.4.refs_6_ = f32[2,128,512]{2,1,0:T(8,128)S(1)} collective-permute-done((f32[2,128,512]{2,1,0:T(8,128)S(1)}, f32[2,128,512]{2,1,0:T(8,128)S(1)}, u32[]{:S(2)}, u32[]{:S(2)}) %collective-permute-start.4) | collective-permute-done | bytes 524320 | tf_op jit(solution)/shard_map/ppermute | solution.py:414
  60.5 10.0 %collective-permute-done.5.refs_7_ = f32[2,128,512]{2,1,0:T(8,128)S(1)} collective-permute-done((f32[2,128,512]{2,1,0:T(8,128)S(1)}, f32[2,128,512]{2,1,0:T(8,128)S(1)}, u32[]{:S(2)}, u32[]{:S(2)}) %collective-permute-start.5) | collective-permute-done | bytes 524320 | tf_op jit(solution)/shard_map/ppermute | solution.py:414
  70.5 0.0 collective-permute-done.refs_1_
  70.5 0.0 collective-permute-done.1.refs_2_
  70.5 0.0 collective-permute-done.2.refs_3_
  70.5 19.2 %sweep.1 = f32[4,128,128]{2,1,0:T(8,128)S(1)} custom-call(f32[64,128]{1,0:T(8,128)} %spread.1, bf16[2,256,512]{2,1,0:T(8,128)(2,1)} %constant.36.clone.fourier, bf16[128,128,256]{2,1,0:T(8,128)(2,1)S(1)} %get-tuple-element.15.analysis, bf16[128,128,256]{2,1,0:T(8,128)(2,1)S(1)} %get-tuple-element.16.synthesis, f32[2,136,512]{2,1,0:T(8,128)S(1)} %get-tuple-element.17.refs_0_, ...), custom_call_target="tpu_custom_call" | custom-call | tf_op jit(solution)/shard_map/sweep/pallas_call | solution.py:385
  89.8 16.3 %all_to_all.5 = f32[32,16,128]{2,1,0:T(8,128)S(1)} all-to-all(f32[32,16,128]{2,1,0:T(8,128)S(1)} %bitcast.15), channel_id=1, replica_groups=mesh['tm'=4,'lev'=8] {'tm','lev'}, dimensions={0} | all-to-all | bytes 524288 | tf_op jit(solution)/shard_map/all_to_all | solution.py:428
  106.1 0.8 reshape.10
  107.0 0.0 copy-done
  107.0 3.0 %convolution_bitcast_fusion = f32[64,16,2,32]{0,3,2,1:T(8,128)} fusion(f32[4,8,16,2,2,32]{5,4,3,2,1,0:T(2,128)S(1)} %reshape.10, f32[8,4,2,64,1,1]{3,2,1,0,5,4:T(2,128)S(1)} %bitcast.14), kind=kOutput, calls=%fused_computation | convolution fusion | flops 50331648 | bytes 540672 | tf_op jit(solution)/shard_map/gukl,ugmkpn->lmpn/dot_general | solution.py:431
Async XLA Ops:
  0.0 107.0 %copy-start = (f32[64,64]{1,0:T(8,128)S(1)}, f32[64,64]{1,0:T(8,128)}, u32[]{:S(2)}) copy-start(f32[64,64]{1,0:T(8,128)} %param.13) | copy-start | bytes 49156
  1.6 23.7 %collective-permute-start.3 = (f32[2,128,512]{2,1,0:T(8,128)S(1)}, f32[2,128,512]{2,1,0:T(8,128)S(1)}, u32[]{:S(2)}, u32[]{:S(2)}) collective-permute-start(f32[2,128,512]{2,1,0:T(8,128)S(1)} %get-tuple-element.22), channel_id=1, source_target_pairs={{0,8},{8,0},{16,24},{24,16},{1,9},{9,1},{17,25},{25,17},{2,10},{10... | collective-permute-start | bytes 1572872 | tf_op jit(solution)/shard_map/ppermute | solution.py:414
  20.8 49.7 %collective-permute-start = (f32[2,136,512]{2,1,0:T(8,128)S(1)}, f32[2,136,512]{2,1,0:T(8,128)S(1)}, u32[]{:S(2)}, u32[]{:S(2)}) collective-permute-start(f32[2,136,512]{2,1,0:T(8,128)S(1)} %get-tuple-element.18), channel_id=1, source_target_pairs={{0,8},{8,0},{16,24},{24,16},{1,9},{9,1},{17,25},{25,17},{2,10},{10... | collective-permute-start | bytes 1671176 | tf_op jit(solution)/shard_map/ppermute | solution.py:414
  20.8 49.7 %collective-permute-start.1 = (f32[2,136,512]{2,1,0:T(8,128)S(1)}, f32[2,136,512]{2,1,0:T(8,128)S(1)}, u32[]{:S(2)}, u32[]{:S(2)}) collective-permute-start(f32[2,136,512]{2,1,0:T(8,128)S(1)} %get-tuple-element.19), channel_id=1, source_target_pairs={{0,16},{8,24},{16,0},{24,8},{1,17},{9,25},{17,1},{25,9},{2,18},{10... | collective-permute-start | bytes 1671176 | tf_op jit(solution)/shard_map/ppermute | solution.py:414
  23.8 46.7 %collective-permute-start.2 = (f32[2,136,512]{2,1,0:T(8,128)S(1)}, f32[2,136,512]{2,1,0:T(8,128)S(1)}, u32[]{:S(2)}, u32[]{:S(2)}) collective-permute-start(f32[2,136,512]{2,1,0:T(8,128)S(1)} %get-tuple-element.20), channel_id=1, source_target_pairs={{0,24},{8,16},{16,8},{24,0},{1,25},{9,17},{17,9},{25,1},{2,26},{10... | collective-permute-start | bytes 1671176 | tf_op jit(solution)/shard_map/ppermute | solution.py:414
  23.8 36.6 %collective-permute-start.4 = (f32[2,128,512]{2,1,0:T(8,128)S(1)}, f32[2,128,512]{2,1,0:T(8,128)S(1)}, u32[]{:S(2)}, u32[]{:S(2)}) collective-permute-start(f32[2,128,512]{2,1,0:T(8,128)S(1)} %get-tuple-element.23), channel_id=1, source_target_pairs={{0,16},{8,24},{16,0},{24,8},{1,17},{9,25},{17,1},{25,9},{2,18},{10... | collective-permute-start | bytes 1572872 | tf_op jit(solution)/shard_map/ppermute | solution.py:414
  25.3 45.2 %collective-permute-start.5 = (f32[2,128,512]{2,1,0:T(8,128)S(1)}, f32[2,128,512]{2,1,0:T(8,128)S(1)}, u32[]{:S(2)}, u32[]{:S(2)}) collective-permute-start(f32[2,128,512]{2,1,0:T(8,128)S(1)} %get-tuple-element.24), channel_id=1, source_target_pairs={{0,24},{8,16},{16,8},{24,0},{1,25},{9,17},{17,9},{25,1},{2,26},{10... | collective-permute-start | bytes 1572872 | tf_op jit(solution)/shard_map/ppermute | solution.py:414

commit v4 on v3

--- a/solution.py
+++ b/solution.py
@@ -11,13 +11,12 @@
 from jax.sharding import PartitionSpec as P
 
 
-PRECISE = lax.Precision.HIGHEST
 LANES = 128
 SUBLANES = 8
 ACCUMULATORS = 8
 OBS_BLOCK = 512
 WAVE_UNROLL = 16
-DEGREE_UNROLL = 16
+DEGREE_BLOCK = 16
 SWEEP_MIB = 20
 
 
@@ -81,70 +80,97 @@
     )
 
 
-def legendre_kernel(seeds, analysis, synthesis, up_now, down_now, values):
+def legendre_kernel(
+    seeds, fourier, spread, analysis, synthesis, fourier_near, spread_near, values, sems
+):
     waves, lats = analysis.shape[:2]
     pitch = values.shape[0] // waves
-    up_now[...] = seeds[0:waves, :]
-    down_now[...] = seeds[waves : 2 * waves, :]
-    order = lax.broadcasted_iota(jnp.int32, (waves, lats), 0)
-    sine_rows = jnp.broadcast_to(seeds[3 * waves : 3 * waves + 1, :], (waves, lats))
-
-    def advance(group, state):
-        one, two = state
-        up = up_now[...]
-        down = down_now[...]
-        for step in range(DEGREE_UNROLL):
-            degree = group * DEGREE_UNROLL + step
-            seed = jnp.where(order == degree, seeds[2 * waves : 3 * waves, :], 0.0)
-            current = (up[:, step : step + 1] * sine_rows) * one
-            current = current - down[:, step : step + 1] * two + seed
-            values[pl.ds(pl.multiple_of(degree * pitch, SUBLANES), waves), :] = current
-            one, two = current, one
-        up_now[...] = pltpu.roll(up, waves - DEGREE_UNROLL, 1)
-        down_now[...] = pltpu.roll(down, waves - DEGREE_UNROLL, 1)
-        return one, two
-
-    zeros = jnp.zeros((waves, lats), jnp.float32)
-    lax.fori_loop(0, waves // DEGREE_UNROLL, advance, (zeros, zeros))
-
-    def emit(wave, carry):
-        rows = values[pl.ds(wave, waves, stride=pitch), :]
-        analysis[wave] = jnp.concatenate(split_parts(rows.T), axis=1)
-        synthesis[wave] = jnp.concatenate(split_parts(rows), axis=1)
-        return carry
-
-    lax.fori_loop(0, waves, emit, 0, unroll=4)
-
-
-def legendre_tables(lat_count, wave_count):
+    nearer = [
+        pltpu.make_async_copy(fourier, fourier_near, sems.at[0]),
+        pltpu.make_async_copy(spread, spread_near, sems.at[1]),
+    ]
+    for copy in nearer:
+        copy.start()
+    sine = seeds[3 * waves : 3 * waves + 1, :]
+    one = jnp.zeros((0, lats), jnp.float32)
+    two = one
+    for degree in range(waves):
+        live = (degree // DEGREE_BLOCK + 1) * DEGREE_BLOCK
+        if one.shape[0] < live:
+            fresh = jnp.zeros((live - one.shape[0], lats), jnp.float32)
+            one = jnp.concatenate([one, fresh], axis=0) if one.shape[0] else fresh
+            two = jnp.concatenate([two, fresh], axis=0) if two.shape[0] else fresh
+        order = lax.broadcasted_iota(jnp.int32, (DEGREE_BLOCK, lats), 0) + (live - DEGREE_BLOCK)
+        edge = slice(2 * waves + live - DEGREE_BLOCK, 2 * waves + live)
+        seed = jnp.where(order == degree, seeds[edge, :], 0.0)
+        if live > DEGREE_BLOCK:
+            seed = jnp.concatenate(
+                [jnp.zeros((live - DEGREE_BLOCK, lats), jnp.float32), seed], axis=0
+            )
+        up = seeds[0:live, degree : degree + 1]
+        down = seeds[waves : waves + live, degree : degree + 1]
+        current = (up * sine) * one - down * two + seed
+        values[degree * pitch : degree * pitch + live, :] = current
+        one, two = current, one
+
+    row = lax.broadcasted_iota(jnp.int32, (lats, lats), 0)
+    identity = (row == lax.broadcasted_iota(jnp.int32, (lats, lats), 1)).astype(jnp.bfloat16)
+    for group in range(waves // DEGREE_BLOCK):
+        skipped = group * DEGREE_BLOCK
+
+        def emit(quad, carry):
+            for step in range(4):
+                wave = skipped + 4 * quad + step
+                start = skipped * pitch + wave
+                rows = values[pl.ds(start, waves - skipped, stride=pitch), :]
+                if skipped:
+                    rows = jnp.concatenate(
+                        [jnp.zeros((skipped, lats), jnp.float32), rows], axis=0
+                    )
+                high, low = split_parts(rows)
+                synthesis[wave] = jnp.concatenate([high, low], axis=1)
+                if step % 2:
+                    both = jnp.concatenate([high, low], axis=0)
+                    analysis[wave] = dot(identity, both, 1, 1).astype(jnp.bfloat16)
+                else:
+                    analysis[wave] = jnp.concatenate(split_parts(rows.T), axis=1)
+            return carry
+
+        lax.fori_loop(0, DEGREE_BLOCK // 4, emit, 0)
+    for copy in nearer:
+        copy.wait()
+
+
+def legendre_tables(lat_count, lon_count, wave_count, spread):
     pitch = wave_count + SUBLANES
+    fourier = np.stack(fourier_rows(lon_count, wave_count))
+    anywhere = pl.BlockSpec(memory_space=pl.ANY)
     return pl.pallas_call(
         legendre_kernel,
         out_shape=[
             jax.ShapeDtypeStruct((wave_count, lat_count, 2 * wave_count), jnp.bfloat16),
             jax.ShapeDtypeStruct((wave_count, wave_count, 2 * lat_count), jnp.bfloat16),
+            jax.ShapeDtypeStruct(fourier.shape, jnp.bfloat16),
+            jax.ShapeDtypeStruct(spread.shape, jnp.float32),
         ],
-        in_specs=[vmem()],
-        out_specs=[vmem()] * 2,
+        in_specs=[vmem(), anywhere, anywhere],
+        out_specs=[vmem()] * 4,
         scratch_shapes=[
-            pltpu.VMEM((wave_count, wave_count), jnp.float32),
-            pltpu.VMEM((wave_count, wave_count), jnp.float32),
             pltpu.VMEM((wave_count * pitch, lat_count), jnp.float32),
+            pltpu.SemaphoreType.DMA((2,)),
         ],
-        compiler_params=pltpu.CompilerParams(vmem_limit_bytes=12 * 2**20),
+        compiler_params=pltpu.CompilerParams(vmem_limit_bytes=14 * 2**20),
         name="legendre",
-    )(*in_hbm(legendre_seeds(lat_count, wave_count)))
-
-
-def scatter_kernel(rows, cells, innov, damping, *refs, sections):
+    )(*in_hbm(legendre_seeds(lat_count, wave_count), fourier, spread))
+
+
+def scatter_kernel(rows, cells, innov, damping, *refs, sections, lats, lons):
     levels, obs = innov.shape
-    waves = damping.shape[1]
     outs = refs[:sections]
     field, even, odd, sems = refs[sections : sections + 4]
     sums = refs[sections + 4 :]
-    lats = field.shape[1] - SUBLANES
-    lons = field.shape[2]
     span = LANES // levels
+    chunk = max(1, levels // sections)
     for part in sums:
         part[...] = jnp.zeros(part.shape, jnp.float32)
     row = lax.broadcasted_iota(jnp.int32, (4 * SUBLANES, 2 * LANES), 0)
@@ -188,6 +214,7 @@
 
     lax.fori_loop(0, blocks // 2, two_blocks, 0)
 
+    first = lax.axis_index("lev") * levels
     for high in range(lats // span):
         for west in range(lons // LANES):
             block = pl.ds(high * lons + west * LANES, LANES)
@@ -196,20 +223,18 @@
                 total = total + part[block, :]
             turned = total.T
             for k in range(levels):
-                field[k, high * span : (high + 1) * span, west * LANES : (west + 1) * LANES] = (
-                    turned[k * span : (k + 1) * span, :]
-                )
-    field[:, lats:, :] = jnp.zeros((levels, SUBLANES, lons), jnp.float32)
-    first = lax.axis_index("lev") * levels
-    for k in range(levels):
-        field[k, lats : lats + 1, 0:waves] = damping[pl.ds(first + k, 1), :]
+                at = ((k % chunk) * (lons // LANES) + west) * lats + high * span
+                field[k // chunk, at : at + span, :] = turned[k * span : (k + 1) * span, :]
+    tail = chunk * lats * lons // LANES
+    for piece in range(levels // chunk):
+        field[piece, tail:, :] = jnp.zeros((SUBLANES, LANES), jnp.float32)
+        for k in range(chunk):
+            rates = damping[pl.ds(first + piece * chunk + k, 1), :]
+            field[piece, tail + k : tail + k + 1, :] = rates
     me = lax.axis_index("tm")
-    chunk = max(1, levels // sections)
     repeat = max(1, sections // levels)
     copies = [
-        pltpu.make_async_copy(
-            field.at[pl.ds(((me ^ slot) // repeat) * chunk, chunk)], outs[slot], sems.at[slot]
-        )
+        pltpu.make_async_copy(field.at[(me ^ slot) // repeat], outs[slot], sems.at[slot])
         for slot in range(sections)
     ]
     for copy in copies:
@@ -255,13 +280,14 @@
     span = LANES // levels
     rows = (cells // (lons * span)) * lons + cells % lons
     chunk = max(1, levels // sections)
+    size = chunk * lats * lons // LANES + SUBLANES
     return pl.pallas_call(
-        functools.partial(scatter_kernel, sections=sections),
-        out_shape=[jax.ShapeDtypeStruct((chunk, lats + SUBLANES, lons), jnp.float32)] * sections,
+        functools.partial(scatter_kernel, sections=sections, lats=lats, lons=lons),
+        out_shape=[jax.ShapeDtypeStruct((size, LANES), jnp.float32)] * sections,
         in_specs=[smem(), vmem(), vmem(), vmem()],
         out_specs=[pl.BlockSpec(memory_space=pl.ANY)] * sections,
         scratch_shapes=[
-            pltpu.VMEM((levels, lats + SUBLANES, lons), jnp.float32),
+            pltpu.VMEM((levels // chunk, size, LANES), jnp.float32),
             pltpu.VMEM((OBS_BLOCK, LANES), jnp.float32),
             pltpu.VMEM((OBS_BLOCK, LANES), jnp.float32),
             pltpu.SemaphoreType.DMA((sections,)),
@@ -272,14 +298,15 @@
     )(rows, *in_hbm(cells[None, :], innov, damping))
 
 
-def sweep_kernel(spread, fourier, analysis, synthesis, *refs, sections):
+def sweep_kernel(analysis, synthesis, fourier, spread, *refs, sections):
     chunks, tangents = refs[:sections], refs[sections : 2 * sections]
     out, forced, work, filtered, total, damp_now = refs[2 * sections :]
     fourier_high, fourier_low = fourier.at[0], fourier.at[1]
     waves, lats = analysis.shape[:2]
     times = sections
     degree_block = waves // times
-    kept = chunks[0].shape[0]
+    kept = tangents[0].shape[0]
+    lons = tangents[0].shape[2]
     levels = spread.shape[0] // lax.axis_size("lev")
     half = 2 * kept
     rows = max(SUBLANES, 2 * half)
@@ -297,8 +324,12 @@
             def _(chunk=chunks[slot]):
                 for k in range(kept):
                     here = slice(k * lats, (k + 1) * lats)
-                    forced[here, :] = forced[here, :] + chunk[k, 0:lats, :]
-                    damp_now[k : k + 1, :] = chunk[k, lats : lats + 1, 0:waves]
+                    for west in range(lons // LANES):
+                        there = slice(west * LANES, (west + 1) * LANES)
+                        at = (k * (lons // LANES) + west) * lats
+                        forced[here, there] = forced[here, there] + chunk[at : at + lats, :]
+                    tail = kept * lats * lons // LANES + k
+                    damp_now[k : k + 1, :] = chunk[tail : tail + 1, :]
 
         high, low = split_parts(forced[...])
         coeffs = dot(fourier_high[...], high, 1, 1)
@@ -375,13 +406,11 @@
         out[block] = jnp.concatenate([piece[:, cols] for piece in scaled], axis=1)
 
 
-def sweep(chunks, tangents, spread, tables):
+def sweep(chunks, tangents, tables):
     sections = len(chunks)
-    kept = chunks[0].shape[0]
-    lats, lons = tangents[0].shape[1:]
+    kept, lats, lons = tangents[0].shape
     waves = tables[0].shape[0]
     rows = max(SUBLANES, 4 * kept)
-    fourier = np.stack(fourier_rows(lons, waves))
     return pl.pallas_call(
         functools.partial(sweep_kernel, sections=sections),
         out_shape=jax.ShapeDtypeStruct(
@@ -398,7 +427,50 @@
         ],
         compiler_params=pltpu.CompilerParams(vmem_limit_bytes=SWEEP_MIB * 2**20),
         name="sweep",
-    )(*in_hbm(spread, fourier), *tables, *chunks, *tangents)
+    )(*tables, *chunks, *tangents)
+
+
+def mix_kernel(owned, vertical, out, *, sections, groups, repeat):
+    peers = sections * groups
+    block_waves = owned.shape[0] // peers
+    lanes = owned.shape[1]
+    steps = sections // repeat
+    levels = vertical.shape[0] // groups
+    kept = levels // steps
+    each = lanes // kept
+    columns = []
+    for wave in range(block_waves):
+        pieces = [
+            owned[pl.ds(step * repeat * groups * block_waves + wave, groups, stride=block_waves), :]
+            for step in range(steps)
+        ]
+        columns.append(jnp.concatenate(pieces, axis=0))
+    high, low = split_parts(jnp.concatenate(columns, axis=1))
+    left = jnp.concatenate([high, low, high], axis=0)
+    for k in range(kept):
+        pieces = [
+            vertical[pl.ds(step * kept + k, groups, stride=levels), :] for step in range(steps)
+        ]
+        mix_high, mix_low = split_parts(jnp.concatenate(pieces, axis=0))
+        product = dot(left, jnp.concatenate([mix_high, mix_high, mix_low], axis=0), 0, 0)
+        for wave in range(block_waves):
+            start = wave * lanes + k * each
+            piece = product[start : start + each, :]
+            out[wave] = piece if k == 0 else out[wave] + piece
+
+
+def mix(owned, vertical, sections, groups, repeat):
+    peers, block_waves, lanes = owned.shape
+    steps = sections // repeat
+    each = lanes // (vertical.shape[0] // groups // steps)
+    return pl.pallas_call(
+        functools.partial(mix_kernel, sections=sections, groups=groups, repeat=repeat),
+        out_shape=jax.ShapeDtypeStruct((block_waves, each, vertical.shape[1]), jnp.float32),
+        in_specs=[vmem()] * 2,
+        out_specs=vmem(),
+        compiler_params=pltpu.CompilerParams(vmem_limit_bytes=16 * 2**20),
+        name="mix",
+    )(owned.reshape(peers * block_waves, lanes), vertical)
 
 
 def shards(obs_cell, innovation, tangent, damping, spread, vertical):
@@ -419,16 +491,16 @@
     tangents = exchange(cut)
     chunks = forcing_chunks(obs_cell[0], innovation[0], damping[0], lat_rows, lon_cols, sections)
     chunks = exchange(chunks)
-    tables = legendre_tables(lat_rows, wave_count)
-    blocks = sweep(chunks, tangents, spread, tables)
+    tables = legendre_tables(lat_rows, lon_cols, wave_count, spread)
+    blocks = sweep(chunks, tangents, tables)
 
     block_waves = wave_count // groups
     block_degrees = wave_count // sections
     blocks = blocks.reshape(sections * groups, block_waves, 2 * kept * block_degrees)
     owned = lax.all_to_all(blocks, ("tm", "lev"), split_axis=0, concat_axis=0, tiled=True)
-    owned = owned.reshape(sections, groups, block_waves, kept, 2, block_degrees)[::repeat]
-    mixing = vertical.reshape(groups, sections // repeat, kept, vertical.shape[1])
-    return jnp.einsum("gukl,ugmkpn->lmpn", mixing, owned, precision=PRECISE)
+    mixed = mix(owned, vertical, sections, groups, repeat)
+    mixed = mixed.reshape(block_waves, 2, block_degrees, vertical.shape[1])
+    return jnp.transpose(mixed, (3, 0, 1, 2))
 
 
 def solution(mesh):

time: 110 us -> 105 us (0.955)
  matrix products: 2.96 us -> 0 us
    dot_general x1 -> x0, matrix products: 2.96 us -> none  [shards(): return jnp.einsum('gukl,ugmkpn->lmpn', mixing, owned, precision=PRECISE)]
    pallas_call x1 -> x2, Pallas kernels: 17.7 us -> 18.9 us  [the longest x1 17.6 us: forcing_chunks(): pl.pallas_call(functools.partial(scatter_kernel, sections=sections, lats=...]
where the time goes in v4:
time: 105 us
  Pallas kernels  48.7 us (46%)
  waiting for transfers between devices  33.9 us (32%)
  blocking collectives  16.3 us (16%)
  starting transfers between devices  5.39 us (5%)
    ppermute x6, waiting for transfers between devices, exchange(): lax.ppermute(chunk, 'tm', [(i, i ^ slot) for i in range(sections)])  33.9 us
    pallas_call x1, Pallas kernels, sweep(): pl.pallas_call(functools.partial(sweep_kernel, sections=sections), out_sh...  18.4 us
    pallas_call x1, Pallas kernels, forcing_chunks(): pl.pallas_call(functools.partial(scatter_kernel, sections=sections, lats=...  17.6 us
    all_to_all x1, blocking collectives, shards(): lax.all_to_all(blocks, ('tm', 'lev'), split_axis=0, concat_axis=0, tiled=...  16.3 us
    pallas_call x1, Pallas kernels, legendre_tables(): pl.pallas_call(legendre_kernel, out_shape=[jax.ShapeDtypeStruct((wave_cou...  9.83 us
    ppermute x6, starting transfers between devices, exchange(): lax.ppermute(chunk, 'tm', [(i, i ^ slot) for i in range(sections)])  5.39 us
  transfers between devices with their start and end apart: 6, of which 2 were waited for; matrix products, arithmetic and copies ran while one was open for 1% of the time, Pallas kernels for 26%

profile of v4, /device:TPU:0, one launch (start us, length us, event | category | flops | bytes accessed | tf_op | source)
XLA Modules:
  0.0 105.2 jit_solution(842718217457918357)
XLA Ops:
  0.0 1.5 %cut.1 = (f32[2,128,512]{2,1,0:T(8,128)S(1)}, f32[2,128,512]{2,1,0:T(8,128)S(1)}, f32[2,128,512]{2,1,0:T(8,128)S(1)}, f32[2,128,512]{2,1,0:T(8,128)S(1)}) custom-call(f32[8,128,512]{2,1,0:T(8,128)} %bitcast.11), custom_call_target="tpu_custom_call" | custom-call | tf_op jit(solution)/shard_map/cut/pallas_call | solution.py:267
  1.6 0.6 collective-permute-start.3
  2.1 0.9 fusion.2.rows
  3.0 17.6 %scatter.1 = (f32[1032,128]{1,0:T(8,128)S(1)}, f32[1032,128]{1,0:T(8,128)S(1)}, f32[1032,128]{1,0:T(8,128)S(1)}, f32[1032,128]{1,0:T(8,128)S(1)}) custom-call(s32[16384]{0:T(1024)S(1)} %fusion.2.rows, s32[1,16384]{1,0:T(1,128)} %cells.1, f32[8,16384]{1,0:T(8,128)} %bitcast.12, f32[64,128]{1,0:T(8,128)} %bitcast.14), custom_call_target="tpu_custom_call" | custom-call | tf_op jit(solution)/shard_map/scatter/pallas_call | solution.py:284
  20.6 0.1 collective-permute-start
  20.7 3.0 %collective-permute-start.1 = (f32[1032,128]{1,0:T(8,128)S(1)}, f32[1032,128]{1,0:T(8,128)S(1)}, u32[]{:S(2)}, u32[]{:S(2)}) collective-permute-start(f32[1032,128]{1,0:T(8,128)S(1)} %get-tuple-element.23), channel_id=1, source_target_pairs={{0,16},{8,24},{16,0},{24,8},{1,17},{9,25},{17,1},{25,9},{2,18},{10... | collective-permute-start | bytes 1585160 | tf_op jit(solution)/shard_map/ppermute | solution.py:486
  23.7 0.0 collective-permute-start.2
  23.7 1.4 %collective-permute-start.4 = (f32[2,128,512]{2,1,0:T(8,128)S(1)}, f32[2,128,512]{2,1,0:T(8,128)S(1)}, u32[]{:S(2)}, u32[]{:S(2)}) collective-permute-start(f32[2,128,512]{2,1,0:T(8,128)S(1)} %get-tuple-element.27), channel_id=1, source_target_pairs={{0,16},{8,24},{16,0},{24,8},{1,17},{9,25},{17,1},{25,9},{2,18},{10... | collective-permute-start | bytes 1572872 | tf_op jit(solution)/shard_map/ppermute | solution.py:486
  25.1 0.0 collective-permute-done.3.refs_5_
  25.1 0.3 collective-permute-start.5
  25.4 9.8 %legendre.1 = (bf16[128,128,256]{2,1,0:T(8,128)(2,1)S(1)}, bf16[128,128,256]{2,1,0:T(8,128)(2,1)S(1)}, bf16[2,256,512]{2,1,0:T(8,128)(2,1)S(1)}, f32[64,128]{1,0:T(8,128)S(1)}) custom-call(f32[392,128]{1,0:T(8,128)} %constant.35.clone.seeds, bf16[2,256,512]{2,1,0:T(8,128)(2,1)} %constant.36.clone.fourier, f32[64,128]{1,0:T(8,128)} %spread.1), custom_call_target="tpu_custom_call" | custom-call | tf_op jit(solution)/shard_map/legendre/pallas_call | solution.py:148
  35.3 23.8 %collective-permute-done.4.refs_6_ = f32[2,128,512]{2,1,0:T(8,128)S(1)} collective-permute-done((f32[2,128,512]{2,1,0:T(8,128)S(1)}, f32[2,128,512]{2,1,0:T(8,128)S(1)}, u32[]{:S(2)}, u32[]{:S(2)}) %collective-permute-start.4) | collective-permute-done | bytes 524320 | tf_op jit(solution)/shard_map/ppermute | solution.py:486
  59.1 10.0 %collective-permute-done.5.refs_7_ = f32[2,128,512]{2,1,0:T(8,128)S(1)} collective-permute-done((f32[2,128,512]{2,1,0:T(8,128)S(1)}, f32[2,128,512]{2,1,0:T(8,128)S(1)}, u32[]{:S(2)}, u32[]{:S(2)}) %collective-permute-start.5) | collective-permute-done | bytes 524320 | tf_op jit(solution)/shard_map/ppermute | solution.py:486
  69.1 0.0 collective-permute-done.refs_1_
  69.1 0.0 collective-permute-done.1.refs_2_
  69.1 0.0 collective-permute-done.2.refs_3_
  69.1 0.0 copy-start
  69.1 18.4 %sweep.1 = f32[4,128,128]{2,1,0:T(8,128)S(1)} custom-call(bf16[128,128,256]{2,1,0:T(8,128)(2,1)S(1)} %get-tuple-element.17.analysis, bf16[128,128,256]{2,1,0:T(8,128)(2,1)S(1)} %get-tuple-element.18.synthesis, bf16[2,256,512]{2,1,0:T(8,128)(2,1)S(1)} %get-tuple-element.19.fourier, f32[64,128]{1,0:T(8,128)S(1)} %get-tuple-element.20.spread, ...), custom_call_target="tpu_custom_call" | custom-call | tf_op jit(solution)/shard_map/sweep/pallas_call | solution.py:414
  87.6 16.3 %all_to_all.5 = f32[32,16,128]{2,1,0:T(8,128)S(1)} all-to-all(f32[32,16,128]{2,1,0:T(8,128)S(1)} %bitcast.9), channel_id=1, replica_groups=mesh['tm'=4,'lev'=8] {'tm','lev'}, dimensions={0} | all-to-all | bytes 524288 | tf_op jit(solution)/shard_map/all_to_all | solution.py:500
  103.9 0.0 copy-done
  103.9 1.3 %mix.1 = f32[16,64,64]{2,1,0:T(8,128)} custom-call(f32[512,128]{1,0:T(8,128)S(1)} %bitcast.10, f32[64,64]{1,0:T(8,128)S(1)} %copy-done), custom_call_target="tpu_custom_call" | custom-call | tf_op jit(solution)/shard_map/mix/pallas_call | solution.py:466
Async XLA Ops:
  1.6 23.5 %collective-permute-start.3 = (f32[2,128,512]{2,1,0:T(8,128)S(1)}, f32[2,128,512]{2,1,0:T(8,128)S(1)}, u32[]{:S(2)}, u32[]{:S(2)}) collective-permute-start(f32[2,128,512]{2,1,0:T(8,128)S(1)} %get-tuple-element.26), channel_id=1, source_target_pairs={{0,8},{8,0},{16,24},{24,16},{1,9},{9,1},{17,25},{25,17},{2,10},{10... | collective-permute-start | bytes 1572872 | tf_op jit(solution)/shard_map/ppermute | solution.py:486
  20.6 48.5 %collective-permute-start = (f32[1032,128]{1,0:T(8,128)S(1)}, f32[1032,128]{1,0:T(8,128)S(1)}, u32[]{:S(2)}, u32[]{:S(2)}) collective-permute-start(f32[1032,128]{1,0:T(8,128)S(1)} %get-tuple-element.22), channel_id=1, source_target_pairs={{0,8},{8,0},{16,24},{24,16},{1,9},{9,1},{17,25},{25,17},{2,10},{10... | collective-permute-start | bytes 1585160 | tf_op jit(solution)/shard_map/ppermute | solution.py:486
  20.7 48.4 %collective-permute-start.1 = (f32[1032,128]{1,0:T(8,128)S(1)}, f32[1032,128]{1,0:T(8,128)S(1)}, u32[]{:S(2)}, u32[]{:S(2)}) collective-permute-start(f32[1032,128]{1,0:T(8,128)S(1)} %get-tuple-element.23), channel_id=1, source_target_pairs={{0,16},{8,24},{16,0},{24,8},{1,17},{9,25},{17,1},{25,9},{2,18},{10... | collective-permute-start | bytes 1585160 | tf_op jit(solution)/shard_map/ppermute | solution.py:486
  23.7 45.4 %collective-permute-start.2 = (f32[1032,128]{1,0:T(8,128)S(1)}, f32[1032,128]{1,0:T(8,128)S(1)}, u32[]{:S(2)}, u32[]{:S(2)}) collective-permute-start(f32[1032,128]{1,0:T(8,128)S(1)} %get-tuple-element.24), channel_id=1, source_target_pairs={{0,24},{8,16},{16,8},{24,0},{1,25},{9,17},{17,9},{25,1},{2,26},{10... | collective-permute-start | bytes 1585160 | tf_op jit(solution)/shard_map/ppermute | solution.py:486
  23.7 35.4 %collective-permute-start.4 = (f32[2,128,512]{2,1,0:T(8,128)S(1)}, f32[2,128,512]{2,1,0:T(8,128)S(1)}, u32[]{:S(2)}, u32[]{:S(2)}) collective-permute-start(f32[2,128,512]{2,1,0:T(8,128)S(1)} %get-tuple-element.27), channel_id=1, source_target_pairs={{0,16},{8,24},{16,0},{24,8},{1,17},{9,25},{17,1},{25,9},{2,18},{10... | collective-permute-start | bytes 1572872 | tf_op jit(solution)/shard_map/ppermute | solution.py:486
  25.1 44.0 %collective-permute-start.5 = (f32[2,128,512]{2,1,0:T(8,128)S(1)}, f32[2,128,512]{2,1,0:T(8,128)S(1)}, u32[]{:S(2)}, u32[]{:S(2)}) collective-permute-start(f32[2,128,512]{2,1,0:T(8,128)S(1)} %get-tuple-element.28), channel_id=1, source_target_pairs={{0,24},{8,16},{16,8},{24,0},{1,25},{9,17},{17,9},{25,1},{2,26},{10... | collective-permute-start | bytes 1572872 | tf_op jit(solution)/shard_map/ppermute | solution.py:486
  69.1 34.8 %copy-start = (f32[64,64]{1,0:T(8,128)S(1)}, f32[64,64]{1,0:T(8,128)}, u32[]{:S(2)}) copy-start(f32[64,64]{1,0:T(8,128)} %vertical.1) | copy-start | bytes 49156

commit v5 on v4

--- a/solution.py
+++ b/solution.py
@@ -14,18 +14,16 @@
 LANES = 128
 SUBLANES = 8
 ACCUMULATORS = 8
-OBS_BLOCK = 512
-WAVE_UNROLL = 16
+OBS_BLOCK = 1024
+INDEX_BUFFERS = 4
+WAVE_UNROLL = 64
 DEGREE_BLOCK = 16
+TABLE_UNROLL = 8
 SWEEP_MIB = 20
 
 
 def vmem():
     return pl.BlockSpec(memory_space=pltpu.VMEM)
-
-
-def smem():
-    return pl.BlockSpec(memory_space=pltpu.SMEM)
 
 
 def in_hbm(*arrays):
@@ -118,9 +116,9 @@
     for group in range(waves // DEGREE_BLOCK):
         skipped = group * DEGREE_BLOCK
 
-        def emit(quad, carry):
-            for step in range(4):
-                wave = skipped + 4 * quad + step
+        def emit(part, carry):
+            for step in range(TABLE_UNROLL):
+                wave = skipped + TABLE_UNROLL * part + step
                 start = skipped * pitch + wave
                 rows = values[pl.ds(start, waves - skipped, stride=pitch), :]
                 if skipped:
@@ -136,7 +134,7 @@
                     analysis[wave] = jnp.concatenate(split_parts(rows.T), axis=1)
             return carry
 
-        lax.fori_loop(0, DEGREE_BLOCK // 4, emit, 0)
+        lax.fori_loop(0, DEGREE_BLOCK // TABLE_UNROLL, emit, 0)
     for copy in nearer:
         copy.wait()
 
@@ -167,12 +165,13 @@
 def scatter_kernel(rows, cells, innov, damping, *refs, sections, lats, lons):
     levels, obs = innov.shape
     outs = refs[:sections]
-    field, even, odd, sems = refs[sections : sections + 4]
-    sums = refs[sections + 4 :]
+    field, sems = refs[sections : sections + 2]
+    datas = refs[sections + 2 : sections + 4]
+    nears = refs[sections + 4 : sections + 4 + INDEX_BUFFERS]
+    near_sems = refs[sections + 4 + INDEX_BUFFERS]
+    sums = refs[sections + 5 + INDEX_BUFFERS :]
     span = LANES // levels
     chunk = max(1, levels // sections)
-    for part in sums:
-        part[...] = jnp.zeros(part.shape, jnp.float32)
     row = lax.broadcasted_iota(jnp.int32, (4 * SUBLANES, 2 * LANES), 0)
     lane = lax.broadcasted_iota(jnp.int32, (4 * SUBLANES, 2 * LANES), 1)
     values_here = (row < 3 * SUBLANES) & (lane < LANES) & (row % SUBLANES == lane // span)
@@ -195,24 +194,39 @@
         placed = dot(stacked, place, 0, 0)
         data[...] = jnp.where(placed[:, LANES:] == lane_low, placed[:, :LANES], 0.0)
 
-    def add_rows(block, data):
-        start = pl.multiple_of(block * OBS_BLOCK, OBS_BLOCK)
+    def add_rows(near, data):
         for step in range(OBS_BLOCK):
             part = sums[step % ACCUMULATORS]
-            at = pl.ds(rows[start + step], 1)
+            at = pl.ds(near[step], 1)
             part[at, :] = part[at, :] + data[step : step + 1, :]
 
+    def fetch(block, buffer):
+        start = pl.multiple_of(block * OBS_BLOCK, OBS_BLOCK)
+        return pltpu.make_async_copy(
+            rows.at[pl.ds(start, OBS_BLOCK)], nears[buffer], near_sems.at[buffer]
+        )
+
     blocks = obs // OBS_BLOCK
-    spread_out(0, even)
-
-    def two_blocks(pair, carry):
-        spread_out(2 * pair + 1, odd)
-        add_rows(2 * pair, even)
-        spread_out(jnp.minimum(2 * pair + 2, blocks - 1), even)
-        add_rows(2 * pair + 1, odd)
+    for buffer in range(INDEX_BUFFERS):
+        fetch(buffer, buffer).start()
+    for part in sums:
+        part[...] = jnp.zeros(part.shape, jnp.float32)
+    spread_out(0, datas[0])
+
+    def some_blocks(group, carry):
+        for buffer in range(INDEX_BUFFERS):
+            block = group * INDEX_BUFFERS + buffer
+            fetch(block, buffer).wait()
+            spread_out(jnp.minimum(block + 1, blocks - 1), datas[(buffer + 1) % 2])
+            add_rows(nears[buffer], datas[buffer % 2])
+
+            @pl.when(block + INDEX_BUFFERS < blocks)
+            def _():
+                fetch(block + INDEX_BUFFERS, buffer).start()
+
         return carry
 
-    lax.fori_loop(0, blocks // 2, two_blocks, 0)
+    lax.fori_loop(0, blocks // INDEX_BUFFERS, some_blocks, 0)
 
     first = lax.axis_index("lev") * levels
     for high in range(lats // span):
@@ -284,14 +298,16 @@
     return pl.pallas_call(
         functools.partial(scatter_kernel, sections=sections, lats=lats, lons=lons),
         out_shape=[jax.ShapeDtypeStruct((size, LANES), jnp.float32)] * sections,
-        in_specs=[smem(), vmem(), vmem(), vmem()],
+        in_specs=[pl.BlockSpec(memory_space=pl.ANY), vmem(), vmem(), vmem()],
         out_specs=[pl.BlockSpec(memory_space=pl.ANY)] * sections,
         scratch_shapes=[
             pltpu.VMEM((levels // chunk, size, LANES), jnp.float32),
+            pltpu.SemaphoreType.DMA((sections,)),
             pltpu.VMEM((OBS_BLOCK, LANES), jnp.float32),
             pltpu.VMEM((OBS_BLOCK, LANES), jnp.float32),
-            pltpu.SemaphoreType.DMA((sections,)),
         ]
+        + [pltpu.SMEM((OBS_BLOCK,), jnp.int32)] * INDEX_BUFFERS
+        + [pltpu.SemaphoreType.DMA((INDEX_BUFFERS,))]
         + [pltpu.VMEM((lats * lons // span, LANES), jnp.float32)] * ACCUMULATORS,
         compiler_params=pltpu.CompilerParams(vmem_limit_bytes=32 * 2**20),
         name="scatter",

time: 105 us -> 98.3 us (0.936)
  Pallas kernels: 48.7 us -> 39.3 us
  waiting for transfers between devices: 33.9 us -> 36.1 us
    pallas_call x1, Pallas kernels: 18.4 us -> 13.5 us  [sweep(): pl.pallas_call(functools.partial(sweep_kernel, sections=sections), out_sh...]
    pallas_call x1, Pallas kernels: 9.83 us -> 7.59 us  [legendre_tables(): pl.pallas_call(legendre_kernel, out_shape=[jax.ShapeDtypeStruct((wave_cou...]
    ppermute x6, waiting for transfers between devices: 33.9 us -> 36.1 us  [exchange(): lax.ppermute(chunk, 'tm', [(i, i ^ slot) for i in range(sections)])]
    pallas_call x1, Pallas kernels: 17.6 us -> 15.4 us  [forcing_chunks(): pl.pallas_call(functools.partial(scatter_kernel, sections=sections, lats=...]
  transfers between devices with their start and end apart: 6 -> 6, of which waited for: 2 -> 2; matrix products, arithmetic and copies ran while one was open for 1% -> 1% of each run, Pallas kernels for 26% -> 23%
where the time goes in v5:
time: 98.3 us; the launch traced here: 98.1 us
  Pallas kernels  39.3 us (40%)
  waiting for transfers between devices  36.1 us (37%)
  blocking collectives  16.3 us (17%)
  starting transfers between devices  5.4 us (5%)
    ppermute x6, waiting for transfers between devices, exchange(): lax.ppermute(chunk, 'tm', [(i, i ^ slot) for i in range(sections)])  36.1 us
    all_to_all x1, blocking collectives, shards(): lax.all_to_all(blocks, ('tm', 'lev'), split_axis=0, concat_axis=0, tiled=...  16.3 us
    pallas_call x1, Pallas kernels, forcing_chunks(): pl.pallas_call(functools.partial(scatter_kernel, sections=sections, lats=...  15.4 us
    pallas_call x1, Pallas kernels, sweep(): pl.pallas_call(functools.partial(sweep_kernel, sections=sections), out_sh...  13.5 us
    pallas_call x1, Pallas kernels, legendre_tables(): pl.pallas_call(legendre_kernel, out_shape=[jax.ShapeDtypeStruct((wave_cou...  7.59 us
    ppermute x6, starting transfers between devices, exchange(): lax.ppermute(chunk, 'tm', [(i, i ^ slot) for i in range(sections)])  5.4 us
  transfers between devices with their start and end apart: 6, of which 2 were waited for; matrix products, arithmetic and copies ran while one was open for 1% of the time, Pallas kernels for 23%

profile of v5, /device:TPU:0, one launch (start us, length us, event | category | flops | bytes accessed | tf_op | source)
XLA Modules:
  0.0 98.1 jit_solution(4182261790252588523)
XLA Ops:
  0.0 1.5 %cut.1 = (f32[2,128,512]{2,1,0:T(8,128)S(1)}, f32[2,128,512]{2,1,0:T(8,128)S(1)}, f32[2,128,512]{2,1,0:T(8,128)S(1)}, f32[2,128,512]{2,1,0:T(8,128)S(1)}) custom-call(f32[8,128,512]{2,1,0:T(8,128)} %bitcast.11), custom_call_target="tpu_custom_call" | custom-call | tf_op jit(solution)/shard_map/cut/pallas_call | solution.py:281
  1.6 0.6 collective-permute-start.3
  2.1 0.9 fusion.2.rows
  3.0 15.4 %scatter.1 = (f32[1032,128]{1,0:T(8,128)S(1)}, f32[1032,128]{1,0:T(8,128)S(1)}, f32[1032,128]{1,0:T(8,128)S(1)}, f32[1032,128]{1,0:T(8,128)S(1)}) custom-call(s32[16384]{0:T(1024)S(1)} %fusion.2.rows, s32[1,16384]{1,0:T(1,128)} %cells.1, f32[8,16384]{1,0:T(8,128)} %bitcast.12, f32[64,128]{1,0:T(8,128)} %bitcast.14), custom_call_target="tpu_custom_call" | custom-call | tf_op jit(solution)/shard_map/scatter/pallas_call | solution.py:298
  18.4 0.1 collective-permute-start
  18.5 3.0 %collective-permute-start.1 = (f32[1032,128]{1,0:T(8,128)S(1)}, f32[1032,128]{1,0:T(8,128)S(1)}, u32[]{:S(2)}, u32[]{:S(2)}) collective-permute-start(f32[1032,128]{1,0:T(8,128)S(1)} %get-tuple-element.23), channel_id=1, source_target_pairs={{0,16},{8,24},{16,0},{24,8},{1,17},{9,25},{17,1},{25,9},{2,18},{10... | collective-permute-start | bytes 1585160 | tf_op jit(solution)/shard_map/ppermute | solution.py:502
  21.5 0.0 collective-permute-start.2
  21.5 1.4 %collective-permute-start.4 = (f32[2,128,512]{2,1,0:T(8,128)S(1)}, f32[2,128,512]{2,1,0:T(8,128)S(1)}, u32[]{:S(2)}, u32[]{:S(2)}) collective-permute-start(f32[2,128,512]{2,1,0:T(8,128)S(1)} %get-tuple-element.27), channel_id=1, source_target_pairs={{0,16},{8,24},{16,0},{24,8},{1,17},{9,25},{17,1},{25,9},{2,18},{10... | collective-permute-start | bytes 1572872 | tf_op jit(solution)/shard_map/ppermute | solution.py:502
  22.9 0.0 collective-permute-done.3.refs_5_
  22.9 0.3 collective-permute-start.5
  23.2 7.6 %legendre.1 = (bf16[128,128,256]{2,1,0:T(8,128)(2,1)S(1)}, bf16[128,128,256]{2,1,0:T(8,128)(2,1)S(1)}, bf16[2,256,512]{2,1,0:T(8,128)(2,1)S(1)}, f32[64,128]{1,0:T(8,128)S(1)}) custom-call(f32[392,128]{1,0:T(8,128)} %constant.35.clone.seeds, bf16[2,256,512]{2,1,0:T(8,128)(2,1)} %constant.36.clone.fourier, f32[64,128]{1,0:T(8,128)} %spread.1), custom_call_target="tpu_custom_call" | custom-call | tf_op jit(solution)/shard_map/legendre/pallas_call | solution.py:146
  30.8 26.1 %collective-permute-done.4.refs_6_ = f32[2,128,512]{2,1,0:T(8,128)S(1)} collective-permute-done((f32[2,128,512]{2,1,0:T(8,128)S(1)}, f32[2,128,512]{2,1,0:T(8,128)S(1)}, u32[]{:S(2)}, u32[]{:S(2)}) %collective-permute-start.4) | collective-permute-done | bytes 524320 | tf_op jit(solution)/shard_map/ppermute | solution.py:502
  56.9 10.0 %collective-permute-done.5.refs_7_ = f32[2,128,512]{2,1,0:T(8,128)S(1)} collective-permute-done((f32[2,128,512]{2,1,0:T(8,128)S(1)}, f32[2,128,512]{2,1,0:T(8,128)S(1)}, u32[]{:S(2)}, u32[]{:S(2)}) %collective-permute-start.5) | collective-permute-done | bytes 524320 | tf_op jit(solution)/shard_map/ppermute | solution.py:502
  66.9 0.0 collective-permute-done.refs_1_
  66.9 0.0 collective-permute-done.1.refs_2_
  66.9 0.0 collective-permute-done.2.refs_3_
  66.9 0.0 copy-start
  67.0 13.5 %sweep.1 = f32[4,128,128]{2,1,0:T(8,128)S(1)} custom-call(bf16[128,128,256]{2,1,0:T(8,128)(2,1)S(1)} %get-tuple-element.17.analysis, bf16[128,128,256]{2,1,0:T(8,128)(2,1)S(1)} %get-tuple-element.18.synthesis, bf16[2,256,512]{2,1,0:T(8,128)(2,1)S(1)} %get-tuple-element.19.fourier, f32[64,128]{1,0:T(8,128)S(1)} %get-tuple-element.20.spread, ...), custom_call_target="tpu_custom_call" | custom-call | tf_op jit(solution)/shard_map/sweep/pallas_call | solution.py:430
  80.5 16.3 %all_to_all.5 = f32[32,16,128]{2,1,0:T(8,128)S(1)} all-to-all(f32[32,16,128]{2,1,0:T(8,128)S(1)} %bitcast.9), channel_id=1, replica_groups=mesh['tm'=4,'lev'=8] {'tm','lev'}, dimensions={0} | all-to-all | bytes 524288 | tf_op jit(solution)/shard_map/all_to_all | solution.py:516
  96.8 0.0 copy-done
  96.8 1.3 %mix.1 = f32[16,64,64]{2,1,0:T(8,128)} custom-call(f32[512,128]{1,0:T(8,128)S(1)} %bitcast.10, f32[64,64]{1,0:T(8,128)S(1)} %copy-done), custom_call_target="tpu_custom_call" | custom-call | tf_op jit(solution)/shard_map/mix/pallas_call | solution.py:482
Async XLA Ops:
  1.6 21.4 %collective-permute-start.3 = (f32[2,128,512]{2,1,0:T(8,128)S(1)}, f32[2,128,512]{2,1,0:T(8,128)S(1)}, u32[]{:S(2)}, u32[]{:S(2)}) collective-permute-start(f32[2,128,512]{2,1,0:T(8,128)S(1)} %get-tuple-element.26), channel_id=1, source_target_pairs={{0,8},{8,0},{16,24},{24,16},{1,9},{9,1},{17,25},{25,17},{2,10},{10... | collective-permute-start | bytes 1572872 | tf_op jit(solution)/shard_map/ppermute | solution.py:502
  18.4 48.5 %collective-permute-start = (f32[1032,128]{1,0:T(8,128)S(1)}, f32[1032,128]{1,0:T(8,128)S(1)}, u32[]{:S(2)}, u32[]{:S(2)}) collective-permute-start(f32[1032,128]{1,0:T(8,128)S(1)} %get-tuple-element.22), channel_id=1, source_target_pairs={{0,8},{8,0},{16,24},{24,16},{1,9},{9,1},{17,25},{25,17},{2,10},{10... | collective-permute-start | bytes 1585160 | tf_op jit(solution)/shard_map/ppermute | solution.py:502
  18.5 48.5 %collective-permute-start.1 = (f32[1032,128]{1,0:T(8,128)S(1)}, f32[1032,128]{1,0:T(8,128)S(1)}, u32[]{:S(2)}, u32[]{:S(2)}) collective-permute-start(f32[1032,128]{1,0:T(8,128)S(1)} %get-tuple-element.23), channel_id=1, source_target_pairs={{0,16},{8,24},{16,0},{24,8},{1,17},{9,25},{17,1},{25,9},{2,18},{10... | collective-permute-start | bytes 1585160 | tf_op jit(solution)/shard_map/ppermute | solution.py:502
  21.5 45.4 %collective-permute-start.2 = (f32[1032,128]{1,0:T(8,128)S(1)}, f32[1032,128]{1,0:T(8,128)S(1)}, u32[]{:S(2)}, u32[]{:S(2)}) collective-permute-start(f32[1032,128]{1,0:T(8,128)S(1)} %get-tuple-element.24), channel_id=1, source_target_pairs={{0,24},{8,16},{16,8},{24,0},{1,25},{9,17},{17,9},{25,1},{2,26},{10... | collective-permute-start | bytes 1585160 | tf_op jit(solution)/shard_map/ppermute | solution.py:502
  21.5 35.4 %collective-permute-start.4 = (f32[2,128,512]{2,1,0:T(8,128)S(1)}, f32[2,128,512]{2,1,0:T(8,128)S(1)}, u32[]{:S(2)}, u32[]{:S(2)}) collective-permute-start(f32[2,128,512]{2,1,0:T(8,128)S(1)} %get-tuple-element.27), channel_id=1, source_target_pairs={{0,16},{8,24},{16,0},{24,8},{1,17},{9,25},{17,1},{25,9},{2,18},{10... | collective-permute-start | bytes 1572872 | tf_op jit(solution)/shard_map/ppermute | solution.py:502
  22.9 44.0 %collective-permute-start.5 = (f32[2,128,512]{2,1,0:T(8,128)S(1)}, f32[2,128,512]{2,1,0:T(8,128)S(1)}, u32[]{:S(2)}, u32[]{:S(2)}) collective-permute-start(f32[2,128,512]{2,1,0:T(8,128)S(1)} %get-tuple-element.28), channel_id=1, source_target_pairs={{0,24},{8,16},{16,8},{24,0},{1,25},{9,17},{17,9},{25,1},{2,26},{10... | collective-permute-start | bytes 1572872 | tf_op jit(solution)/shard_map/ppermute | solution.py:502
  66.9 29.8 %copy-start = (f32[64,64]{1,0:T(8,128)S(1)}, f32[64,64]{1,0:T(8,128)}, u32[]{:S(2)}) copy-start(f32[64,64]{1,0:T(8,128)} %vertical.1) | copy-start | bytes 49156

commit v6 on v5

--- a/solution.py
+++ b/solution.py
@@ -162,14 +162,15 @@
     )(*in_hbm(legendre_seeds(lat_count, wave_count), fourier, spread))
 
 
-def scatter_kernel(rows, cells, innov, damping, *refs, sections, lats, lons):
-    levels, obs = innov.shape
-    outs = refs[:sections]
-    field, sems = refs[sections : sections + 2]
-    datas = refs[sections + 2 : sections + 4]
-    nears = refs[sections + 4 : sections + 4 + INDEX_BUFFERS]
-    near_sems = refs[sections + 4 + INDEX_BUFFERS]
-    sums = refs[sections + 5 + INDEX_BUFFERS :]
+def scatter_kernel(rows, cells, innov, damping, *refs, sections, slots, relayed, lats, lons):
+    levels = innov.shape[0]
+    obs = cells.shape[1]
+    outs, refs = refs[:slots], refs[slots:]
+    field, sems = refs[:2]
+    datas = refs[2:4]
+    nears = refs[4 : 4 + INDEX_BUFFERS]
+    near_sems = refs[4 + INDEX_BUFFERS]
+    sums = refs[5 + INDEX_BUFFERS :]
     span = LANES // levels
     chunk = max(1, levels // sections)
     row = lax.broadcasted_iota(jnp.int32, (4 * SUBLANES, 2 * LANES), 0)
@@ -243,13 +244,17 @@
     for piece in range(levels // chunk):
         field[piece, tail:, :] = jnp.zeros((SUBLANES, LANES), jnp.float32)
         for k in range(chunk):
-            rates = damping[pl.ds(first + piece * chunk + k, 1), :]
+            if relayed:
+                rates = innov[k : k + 1, obs:]
+            else:
+                rates = damping[pl.ds(first + piece * chunk + k, 1), :]
             field[piece, tail + k : tail + k + 1, :] = rates
     me = lax.axis_index("tm")
     repeat = max(1, sections // levels)
+    pieces = levels // chunk
     copies = [
-        pltpu.make_async_copy(field.at[(me ^ slot) // repeat], outs[slot], sems.at[slot])
-        for slot in range(sections)
+        pltpu.make_async_copy(field.at[(me ^ slot) // repeat % pieces], outs[slot], sems.at[slot])
+        for slot in range(slots)
     ]
     for copy in copies:
         copy.start()
@@ -257,61 +262,97 @@
         copy.wait()
 
 
-def cut_kernel(field, *refs, sections):
-    outs, sems = refs[:sections], refs[sections]
+def cut_kernel(field, innov, damping, *refs, sections, relayed):
+    outs, refs = refs[:sections], refs[sections:]
     levels = field.shape[0]
     me = lax.axis_index("tm")
     chunk = max(1, levels // sections)
     repeat = max(1, sections // levels)
+    sems = refs[-1]
     copies = [
         pltpu.make_async_copy(
             field.at[pl.ds(((me ^ slot) // repeat) * chunk, chunk)], outs[slot], sems.at[slot]
         )
         for slot in range(sections)
     ]
+    if relayed:
+        relay, innov_near, damping_near = refs[:3]
+        nearer = [
+            pltpu.make_async_copy(innov, innov_near, sems.at[sections]),
+            pltpu.make_async_copy(damping, damping_near, sems.at[sections + 1]),
+        ]
+        copies = nearer + copies
     for copy in copies:
         copy.start()
+    if relayed:
+        for copy in nearer:
+            copy.wait()
+        obs = innov.shape[1]
+        first = lax.axis_index("lev") * levels + (me ^ relayed) * chunk
+        for k in range(chunk):
+            relay[k : k + 1, obs:] = damping_near[pl.ds(first + k, 1), :]
+        for piece in range(sections):
+
+            @pl.when(me ^ relayed == piece)
+            def _(here=slice(piece * chunk, (piece + 1) * chunk)):
+                relay[:, 0:obs] = innov_near[here, :]
+
+        copies = copies[2:]
     for copy in copies:
         copy.wait()
 
 
-def cut_chunks(field, sections):
+def cut_chunks(field, innov, damping, sections, relayed):
     levels, lats, lons = field.shape
     chunk = max(1, levels // sections)
+    out_shape = [jax.ShapeDtypeStruct((chunk, lats, lons), jnp.float32)] * sections
+    scratch = []
+    if relayed:
+        width = innov.shape[1] + damping.shape[1]
+        out_shape = out_shape + [jax.ShapeDtypeStruct((chunk, width), jnp.float32)]
+        scratch = [pltpu.VMEM(innov.shape, jnp.float32), pltpu.VMEM(damping.shape, jnp.float32)]
     return pl.pallas_call(
-        functools.partial(cut_kernel, sections=sections),
-        out_shape=[jax.ShapeDtypeStruct((chunk, lats, lons), jnp.float32)] * sections,
-        in_specs=[pl.BlockSpec(memory_space=pl.ANY)],
-        out_specs=[vmem()] * sections,
-        scratch_shapes=[pltpu.SemaphoreType.DMA((sections,))],
-        compiler_params=pltpu.CompilerParams(vmem_limit_bytes=4 * 2**20),
+        functools.partial(cut_kernel, sections=sections, relayed=relayed),
+        out_shape=out_shape,
+        in_specs=[pl.BlockSpec(memory_space=pl.ANY)] * 3,
+        out_specs=[vmem()] * len(out_shape),
+        scratch_shapes=scratch + [pltpu.SemaphoreType.DMA((sections + 2,))],
+        compiler_params=pltpu.CompilerParams(vmem_limit_bytes=6 * 2**20),
         name="cut",
-    )(field)
-
-
-def forcing_chunks(cells, innov, damping, lats, lons, sections):
-    levels, _ = innov.shape
+    )(*in_hbm(field, innov, damping))
+
+
+def forcing_chunks(cells, innov, damping, lats, lons, sections, slots, relayed=False):
+    levels = innov.shape[0]
     span = LANES // levels
     rows = (cells // (lons * span)) * lons + cells % lons
+    inputs = (cells[None, :], innov, damping)
     chunk = max(1, levels // sections)
     size = chunk * lats * lons // LANES + SUBLANES
     return pl.pallas_call(
-        functools.partial(scatter_kernel, sections=sections, lats=lats, lons=lons),
-        out_shape=[jax.ShapeDtypeStruct((size, LANES), jnp.float32)] * sections,
+        functools.partial(
+            scatter_kernel,
+            sections=sections,
+            slots=slots,
+            relayed=relayed,
+            lats=lats,
+            lons=lons,
+        ),
+        out_shape=[jax.ShapeDtypeStruct((size, LANES), jnp.float32)] * slots,
         in_specs=[pl.BlockSpec(memory_space=pl.ANY), vmem(), vmem(), vmem()],
-        out_specs=[pl.BlockSpec(memory_space=pl.ANY)] * sections,
+        out_specs=[pl.BlockSpec(memory_space=pl.ANY)] * slots,
         scratch_shapes=[
             pltpu.VMEM((levels // chunk, size, LANES), jnp.float32),
-            pltpu.SemaphoreType.DMA((sections,)),
+            pltpu.SemaphoreType.DMA((slots,)),
             pltpu.VMEM((OBS_BLOCK, LANES), jnp.float32),
             pltpu.VMEM((OBS_BLOCK, LANES), jnp.float32),
         ]
         + [pltpu.SMEM((OBS_BLOCK,), jnp.int32)] * INDEX_BUFFERS
         + [pltpu.SemaphoreType.DMA((INDEX_BUFFERS,))]
         + [pltpu.VMEM((lats * lons // span, LANES), jnp.float32)] * ACCUMULATORS,
-        compiler_params=pltpu.CompilerParams(vmem_limit_bytes=32 * 2**20),
+        compiler_params=pltpu.CompilerParams(vmem_limit_bytes=(12 if relayed else 32) * 2**20),
         name="scatter",
-    )(rows, *in_hbm(cells[None, :], innov, damping))
+    )(rows, *(inputs if relayed else in_hbm(*inputs)))
 
 
 def sweep_kernel(analysis, synthesis, fourier, spread, *refs, sections):
@@ -497,16 +538,27 @@
     repeat = max(1, sections // lev_dev)
     kept = max(1, lev_dev // sections)
 
+    relayed = sections - 1 if lev_dev >= sections > 2 else 0
+    direct = relayed or sections
+
+    def send(value, slot):
+        return lax.ppermute(value, "tm", [(i, i ^ slot) for i in range(sections)])
+
     def exchange(chunks):
-        return [
-            lax.ppermute(chunk, "tm", [(i, i ^ slot) for i in range(sections)]) if slot else chunk
-            for slot, chunk in enumerate(chunks)
-        ]
-
-    cut = cut_chunks(*in_hbm(tangent[0]), sections)
-    tangents = exchange(cut)
-    chunks = forcing_chunks(obs_cell[0], innovation[0], damping[0], lat_rows, lon_cols, sections)
+        return [send(chunk, slot) if slot else chunk for slot, chunk in enumerate(chunks)]
+
+    cells, innov, rates = obs_cell[0], innovation[0], damping[0]
+    cut = cut_chunks(tangent[0], innov, rates, sections, relayed)
+    if relayed:
+        far = send(cut[sections], relayed)
+        far_cells = send(obs_cell, relayed)[0]
+    tangents = exchange(cut[:sections])
+    chunks = forcing_chunks(
+        cells, innov, rates, lat_rows, lon_cols, sections, direct
+    )
     chunks = exchange(chunks)
+    if relayed:
+        chunks += forcing_chunks(far_cells, far, rates, lat_rows, lon_cols, 1, 1, True)
     tables = legendre_tables(lat_rows, lon_cols, wave_count, spread)
     blocks = sweep(chunks, tangents, tables)
 

time: 98.3 us -> 88.7 us (0.902)
  waiting for transfers between devices: 36.1 us -> 11.2 us
  Pallas kernels: 39.3 us -> 52.2 us
  starting transfers between devices: 5.4 us -> 6.81 us
    ppermute x6 -> x7, waiting for transfers between devices: 36.1 us -> 11.2 us  [send(): return lax.ppermute(value, 'tm', [(i, i ^ slot) for i in range(sections)])]
    pallas_call x2 -> x3, Pallas kernels: 16.9 us -> 30.1 us  [the longest x2 28.3 us: forcing_chunks(): pl.pallas_call(functools.partial(scatter_kernel, sections=sections, slots...]
    ppermute x6 -> x7, starting transfers between devices: 5.4 us -> 6.81 us  [send(): return lax.ppermute(value, 'tm', [(i, i ^ slot) for i in range(sections)])]
  transfers between devices with their start and end apart: 6 -> 7, of which waited for: 2 -> 2; matrix products, arithmetic and copies ran while one was open for 1% -> 1% of each run, Pallas kernels for 23% -> 43%
where the time goes in v6:
time: 88.7 us; the launch traced here: 88.4 us
  Pallas kernels  52.2 us (59%)
  blocking collectives  16.4 us (18%)
  waiting for transfers between devices  11.2 us (13%)
  starting transfers between devices  6.81 us (8%)
  other arithmetic  0.96 us (1%)
    pallas_call x2, Pallas kernels, forcing_chunks(): pl.pallas_call(functools.partial(scatter_kernel, sections=sections, slots...  28.3 us
    all_to_all x1, blocking collectives, shards(): lax.all_to_all(blocks, ('tm', 'lev'), split_axis=0, concat_axis=0, tiled=...  16.4 us
    pallas_call x1, Pallas kernels, sweep(): pl.pallas_call(functools.partial(sweep_kernel, sections=sections), out_sh...  13.3 us
    ppermute x7, waiting for transfers between devices, send(): return lax.ppermute(value, 'tm', [(i, i ^ slot) for i in range(sections)])  11.2 us
    pallas_call x1, Pallas kernels, legendre_tables(): pl.pallas_call(legendre_kernel, out_shape=[jax.ShapeDtypeStruct((wave_cou...  7.59 us
    ppermute x7, starting transfers between devices, send(): return lax.ppermute(value, 'tm', [(i, i ^ slot) for i in range(sections)])  6.81 us
  transfers between devices with their start and end apart: 7, of which 2 were waited for; matrix products, arithmetic and copies ran while one was open for 1% of the time, Pallas kernels for 43%

profile of v6, /device:TPU:0, one launch (start us, length us, event | category | flops | bytes accessed | tf_op | source)
XLA Modules:
  0.0 88.4 jit_solution(13386465678439716890)
XLA Ops:
  0.0 2.4 %collective-permute-start.2 = (s32[1,16384]{1,0:T(1,128)}, s32[1,16384]{1,0:T(1,128)S(1)}, u32[]{:S(2)}, u32[]{:S(2)}) collective-permute-start(s32[1,16384]{1,0:T(1,128)} %cells.1), channel_id=1, source_target_pairs={{0,24},{8,16},{16,8},{24,0},{1,25},{9,17},{17,9},{25,1},{2,26},{10... | collective-permute-start | bytes 196616 | tf_op jit(solution)/shard_map/ppermute | solution.py:545
  2.4 1.7 %cut.1 = (f32[2,128,512]{2,1,0:T(8,128)S(1)}, f32[2,128,512]{2,1,0:T(8,128)S(1)}, f32[2,128,512]{2,1,0:T(8,128)S(1)}, f32[2,128,512]{2,1,0:T(8,128)S(1)}, f32[2,16512]{1,0:T(2,128)S(1)}) custom-call(f32[8,128,512]{2,1,0:T(8,128)} %bitcast.16, f32[8,16384]{1,0:T(8,128)} %bitcast.17, f32[64,128]{1,0:T(8,128)} %bitcast.12), custom_call_target="tpu_custom_call" | custom-call | tf_op jit(solution)/shard_map/cut/pallas_call | solution.py:314
  4.2 0.1 collective-permute-start.3
  4.3 0.9 %fusion.2.rows = s32[16384]{0:T(1024)S(1)} fusion(s32[16384]{0:T(1024)} %bitcast.19), kind=kLoop, calls=%fused_computation.14 | loop fusion | flops 409600 | bytes 131072 | tf_op jit(solution)/shard_map/add | solution.py:328
  5.2 15.3 %scatter.2 = (f32[1032,128]{1,0:T(8,128)S(1)}, f32[1032,128]{1,0:T(8,128)S(1)}, f32[1032,128]{1,0:T(8,128)S(1)}) custom-call(s32[16384]{0:T(1024)S(1)} %fusion.2.rows, s32[1,16384]{1,0:T(1,128)} %cells.1, f32[8,16384]{1,0:T(8,128)} %bitcast.18, f32[64,128]{1,0:T(8,128)} %bitcast.13), custom_call_target="tpu_custom_call" | custom-call | tf_op jit(solution)/shard_map/scatter/pallas_call | solution.py:332
  20.5 0.7 collective-permute-start
  21.2 1.7 %collective-permute-start.1 = (f32[1032,128]{1,0:T(8,128)S(1)}, f32[1032,128]{1,0:T(8,128)S(1)}, u32[]{:S(2)}, u32[]{:S(2)}) collective-permute-start(f32[1032,128]{1,0:T(8,128)S(1)} %get-tuple-element.23), channel_id=1, source_target_pairs={{0,16},{8,24},{16,0},{24,8},{1,17},{9,25},{17,1},{25,9},{2,18},{10... | collective-permute-start | bytes 1585160 | tf_op jit(solution)/shard_map/ppermute | solution.py:545
  22.9 0.2 collective-permute-start.4
  23.1 0.0 collective-permute-done.2.cells
  23.1 0.3 collective-permute-start.5
  23.4 0.0 collective-permute-done.3.innov
  23.4 1.4 %collective-permute-start.6 = (f32[2,128,512]{2,1,0:T(8,128)S(1)}, f32[2,128,512]{2,1,0:T(8,128)S(1)}, u32[]{:S(2)}, u32[]{:S(2)}) collective-permute-start(f32[2,128,512]{2,1,0:T(8,128)S(1)} %get-tuple-element.28), channel_id=1, source_target_pairs={{0,24},{8,16},{16,8},{24,0},{1,25},{9,17},{17,9},{25,1},{2,26},{10... | collective-permute-start | bytes 1572872 | tf_op jit(solution)/shard_map/ppermute | solution.py:545
  24.8 7.6 %legendre.1 = (bf16[128,128,256]{2,1,0:T(8,128)(2,1)S(1)}, bf16[128,128,256]{2,1,0:T(8,128)(2,1)S(1)}, bf16[2,256,512]{2,1,0:T(8,128)(2,1)S(1)}, f32[64,128]{1,0:T(8,128)S(1)}) custom-call(f32[392,128]{1,0:T(8,128)} %constant.51.clone.seeds, bf16[2,256,512]{2,1,0:T(8,128)(2,1)} %constant.52.clone.fourier, f32[64,128]{1,0:T(8,128)} %spread.1), custom_call_target="tpu_custom_call" | custom-call | tf_op jit(solution)/shard_map/legendre/pallas_call | solution.py:146
  32.4 0.1 fusion.5.rows
  32.5 0.0 copy-start
  32.5 0.7 copy-done
  33.2 13.0 %scatter.3.refs_3_ = f32[1032,128]{1,0:T(8,128)S(1)} custom-call(s32[16384]{0:T(1024)S(1)} %fusion.5.rows, s32[1,16384]{1,0:T(1,128)S(1)} %collective-permute-done.2.cells, f32[2,16512]{1,0:T(2,128)S(1)} %collective-permute-done.3.innov, f32[64,128]{1,0:T(8,128)S(1)} %bitcast.14), custom_call_target="tpu_custom_call" | custom-call | tf_op jit(solution)/shard_map/scatter/pallas_call | solution.py:332
  46.2 0.0 collective-permute-done.4.refs_5_
  46.2 1.1 %collective-permute-done.5.refs_6_ = f32[2,128,512]{2,1,0:T(8,128)S(1)} collective-permute-done((f32[2,128,512]{2,1,0:T(8,128)S(1)}, f32[2,128,512]{2,1,0:T(8,128)S(1)}, u32[]{:S(2)}, u32[]{:S(2)}) %collective-permute-start.5) | collective-permute-done | bytes 524320 | tf_op jit(solution)/shard_map/ppermute | solution.py:545
  47.4 10.1 %collective-permute-done.6.refs_7_ = f32[2,128,512]{2,1,0:T(8,128)S(1)} collective-permute-done((f32[2,128,512]{2,1,0:T(8,128)S(1)}, f32[2,128,512]{2,1,0:T(8,128)S(1)}, u32[]{:S(2)}, u32[]{:S(2)}) %collective-permute-start.6) | collective-permute-done | bytes 524320 | tf_op jit(solution)/shard_map/ppermute | solution.py:545
  57.4 0.0 collective-permute-done.refs_1_
  57.4 0.0 collective-permute-done.1.refs_2_
  57.4 0.0 copy-start.1
  57.4 13.3 %sweep.1 = f32[4,128,128]{2,1,0:T(8,128)S(1)} custom-call(bf16[128,128,256]{2,1,0:T(8,128)(2,1)S(1)} %get-tuple-element.17.analysis, bf16[128,128,256]{2,1,0:T(8,128)(2,1)S(1)} %get-tuple-element.18.synthesis, bf16[2,256,512]{2,1,0:T(8,128)(2,1)S(1)} %get-tuple-element.19.fourier, f32[64,128]{1,0:T(8,128)S(1)} %get-tuple-element.20.spread, ...), custom_call_target="tpu_custom_call" | custom-call | tf_op jit(solution)/shard_map/sweep/pallas_call | solution.py:471
  70.7 16.4 %all_to_all.5 = f32[32,16,128]{2,1,0:T(8,128)S(1)} all-to-all(f32[32,16,128]{2,1,0:T(8,128)S(1)} %bitcast.10), channel_id=1, replica_groups=mesh['tm'=4,'lev'=8] {'tm','lev'}, dimensions={0} | all-to-all | bytes 524288 | tf_op jit(solution)/shard_map/all_to_all | solution.py:568
  87.1 0.0 copy-done.1
  87.1 1.3 %mix.1 = f32[16,64,64]{2,1,0:T(8,128)} custom-call(f32[512,128]{1,0:T(8,128)S(1)} %bitcast.11, f32[64,64]{1,0:T(8,128)S(1)} %copy-done.1), custom_call_target="tpu_custom_call" | custom-call | tf_op jit(solution)/shard_map/mix/pallas_call | solution.py:523
Async XLA Ops:
  0.0 23.1 %collective-permute-start.2 = (s32[1,16384]{1,0:T(1,128)}, s32[1,16384]{1,0:T(1,128)S(1)}, u32[]{:S(2)}, u32[]{:S(2)}) collective-permute-start(s32[1,16384]{1,0:T(1,128)} %cells.1), channel_id=1, source_target_pairs={{0,24},{8,16},{16,8},{24,0},{1,25},{9,17},{17,9},{25,1},{2,26},{10... | collective-permute-start | bytes 196616 | tf_op jit(solution)/shard_map/ppermute | solution.py:545
  4.2 19.2 %collective-permute-start.3 = (f32[2,16512]{1,0:T(2,128)S(1)}, f32[2,16512]{1,0:T(2,128)S(1)}, u32[]{:S(2)}, u32[]{:S(2)}) collective-permute-start(f32[2,16512]{1,0:T(2,128)S(1)} %get-tuple-element.24), channel_id=1, source_target_pairs={{0,24},{8,16},{16,8},{24,0},{1,25},{9,17},{17,9},{25,1},{2,26},{10... | collective-permute-start | bytes 396296 | tf_op jit(solution)/shard_map/ppermute | solution.py:545
  20.5 36.9 %collective-permute-start = (f32[1032,128]{1,0:T(8,128)S(1)}, f32[1032,128]{1,0:T(8,128)S(1)}, u32[]{:S(2)}, u32[]{:S(2)}) collective-permute-start(f32[1032,128]{1,0:T(8,128)S(1)} %get-tuple-element.22), channel_id=1, source_target_pairs={{0,8},{8,0},{16,24},{24,16},{1,9},{9,1},{17,25},{25,17},{2,10},{10... | collective-permute-start | bytes 1585160 | tf_op jit(solution)/shard_map/ppermute | solution.py:545
  21.2 36.2 %collective-permute-start.1 = (f32[1032,128]{1,0:T(8,128)S(1)}, f32[1032,128]{1,0:T(8,128)S(1)}, u32[]{:S(2)}, u32[]{:S(2)}) collective-permute-start(f32[1032,128]{1,0:T(8,128)S(1)} %get-tuple-element.23), channel_id=1, source_target_pairs={{0,16},{8,24},{16,0},{24,8},{1,17},{9,25},{17,1},{25,9},{2,18},{10... | collective-permute-start | bytes 1585160 | tf_op jit(solution)/shard_map/ppermute | solution.py:545
  22.9 23.3 %collective-permute-start.4 = (f32[2,128,512]{2,1,0:T(8,128)S(1)}, f32[2,128,512]{2,1,0:T(8,128)S(1)}, u32[]{:S(2)}, u32[]{:S(2)}) collective-permute-start(f32[2,128,512]{2,1,0:T(8,128)S(1)} %get-tuple-element.26), channel_id=1, source_target_pairs={{0,8},{8,0},{16,24},{24,16},{1,9},{9,1},{17,25},{25,17},{2,10},{10... | collective-permute-start | bytes 1572872 | tf_op jit(solution)/shard_map/ppermute | solution.py:545
  23.1 24.3 %collective-permute-start.5 = (f32[2,128,512]{2,1,0:T(8,128)S(1)}, f32[2,128,512]{2,1,0:T(8,128)S(1)}, u32[]{:S(2)}, u32[]{:S(2)}) collective-permute-start(f32[2,128,512]{2,1,0:T(8,128)S(1)} %get-tuple-element.27), channel_id=1, source_target_pairs={{0,16},{8,24},{16,0},{24,8},{1,17},{9,25},{17,1},{25,9},{2,18},{10... | collective-permute-start | bytes 1572872 | tf_op jit(solution)/shard_map/ppermute | solution.py:545
  23.4 34.1 %collective-permute-start.6 = (f32[2,128,512]{2,1,0:T(8,128)S(1)}, f32[2,128,512]{2,1,0:T(8,128)S(1)}, u32[]{:S(2)}, u32[]{:S(2)}) collective-permute-start(f32[2,128,512]{2,1,0:T(8,128)S(1)} %get-tuple-element.28), channel_id=1, source_target_pairs={{0,24},{8,16},{16,8},{24,0},{1,25},{9,17},{17,9},{25,1},{2,26},{10... | collective-permute-start | bytes 1572872 | tf_op jit(solution)/shard_map/ppermute | solution.py:545
  32.5 0.8 copy-start
  57.4 29.7 %copy-start.1 = (f32[64,64]{1,0:T(8,128)S(1)}, f32[64,64]{1,0:T(8,128)}, u32[]{:S(2)}) copy-start(f32[64,64]{1,0:T(8,128)} %vertical.1) | copy-start | bytes 49156

commit v7 on v6

--- a/solution.py
+++ b/solution.py
@@ -78,17 +78,17 @@
     )
 
 
-def legendre_kernel(
-    seeds, fourier, spread, analysis, synthesis, fourier_near, spread_near, values, sems
-):
-    waves, lats = analysis.shape[:2]
-    pitch = values.shape[0] // waves
-    nearer = [
+def bring_near(fourier, spread, fourier_near, spread_near, sems):
+    return [
         pltpu.make_async_copy(fourier, fourier_near, sems.at[0]),
         pltpu.make_async_copy(spread, spread_near, sems.at[1]),
     ]
-    for copy in nearer:
-        copy.start()
+
+
+def legendre_values(seeds, values, fill):
+    lats = values.shape[1]
+    waves = seeds.shape[0] // 3 // DEGREE_BLOCK * DEGREE_BLOCK
+    pitch = values.shape[0] // waves
     sine = seeds[3 * waves : 3 * waves + 1, :]
     one = jnp.zeros((0, lats), jnp.float32)
     two = one
@@ -109,34 +109,133 @@
         down = seeds[waves : waves + live, degree : degree + 1]
         current = (up * sine) * one - down * two + seed
         values[degree * pitch : degree * pitch + live, :] = current
+        if fill and live < waves:
+            values[degree * pitch + live : degree * pitch + waves, :] = jnp.zeros(
+                (waves - live, lats), jnp.float32
+            )
         one, two = current, one
 
-    row = lax.broadcasted_iota(jnp.int32, (lats, lats), 0)
-    identity = (row == lax.broadcasted_iota(jnp.int32, (lats, lats), 1)).astype(jnp.bfloat16)
+
+def write_tables(values, analysis, synthesis, wave, skipped, turn):
+    waves, lats = analysis.shape[:2]
+    pitch = values.shape[0] // waves
+    start = skipped * pitch + wave
+    rows = values[pl.ds(start, waves - skipped, stride=pitch), :]
+    if skipped:
+        rows = jnp.concatenate([jnp.zeros((skipped, lats), jnp.float32), rows], axis=0)
+    high, low = split_parts(rows)
+    synthesis[wave] = jnp.concatenate([high, low], axis=1)
+    if turn:
+        row = lax.broadcasted_iota(jnp.int32, (lats, lats), 0)
+        column = lax.broadcasted_iota(jnp.int32, (lats, lats), 1)
+        identity = (row == column).astype(jnp.bfloat16)
+        both = jnp.concatenate([high, low], axis=0)
+        analysis[wave] = dot(identity, both, 1, 1).astype(jnp.bfloat16)
+    else:
+        analysis[wave] = jnp.concatenate(split_parts(rows.T), axis=1)
+
+
+def legendre_kernel(
+    seeds, fourier, spread, analysis, synthesis, fourier_near, spread_near, values, sems
+):
+    waves = analysis.shape[0]
+    nearer = bring_near(fourier, spread, fourier_near, spread_near, sems)
+    for copy in nearer:
+        copy.start()
+    legendre_values(seeds, values, False)
     for group in range(waves // DEGREE_BLOCK):
         skipped = group * DEGREE_BLOCK
 
         def emit(part, carry):
             for step in range(TABLE_UNROLL):
                 wave = skipped + TABLE_UNROLL * part + step
-                start = skipped * pitch + wave
-                rows = values[pl.ds(start, waves - skipped, stride=pitch), :]
-                if skipped:
-                    rows = jnp.concatenate(
-                        [jnp.zeros((skipped, lats), jnp.float32), rows], axis=0
-                    )
-                high, low = split_parts(rows)
-                synthesis[wave] = jnp.concatenate([high, low], axis=1)
-                if step % 2:
-                    both = jnp.concatenate([high, low], axis=0)
-                    analysis[wave] = dot(identity, both, 1, 1).astype(jnp.bfloat16)
-                else:
-                    analysis[wave] = jnp.concatenate(split_parts(rows.T), axis=1)
+                write_tables(values, analysis, synthesis, wave, skipped, step % 2)
             return carry
 
         lax.fori_loop(0, DEGREE_BLOCK // TABLE_UNROLL, emit, 0)
     for copy in nearer:
         copy.wait()
+
+
+def far_kernel(
+    rows,
+    cells,
+    innov,
+    damping,
+    seeds,
+    fourier,
+    spread,
+    chunk,
+    analysis,
+    synthesis,
+    fourier_near,
+    spread_near,
+    values,
+    near_sems,
+    *scratch,
+    lats,
+    lons,
+):
+    nearer = bring_near(fourier, spread, fourier_near, spread_near, near_sems)
+    for copy in nearer:
+        copy.start()
+    legendre_values(seeds, values, True)
+    each = analysis.shape[0] // (cells.shape[1] // OBS_BLOCK)
+
+    def some_tables(block):
+        for step in range(each):
+            write_tables(values, analysis, synthesis, block * each + step, 0, step % 2)
+
+    scatter_kernel(
+        rows,
+        cells,
+        innov,
+        damping,
+        chunk,
+        *scratch,
+        sections=1,
+        slots=1,
+        relayed=True,
+        lats=lats,
+        lons=lons,
+        beside=some_tables,
+    )
+    for copy in nearer:
+        copy.wait()
+
+
+def table_shapes(lats, waves, fourier, spread):
+    return [
+        jax.ShapeDtypeStruct((waves, lats, 2 * waves), jnp.bfloat16),
+        jax.ShapeDtypeStruct((waves, waves, 2 * lats), jnp.bfloat16),
+        jax.ShapeDtypeStruct(fourier.shape, jnp.bfloat16),
+        jax.ShapeDtypeStruct(spread.shape, jnp.float32),
+    ]
+
+
+def far_chunk_and_tables(cells, innov, damping, lats, lons, waves, spread):
+    levels = innov.shape[0]
+    span = LANES // levels
+    rows = (cells // (lons * span)) * lons + cells % lons
+    size = levels * lats * lons // LANES + SUBLANES
+    fourier = np.stack(fourier_rows(lons, waves))
+    anywhere = pl.BlockSpec(memory_space=pl.ANY)
+    far = in_hbm(damping, legendre_seeds(lats, waves), fourier, spread)
+    chunk, *tables = pl.pallas_call(
+        functools.partial(far_kernel, lats=lats, lons=lons),
+        out_shape=[jax.ShapeDtypeStruct((size, LANES), jnp.float32)]
+        + table_shapes(lats, waves, fourier, spread),
+        in_specs=[anywhere, vmem(), vmem(), anywhere, vmem(), anywhere, anywhere],
+        out_specs=[anywhere] + [vmem()] * 4,
+        scratch_shapes=[
+            pltpu.VMEM((waves * (waves + SUBLANES), lats), jnp.float32),
+            pltpu.SemaphoreType.DMA((2,)),
+        ]
+        + scatter_scratch(levels, levels, size, 1, lats * lons // span),
+        compiler_params=pltpu.CompilerParams(vmem_limit_bytes=24 * 2**20),
+        name="far",
+    )(rows, cells[None, :], innov, *far)
+    return chunk, tables
 
 
 def legendre_tables(lat_count, lon_count, wave_count, spread):
@@ -145,12 +244,7 @@
     anywhere = pl.BlockSpec(memory_space=pl.ANY)
     return pl.pallas_call(
         legendre_kernel,
-        out_shape=[
-            jax.ShapeDtypeStruct((wave_count, lat_count, 2 * wave_count), jnp.bfloat16),
-            jax.ShapeDtypeStruct((wave_count, wave_count, 2 * lat_count), jnp.bfloat16),
-            jax.ShapeDtypeStruct(fourier.shape, jnp.bfloat16),
-            jax.ShapeDtypeStruct(spread.shape, jnp.float32),
-        ],
+        out_shape=table_shapes(lat_count, wave_count, fourier, spread),
         in_specs=[vmem(), anywhere, anywhere],
         out_specs=[vmem()] * 4,
         scratch_shapes=[
@@ -162,7 +256,9 @@
     )(*in_hbm(legendre_seeds(lat_count, wave_count), fourier, spread))
 
 
-def scatter_kernel(rows, cells, innov, damping, *refs, sections, slots, relayed, lats, lons):
+def scatter_kernel(
+    rows, cells, innov, damping, *refs, sections, slots, relayed, lats, lons, beside=None
+):
     levels = innov.shape[0]
     obs = cells.shape[1]
     outs, refs = refs[:slots], refs[slots:]
@@ -219,6 +315,8 @@
             block = group * INDEX_BUFFERS + buffer
             fetch(block, buffer).wait()
             spread_out(jnp.minimum(block + 1, blocks - 1), datas[(buffer + 1) % 2])
+            if beside:
+                beside(block)
             add_rows(nears[buffer], datas[buffer % 2])
 
             @pl.when(block + INDEX_BUFFERS < blocks)
@@ -322,11 +420,24 @@
     )(*in_hbm(field, innov, damping))
 
 
-def forcing_chunks(cells, innov, damping, lats, lons, sections, slots, relayed=False):
+def scatter_scratch(levels, chunk, size, slots, sum_rows):
+    return (
+        [
+            pltpu.VMEM((levels // chunk, size, LANES), jnp.float32),
+            pltpu.SemaphoreType.DMA((slots,)),
+            pltpu.VMEM((OBS_BLOCK, LANES), jnp.float32),
+            pltpu.VMEM((OBS_BLOCK, LANES), jnp.float32),
+        ]
+        + [pltpu.SMEM((OBS_BLOCK,), jnp.int32)] * INDEX_BUFFERS
+        + [pltpu.SemaphoreType.DMA((INDEX_BUFFERS,))]
+        + [pltpu.VMEM((sum_rows, LANES), jnp.float32)] * ACCUMULATORS
+    )
+
+
+def forcing_chunks(cells, innov, damping, lats, lons, sections, slots):
     levels = innov.shape[0]
     span = LANES // levels
     rows = (cells // (lons * span)) * lons + cells % lons
-    inputs = (cells[None, :], innov, damping)
     chunk = max(1, levels // sections)
     size = chunk * lats * lons // LANES + SUBLANES
     return pl.pallas_call(
@@ -334,25 +445,17 @@
             scatter_kernel,
             sections=sections,
             slots=slots,
-            relayed=relayed,
+            relayed=False,
             lats=lats,
             lons=lons,
         ),
         out_shape=[jax.ShapeDtypeStruct((size, LANES), jnp.float32)] * slots,
         in_specs=[pl.BlockSpec(memory_space=pl.ANY), vmem(), vmem(), vmem()],
         out_specs=[pl.BlockSpec(memory_space=pl.ANY)] * slots,
-        scratch_shapes=[
-            pltpu.VMEM((levels // chunk, size, LANES), jnp.float32),
-            pltpu.SemaphoreType.DMA((slots,)),
-            pltpu.VMEM((OBS_BLOCK, LANES), jnp.float32),
-            pltpu.VMEM((OBS_BLOCK, LANES), jnp.float32),
-        ]
-        + [pltpu.SMEM((OBS_BLOCK,), jnp.int32)] * INDEX_BUFFERS
-        + [pltpu.SemaphoreType.DMA((INDEX_BUFFERS,))]
-        + [pltpu.VMEM((lats * lons // span, LANES), jnp.float32)] * ACCUMULATORS,
-        compiler_params=pltpu.CompilerParams(vmem_limit_bytes=(12 if relayed else 32) * 2**20),
+        scratch_shapes=scatter_scratch(levels, chunk, size, slots, lats * lons // span),
+        compiler_params=pltpu.CompilerParams(vmem_limit_bytes=32 * 2**20),
         name="scatter",
-    )(rows, *(inputs if relayed else in_hbm(*inputs)))
+    )(rows, *in_hbm(cells[None, :], innov, damping))
 
 
 def sweep_kernel(analysis, synthesis, fourier, spread, *refs, sections):
@@ -558,8 +661,12 @@
     )
     chunks = exchange(chunks)
     if relayed:
-        chunks += forcing_chunks(far_cells, far, rates, lat_rows, lon_cols, 1, 1, True)
-    tables = legendre_tables(lat_rows, lon_cols, wave_count, spread)
+        chunk, tables = far_chunk_and_tables(
+            far_cells, far, rates, lat_rows, lon_cols, wave_count, spread
+        )
+        chunks.append(chunk)
+    else:
+        tables = legendre_tables(lat_rows, lon_cols, wave_count, spread)
     blocks = sweep(chunks, tangents, tables)
 
     block_waves = wave_count // groups

time: 88.7 us -> 89.1 us (level)
  waiting for transfers between devices: 11.2 us -> 14.5 us
  Pallas kernels: 52.2 us -> 50.2 us
    pallas_call x2 -> x1, Pallas kernels: 28.3 us -> 15.3 us  [forcing_chunks(): pl.pallas_call(functools.partial(scatter_kernel, sections=sections, slots...]
    pallas_call x1, Pallas kernels: 7.59 us -> 18 us  [far_chunk_and_tables(): pl.pallas_call(functools.partial(far_kernel, lats=lats, lons=lons), out_s...]
    ppermute x7, waiting for transfers between devices: 11.2 us -> 14.5 us  [send(): return lax.ppermute(value, 'tm', [(i, i ^ slot) for i in range(sections)])]
  transfers between devices with their start and end apart: 7 -> 7, of which waited for: 2 -> 2; matrix products, arithmetic and copies ran while one was open for 1% -> 1% of each run, Pallas kernels for 43% -> 39%
where the time goes in v7:
time: 89.1 us; the launch traced here: 88.9 us
  Pallas kernels  50.2 us (56%)
  blocking collectives  16.4 us (18%)
  waiting for transfers between devices  14.5 us (16%)
  starting transfers between devices  6.81 us (8%)
  other arithmetic  0.96 us (1%)
    pallas_call x1, Pallas kernels, far_chunk_and_tables(): pl.pallas_call(functools.partial(far_kernel, lats=lats, lons=lons), out_s...  18 us
    all_to_all x1, blocking collectives, shards(): lax.all_to_all(blocks, ('tm', 'lev'), split_axis=0, concat_axis=0, tiled=...  16.4 us
    pallas_call x1, Pallas kernels, forcing_chunks(): pl.pallas_call(functools.partial(scatter_kernel, sections=sections, slots...  15.3 us
    ppermute x7, waiting for transfers between devices, send(): return lax.ppermute(value, 'tm', [(i, i ^ slot) for i in range(sections)])  14.5 us
    pallas_call x1, Pallas kernels, sweep(): pl.pallas_call(functools.partial(sweep_kernel, sections=sections), out_sh...  13.7 us
    ppermute x7, starting transfers between devices, send(): return lax.ppermute(value, 'tm', [(i, i ^ slot) for i in range(sections)])  6.81 us
  transfers between devices with their start and end apart: 7, of which 2 were waited for; matrix products, arithmetic and copies ran while one was open for 1% of the time, Pallas kernels for 39%

profile of v7, /device:TPU:0, one launch (start us, length us, event | category | flops | bytes accessed | tf_op | source)
XLA Modules:
  0.0 88.9 jit_solution(14938463917864662293)
XLA Ops:
  0.0 2.4 %collective-permute-start = (s32[1,16384]{1,0:T(1,128)}, s32[1,16384]{1,0:T(1,128)S(1)}, u32[]{:S(2)}, u32[]{:S(2)}) collective-permute-start(s32[1,16384]{1,0:T(1,128)} %cells.1), channel_id=1, source_target_pairs={{0,24},{8,16},{16,8},{24,0},{1,25},{9,17},{17,9},{25,1},{2,26},{10... | collective-permute-start | bytes 196616 | tf_op jit(solution)/shard_map/ppermute | solution.py:648
  2.4 1.7 %cut.1 = (f32[2,128,512]{2,1,0:T(8,128)S(1)}, f32[2,128,512]{2,1,0:T(8,128)S(1)}, f32[2,128,512]{2,1,0:T(8,128)S(1)}, f32[2,128,512]{2,1,0:T(8,128)S(1)}, f32[2,16512]{1,0:T(2,128)S(1)}) custom-call(f32[8,128,512]{2,1,0:T(8,128)} %bitcast.13, f32[8,16384]{1,0:T(8,128)} %bitcast.14, f32[64,128]{1,0:T(8,128)} %bitcast.16), custom_call_target="tpu_custom_call" | custom-call | tf_op jit(solution)/shard_map/cut/pallas_call | solution.py:412
  4.2 0.1 collective-permute-start.1
  4.3 0.9 %fusion.5.rows = s32[16384]{0:T(1024)S(1)} fusion(s32[16384]{0:T(1024)} %bitcast.19), kind=kLoop, calls=%fused_computation.17 | loop fusion | flops 409600 | bytes 131072 | tf_op jit(solution)/shard_map/add | solution.py:440
  5.2 15.3 %scatter.1 = (f32[1032,128]{1,0:T(8,128)S(1)}, f32[1032,128]{1,0:T(8,128)S(1)}, f32[1032,128]{1,0:T(8,128)S(1)}) custom-call(s32[16384]{0:T(1024)S(1)} %fusion.5.rows, s32[1,16384]{1,0:T(1,128)} %cells.1, f32[8,16384]{1,0:T(8,128)} %bitcast.15, f32[64,128]{1,0:T(8,128)} %bitcast.17), custom_call_target="tpu_custom_call" | custom-call | tf_op jit(solution)/shard_map/scatter/pallas_call | solution.py:443
  20.5 0.7 collective-permute-start.2
  21.2 1.7 %collective-permute-start.3 = (f32[1032,128]{1,0:T(8,128)S(1)}, f32[1032,128]{1,0:T(8,128)S(1)}, u32[]{:S(2)}, u32[]{:S(2)}) collective-permute-start(f32[1032,128]{1,0:T(8,128)S(1)} %get-tuple-element.25), channel_id=1, source_target_pairs={{0,16},{8,24},{16,0},{24,8},{1,17},{9,25},{17,1},{25,9},{2,18},{10... | collective-permute-start | bytes 1585160 | tf_op jit(solution)/shard_map/ppermute | solution.py:648
  22.9 0.2 collective-permute-start.4
  23.1 0.0 collective-permute-done.cells
  23.1 0.3 collective-permute-start.5
  23.4 0.0 collective-permute-done.1.innov
  23.4 1.4 %collective-permute-start.6 = (f32[2,128,512]{2,1,0:T(8,128)S(1)}, f32[2,128,512]{2,1,0:T(8,128)S(1)}, u32[]{:S(2)}, u32[]{:S(2)}) collective-permute-start(f32[2,128,512]{2,1,0:T(8,128)S(1)} %get-tuple-element.30), channel_id=1, source_target_pairs={{0,24},{8,16},{16,8},{24,0},{1,25},{9,17},{17,9},{25,1},{2,26},{10... | collective-permute-start | bytes 1572872 | tf_op jit(solution)/shard_map/ppermute | solution.py:648
  24.8 0.1 fusion.2.rows
  24.9 18.0 %far.1 = (f32[1032,128]{1,0:T(8,128)S(1)}, bf16[128,128,256]{2,1,0:T(8,128)(2,1)S(1)}, bf16[128,128,256]{2,1,0:T(8,128)(2,1)S(1)}, bf16[2,256,512]{2,1,0:T(8,128)(2,1)S(1)}, f32[64,128]{1,0:T(8,128)S(1)}) custom-call(s32[16384]{0:T(1024)S(1)} %fusion.2.rows, s32[1,16384]{1,0:T(1,128)S(1)} %collective-permute-done.cells, ...), custom_call_target="tpu_custom_call" | custom-call | tf_op jit(solution)/shard_map/far/pallas_call | solution.py:224
  42.9 0.0 collective-permute-done.4.refs_5_
  42.9 4.4 %collective-permute-done.5.refs_6_ = f32[2,128,512]{2,1,0:T(8,128)S(1)} collective-permute-done((f32[2,128,512]{2,1,0:T(8,128)S(1)}, f32[2,128,512]{2,1,0:T(8,128)S(1)}, u32[]{:S(2)}, u32[]{:S(2)}) %collective-permute-start.5) | collective-permute-done | bytes 524320 | tf_op jit(solution)/shard_map/ppermute | solution.py:648
  47.4 10.1 %collective-permute-done.6.refs_7_ = f32[2,128,512]{2,1,0:T(8,128)S(1)} collective-permute-done((f32[2,128,512]{2,1,0:T(8,128)S(1)}, f32[2,128,512]{2,1,0:T(8,128)S(1)}, u32[]{:S(2)}, u32[]{:S(2)}) %collective-permute-start.6) | collective-permute-done | bytes 524320 | tf_op jit(solution)/shard_map/ppermute | solution.py:648
  57.4 0.0 collective-permute-done.2.refs_1_
  57.4 0.0 collective-permute-done.3.refs_2_
  57.4 0.0 copy-start
  57.4 13.7 %sweep.1 = f32[4,128,128]{2,1,0:T(8,128)S(1)} custom-call(bf16[128,128,256]{2,1,0:T(8,128)(2,1)S(1)} %get-tuple-element.19.analysis, bf16[128,128,256]{2,1,0:T(8,128)(2,1)S(1)} %get-tuple-element.20.synthesis, bf16[2,256,512]{2,1,0:T(8,128)(2,1)S(1)} %get-tuple-element.21.fourier, f32[64,128]{1,0:T(8,128)S(1)} %get-tuple-element.22.spread, ...), custom_call_target="tpu_custom_call" | custom-call | tf_op jit(solution)/shard_map/sweep/pallas_call | solution.py:574
  71.2 16.4 %all_to_all.5 = f32[32,16,128]{2,1,0:T(8,128)S(1)} all-to-all(f32[32,16,128]{2,1,0:T(8,128)S(1)} %bitcast.10), channel_id=1, replica_groups=mesh['tm'=4,'lev'=8] {'tm','lev'}, dimensions={0} | all-to-all | bytes 524288 | tf_op jit(solution)/shard_map/all_to_all | solution.py:675
  87.6 0.0 copy-done
  87.6 1.3 %mix.1 = f32[16,64,64]{2,1,0:T(8,128)} custom-call(f32[512,128]{1,0:T(8,128)S(1)} %bitcast.11, f32[64,64]{1,0:T(8,128)S(1)} %copy-done), custom_call_target="tpu_custom_call" | custom-call | tf_op jit(solution)/shard_map/mix/pallas_call | solution.py:626
Async XLA Ops:
  0.0 23.1 %collective-permute-start = (s32[1,16384]{1,0:T(1,128)}, s32[1,16384]{1,0:T(1,128)S(1)}, u32[]{:S(2)}, u32[]{:S(2)}) collective-permute-start(s32[1,16384]{1,0:T(1,128)} %cells.1), channel_id=1, source_target_pairs={{0,24},{8,16},{16,8},{24,0},{1,25},{9,17},{17,9},{25,1},{2,26},{10... | collective-permute-start | bytes 196616 | tf_op jit(solution)/shard_map/ppermute | solution.py:648
  4.2 19.2 %collective-permute-start.1 = (f32[2,16512]{1,0:T(2,128)S(1)}, f32[2,16512]{1,0:T(2,128)S(1)}, u32[]{:S(2)}, u32[]{:S(2)}) collective-permute-start(f32[2,16512]{1,0:T(2,128)S(1)} %get-tuple-element.18), channel_id=1, source_target_pairs={{0,24},{8,16},{16,8},{24,0},{1,25},{9,17},{17,9},{25,1},{2,26},{10... | collective-permute-start | bytes 396296 | tf_op jit(solution)/shard_map/ppermute | solution.py:648
  20.5 36.9 %collective-permute-start.2 = (f32[1032,128]{1,0:T(8,128)S(1)}, f32[1032,128]{1,0:T(8,128)S(1)}, u32[]{:S(2)}, u32[]{:S(2)}) collective-permute-start(f32[1032,128]{1,0:T(8,128)S(1)} %get-tuple-element.24), channel_id=1, source_target_pairs={{0,8},{8,0},{16,24},{24,16},{1,9},{9,1},{17,25},{25,17},{2,10},{10... | collective-permute-start | bytes 1585160 | tf_op jit(solution)/shard_map/ppermute | solution.py:648
  21.2 36.2 %collective-permute-start.3 = (f32[1032,128]{1,0:T(8,128)S(1)}, f32[1032,128]{1,0:T(8,128)S(1)}, u32[]{:S(2)}, u32[]{:S(2)}) collective-permute-start(f32[1032,128]{1,0:T(8,128)S(1)} %get-tuple-element.25), channel_id=1, source_target_pairs={{0,16},{8,24},{16,0},{24,8},{1,17},{9,25},{17,1},{25,9},{2,18},{10... | collective-permute-start | bytes 1585160 | tf_op jit(solution)/shard_map/ppermute | solution.py:648
  22.9 20.0 %collective-permute-start.4 = (f32[2,128,512]{2,1,0:T(8,128)S(1)}, f32[2,128,512]{2,1,0:T(8,128)S(1)}, u32[]{:S(2)}, u32[]{:S(2)}) collective-permute-start(f32[2,128,512]{2,1,0:T(8,128)S(1)} %get-tuple-element.28), channel_id=1, source_target_pairs={{0,8},{8,0},{16,24},{24,16},{1,9},{9,1},{17,25},{25,17},{2,10},{10... | collective-permute-start | bytes 1572872 | tf_op jit(solution)/shard_map/ppermute | solution.py:648
  23.1 24.3 %collective-permute-start.5 = (f32[2,128,512]{2,1,0:T(8,128)S(1)}, f32[2,128,512]{2,1,0:T(8,128)S(1)}, u32[]{:S(2)}, u32[]{:S(2)}) collective-permute-start(f32[2,128,512]{2,1,0:T(8,128)S(1)} %get-tuple-element.29), channel_id=1, source_target_pairs={{0,16},{8,24},{16,0},{24,8},{1,17},{9,25},{17,1},{25,9},{2,18},{10... | collective-permute-start | bytes 1572872 | tf_op jit(solution)/shard_map/ppermute | solution.py:648
  23.4 34.1 %collective-permute-start.6 = (f32[2,128,512]{2,1,0:T(8,128)S(1)}, f32[2,128,512]{2,1,0:T(8,128)S(1)}, u32[]{:S(2)}, u32[]{:S(2)}) collective-permute-start(f32[2,128,512]{2,1,0:T(8,128)S(1)} %get-tuple-element.30), channel_id=1, source_target_pairs={{0,24},{8,16},{16,8},{24,0},{1,25},{9,17},{17,9},{25,1},{2,26},{10... | collective-permute-start | bytes 1572872 | tf_op jit(solution)/shard_map/ppermute | solution.py:648
  57.4 30.1 %copy-start = (f32[64,64]{1,0:T(8,128)S(1)}, f32[64,64]{1,0:T(8,128)}, u32[]{:S(2)}) copy-start(f32[64,64]{1,0:T(8,128)} %vertical.1) | copy-start | bytes 49156

commit v8 on v7

--- a/solution.py
+++ b/solution.py
@@ -85,7 +85,7 @@
     ]
 
 
-def legendre_values(seeds, values, fill):
+def legendre_values(seeds, values):
     lats = values.shape[1]
     waves = seeds.shape[0] // 3 // DEGREE_BLOCK * DEGREE_BLOCK
     pitch = values.shape[0] // waves
@@ -109,17 +109,13 @@
         down = seeds[waves : waves + live, degree : degree + 1]
         current = (up * sine) * one - down * two + seed
         values[degree * pitch : degree * pitch + live, :] = current
-        if fill and live < waves:
-            values[degree * pitch + live : degree * pitch + waves, :] = jnp.zeros(
-                (waves - live, lats), jnp.float32
-            )
         one, two = current, one
 
 
-def write_tables(values, analysis, synthesis, wave, skipped, turn):
+def write_tables(values, analysis, synthesis, wave, skipped, turn, lead=0):
     waves, lats = analysis.shape[:2]
-    pitch = values.shape[0] // waves
-    start = skipped * pitch + wave
+    pitch = waves + SUBLANES
+    start = (skipped + lead) * pitch + wave
     rows = values[pl.ds(start, waves - skipped, stride=pitch), :]
     if skipped:
         rows = jnp.concatenate([jnp.zeros((skipped, lats), jnp.float32), rows], axis=0)
@@ -142,7 +138,7 @@
     nearer = bring_near(fourier, spread, fourier_near, spread_near, sems)
     for copy in nearer:
         copy.start()
-    legendre_values(seeds, values, False)
+    legendre_values(seeds, values)
     for group in range(waves // DEGREE_BLOCK):
         skipped = group * DEGREE_BLOCK
 
@@ -157,12 +153,86 @@
         copy.wait()
 
 
+def near_kernel(rows, cells, innov, damping, seeds, *refs, sections, slots, lats, lons):
+    values, seeds_near, up_now, down_now, sem = refs[slots : slots + 5]
+    waves = up_now.shape[0]
+    pitch = waves + SUBLANES
+    each = waves // (cells.shape[1] // OBS_BLOCK)
+    nearer = pltpu.make_async_copy(seeds, seeds_near, sem.at[0])
+    nearer.start()
+    values[0 : 2 * pitch, :] = jnp.zeros((2 * pitch, lats), jnp.float32)
+    nearer.wait()
+    up_now[...] = seeds_near[0:waves, :]
+    down_now[...] = seeds_near[waves : 2 * waves, :]
+
+    def some_degrees(block):
+        order = lax.broadcasted_iota(jnp.int32, (waves, lats), 0)
+        sine = seeds_near[3 * waves : 3 * waves + 1, :]
+
+        def stored(degree):
+            return pl.ds(pl.multiple_of((degree + 2) * pitch, SUBLANES), waves)
+
+        one = values[stored(block * each - 1), :]
+        two = values[stored(block * each - 2), :]
+        for step in range(each):
+            degree = block * each + step
+            seed = jnp.where(order == degree, seeds_near[2 * waves : 3 * waves, :], 0.0)
+            current = (up_now[:, step : step + 1] * sine) * one
+            current = current - down_now[:, step : step + 1] * two + seed
+            values[stored(degree), :] = current
+            one, two = current, one
+        up_now[...] = pltpu.roll(up_now[...], waves - each, 1)
+        down_now[...] = pltpu.roll(down_now[...], waves - each, 1)
+
+    scatter_kernel(
+        rows,
+        cells,
+        innov,
+        damping,
+        *refs[:slots],
+        *refs[slots + 5 :],
+        sections=sections,
+        slots=slots,
+        relayed=False,
+        lats=lats,
+        lons=lons,
+        beside=some_degrees,
+    )
+
+
+def near_chunks_and_values(cells, innov, damping, lats, lons, waves, sections, slots):
+    levels = innov.shape[0]
+    span = LANES // levels
+    rows = (cells // (lons * span)) * lons + cells % lons
+    chunk = max(1, levels // sections)
+    size = chunk * lats * lons // LANES + SUBLANES
+    seeds = legendre_seeds(lats, waves)
+    anywhere = pl.BlockSpec(memory_space=pl.ANY)
+    *chunks, values = pl.pallas_call(
+        functools.partial(near_kernel, sections=sections, slots=slots, lats=lats, lons=lons),
+        out_shape=[jax.ShapeDtypeStruct((size, LANES), jnp.float32)] * slots
+        + [jax.ShapeDtypeStruct(((waves + 2) * (waves + SUBLANES), lats), jnp.float32)],
+        in_specs=[anywhere, vmem(), vmem(), vmem(), anywhere],
+        out_specs=[anywhere] * slots + [vmem()],
+        scratch_shapes=[
+            pltpu.VMEM(seeds.shape, jnp.float32),
+            pltpu.VMEM((waves, waves), jnp.float32),
+            pltpu.VMEM((waves, waves), jnp.float32),
+            pltpu.SemaphoreType.DMA((1,)),
+        ]
+        + scatter_scratch(levels, chunk, size, slots, lats * lons // span),
+        compiler_params=pltpu.CompilerParams(vmem_limit_bytes=32 * 2**20),
+        name="near",
+    )(rows, *in_hbm(cells[None, :], innov, damping, seeds))
+    return chunks, values
+
+
 def far_kernel(
     rows,
     cells,
     innov,
     damping,
-    seeds,
+    values,
     fourier,
     spread,
     chunk,
@@ -170,7 +240,6 @@
     synthesis,
     fourier_near,
     spread_near,
-    values,
     near_sems,
     *scratch,
     lats,
@@ -179,12 +248,11 @@
     nearer = bring_near(fourier, spread, fourier_near, spread_near, near_sems)
     for copy in nearer:
         copy.start()
-    legendre_values(seeds, values, True)
     each = analysis.shape[0] // (cells.shape[1] // OBS_BLOCK)
 
     def some_tables(block):
         for step in range(each):
-            write_tables(values, analysis, synthesis, block * each + step, 0, step % 2)
+            write_tables(values, analysis, synthesis, block * each + step, 0, step % 2, 2)
 
     scatter_kernel(
         rows,
@@ -213,26 +281,23 @@
     ]
 
 
-def far_chunk_and_tables(cells, innov, damping, lats, lons, waves, spread):
+def far_chunk_and_tables(cells, innov, damping, values, lats, lons, waves, spread):
     levels = innov.shape[0]
     span = LANES // levels
     rows = (cells // (lons * span)) * lons + cells % lons
     size = levels * lats * lons // LANES + SUBLANES
     fourier = np.stack(fourier_rows(lons, waves))
     anywhere = pl.BlockSpec(memory_space=pl.ANY)
-    far = in_hbm(damping, legendre_seeds(lats, waves), fourier, spread)
+    far = [*in_hbm(damping), values, *in_hbm(fourier, spread)]
     chunk, *tables = pl.pallas_call(
         functools.partial(far_kernel, lats=lats, lons=lons),
         out_shape=[jax.ShapeDtypeStruct((size, LANES), jnp.float32)]
         + table_shapes(lats, waves, fourier, spread),
         in_specs=[anywhere, vmem(), vmem(), anywhere, vmem(), anywhere, anywhere],
         out_specs=[anywhere] + [vmem()] * 4,
-        scratch_shapes=[
-            pltpu.VMEM((waves * (waves + SUBLANES), lats), jnp.float32),
-            pltpu.SemaphoreType.DMA((2,)),
-        ]
+        scratch_shapes=[pltpu.SemaphoreType.DMA((2,))]
         + scatter_scratch(levels, levels, size, 1, lats * lons // span),
-        compiler_params=pltpu.CompilerParams(vmem_limit_bytes=24 * 2**20),
+        compiler_params=pltpu.CompilerParams(vmem_limit_bytes=14 * 2**20),
         name="far",
     )(rows, cells[None, :], innov, *far)
     return chunk, tables
@@ -653,16 +718,22 @@
     cells, innov, rates = obs_cell[0], innovation[0], damping[0]
     cut = cut_chunks(tangent[0], innov, rates, sections, relayed)
     if relayed:
+        *cut, cells_late = lax.optimization_barrier((*cut, obs_cell))
         far = send(cut[sections], relayed)
-        far_cells = send(obs_cell, relayed)[0]
+        far_cells = send(cells_late, relayed)[0]
     tangents = exchange(cut[:sections])
-    chunks = forcing_chunks(
-        cells, innov, rates, lat_rows, lon_cols, sections, direct
-    )
+    if relayed:
+        chunks, values = near_chunks_and_values(
+            cells, innov, rates, lat_rows, lon_cols, wave_count, sections, direct
+        )
+    else:
+        chunks = forcing_chunks(
+            cells, innov, rates, lat_rows, lon_cols, sections, direct
+        )
     chunks = exchange(chunks)
     if relayed:
         chunk, tables = far_chunk_and_tables(
-            far_cells, far, rates, lat_rows, lon_cols, wave_count, spread
+            far_cells, far, rates, values, lat_rows, lon_cols, wave_count, spread
         )
         chunks.append(chunk)
     else:

time: 89.1 us -> 91.9 us (1.031)
  waiting for transfers between devices: 14.5 us -> 18 us
    pallas_call x1, Pallas kernels: 18 us -> 14.4 us  [far_chunk_and_tables(): pl.pallas_call(functools.partial(far_kernel, lats=lats, lons=lons), out_s...]
    ppermute x7, waiting for transfers between devices: 14.5 us -> 18 us  [send(): return lax.ppermute(value, 'tm', [(i, i ^ slot) for i in range(sections)])]
    pallas_call x1, Pallas kernels: 15.3 us -> 18.3 us  [near_chunks_and_values(): pl.pallas_call(functools.partial(near_kernel, sections=sections, slots=sl...]
  transfers between devices with their start and end apart: 7 -> 7, of which waited for: 2 -> 2; matrix products, arithmetic and copies ran while one was open for 1% -> 1% of each run, Pallas kernels for 39% -> 36%
where the time goes in v8:
time: 91.9 us; the launch traced here: 91.7 us
  Pallas kernels  49.3 us (54%)
  waiting for transfers between devices  18 us (20%)
  blocking collectives  16.5 us (18%)
  starting transfers between devices  6.8 us (7%)
  other arithmetic  0.96 us (1%)
    pallas_call x1, Pallas kernels, near_chunks_and_values(): pl.pallas_call(functools.partial(near_kernel, sections=sections, slots=sl...  18.3 us
    ppermute x7, waiting for transfers between devices, send(): return lax.ppermute(value, 'tm', [(i, i ^ slot) for i in range(sections)])  18 us
    all_to_all x1, blocking collectives, shards(): lax.all_to_all(blocks, ('tm', 'lev'), split_axis=0, concat_axis=0, tiled=...  16.5 us
    pallas_call x1, Pallas kernels, far_chunk_and_tables(): pl.pallas_call(functools.partial(far_kernel, lats=lats, lons=lons), out_s...  14.4 us
    pallas_call x1, Pallas kernels, sweep(): pl.pallas_call(functools.partial(sweep_kernel, sections=sections), out_sh...  13.6 us
    ppermute x7, starting transfers between devices, send(): return lax.ppermute(value, 'tm', [(i, i ^ slot) for i in range(sections)])  6.8 us
  transfers between devices with their start and end apart: 7, of which 2 were waited for; matrix products, arithmetic and copies ran while one was open for 1% of the time, Pallas kernels for 36%

profile of v8, /device:TPU:0, one launch (start us, length us, event | category | flops | bytes accessed | tf_op | source)
XLA Modules:
  0.0 91.7 jit_solution(6584038073707811644)
XLA Ops:
  0.0 1.7 %cut.1 = (f32[2,128,512]{2,1,0:T(8,128)S(1)}, f32[2,128,512]{2,1,0:T(8,128)S(1)}, f32[2,128,512]{2,1,0:T(8,128)S(1)}, f32[2,128,512]{2,1,0:T(8,128)S(1)}, f32[2,16512]{1,0:T(2,128)S(1)}) custom-call(f32[8,128,512]{2,1,0:T(8,128)} %bitcast.13, f32[8,16384]{1,0:T(8,128)} %bitcast.14, f32[64,128]{1,0:T(8,128)} %bitcast.16), custom_call_target="tpu_custom_call" | custom-call | tf_op jit(solution)/shard_map/cut/pallas_call | solution.py:477
  1.7 2.5 %collective-permute-start = (s32[1,16384]{1,0:T(1,128)}, s32[1,16384]{1,0:T(1,128)S(1)}, u32[]{:S(2)}, u32[]{:S(2)}) collective-permute-start(s32[1,16384]{1,0:T(1,128)} %cells.1), channel_id=1, source_target_pairs={{0,24},{8,16},{16,8},{24,0},{1,25},{9,17},{17,9},{25,1},{2,26},{10... | collective-permute-start | bytes 196616 | tf_op jit(solution)/shard_map/ppermute | solution.py:713
  4.2 0.1 collective-permute-start.1
  4.3 0.9 fusion.5.rows
  5.2 18.3 %near.1 = (f32[1032,128]{1,0:T(8,128)S(1)}, f32[1032,128]{1,0:T(8,128)S(1)}, f32[1032,128]{1,0:T(8,128)S(1)}, f32[17680,128]{1,0:T(8,128)S(1)}) custom-call(s32[16384]{0:T(1024)S(1)} %fusion.5.rows, s32[1,16384]{1,0:T(1,128)} %cells.1, f32[8,16384]{1,0:T(8,128)} %bitcast.15, f32[64,128]{1,0:T(8,128)} %bitcast.17, f32[392,128]{1,0:T(8,128)} %constant.51.clone.seeds), custom_call_target="tpu_custom_call" | custom-call | tf_op jit(solution)/shard_map/near/pallas_call | solution.py:211
  23.5 0.7 collective-permute-start.2
  24.2 1.6 %collective-permute-start.3 = (f32[1032,128]{1,0:T(8,128)S(1)}, f32[1032,128]{1,0:T(8,128)S(1)}, u32[]{:S(2)}, u32[]{:S(2)}) collective-permute-start(f32[1032,128]{1,0:T(8,128)S(1)} %get-tuple-element.39), channel_id=1, source_target_pairs={{0,16},{8,24},{16,0},{24,8},{1,17},{9,25},{17,1},{25,9},{2,18},{10... | collective-permute-start | bytes 1585160 | tf_op jit(solution)/shard_map/ppermute | solution.py:713
  25.9 0.2 collective-permute-start.4
  26.0 0.0 collective-permute-done.cells
  26.0 0.3 collective-permute-start.5
  26.3 0.0 collective-permute-done.1.innov
  26.3 1.4 %collective-permute-start.6 = (f32[2,128,512]{2,1,0:T(8,128)S(1)}, f32[2,128,512]{2,1,0:T(8,128)S(1)}, u32[]{:S(2)}, u32[]{:S(2)}) collective-permute-start(f32[2,128,512]{2,1,0:T(8,128)S(1)} %get-tuple-element.44), channel_id=1, source_target_pairs={{0,24},{8,16},{16,8},{24,0},{1,25},{9,17},{17,9},{25,1},{2,26},{10... | collective-permute-start | bytes 1572872 | tf_op jit(solution)/shard_map/ppermute | solution.py:713
  27.7 0.1 fusion.2.rows
  27.8 14.4 %far.1 = (f32[1032,128]{1,0:T(8,128)S(1)}, bf16[128,128,256]{2,1,0:T(8,128)(2,1)S(1)}, bf16[128,128,256]{2,1,0:T(8,128)(2,1)S(1)}, bf16[2,256,512]{2,1,0:T(8,128)(2,1)S(1)}, f32[64,128]{1,0:T(8,128)S(1)}) custom-call(s32[16384]{0:T(1024)S(1)} %fusion.2.rows, s32[1,16384]{1,0:T(1,128)S(1)} %collective-permute-done.cells, ...), custom_call_target="tpu_custom_call" | custom-call | tf_op jit(solution)/shard_map/far/pallas_call | solution.py:292
  42.2 0.0 collective-permute-done.4.refs_5_
  42.2 8.1 %collective-permute-done.5.refs_6_ = f32[2,128,512]{2,1,0:T(8,128)S(1)} collective-permute-done((f32[2,128,512]{2,1,0:T(8,128)S(1)}, f32[2,128,512]{2,1,0:T(8,128)S(1)}, u32[]{:S(2)}, u32[]{:S(2)}) %collective-permute-start.5) | collective-permute-done | bytes 524320 | tf_op jit(solution)/shard_map/ppermute | solution.py:713
  50.4 9.9 %collective-permute-done.6.refs_7_ = f32[2,128,512]{2,1,0:T(8,128)S(1)} collective-permute-done((f32[2,128,512]{2,1,0:T(8,128)S(1)}, f32[2,128,512]{2,1,0:T(8,128)S(1)}, u32[]{:S(2)}, u32[]{:S(2)}) %collective-permute-start.6) | collective-permute-done | bytes 524320 | tf_op jit(solution)/shard_map/ppermute | solution.py:713
  60.3 0.0 collective-permute-done.2.refs_1_
  60.3 0.0 collective-permute-done.3.refs_2_
  60.3 0.0 copy-start
  60.3 13.6 %sweep.1 = f32[4,128,128]{2,1,0:T(8,128)S(1)} custom-call(bf16[128,128,256]{2,1,0:T(8,128)(2,1)S(1)} %get-tuple-element.33.analysis, bf16[128,128,256]{2,1,0:T(8,128)(2,1)S(1)} %get-tuple-element.34.synthesis, bf16[2,256,512]{2,1,0:T(8,128)(2,1)S(1)} %get-tuple-element.35.fourier, f32[64,128]{1,0:T(8,128)S(1)} %get-tuple-element.36.spread, ...), custom_call_target="tpu_custom_call" | custom-call | tf_op jit(solution)/shard_map/sweep/pallas_call | solution.py:639
  73.9 16.5 %all_to_all.5 = f32[32,16,128]{2,1,0:T(8,128)S(1)} all-to-all(f32[32,16,128]{2,1,0:T(8,128)S(1)} %bitcast.10), channel_id=1, replica_groups=mesh['tm'=4,'lev'=8] {'tm','lev'}, dimensions={0} | all-to-all | bytes 524288 | tf_op jit(solution)/shard_map/all_to_all | solution.py:746
  90.3 0.0 copy-done
  90.3 1.3 %mix.1 = f32[16,64,64]{2,1,0:T(8,128)} custom-call(f32[512,128]{1,0:T(8,128)S(1)} %bitcast.11, f32[64,64]{1,0:T(8,128)S(1)} %copy-done), custom_call_target="tpu_custom_call" | custom-call | tf_op jit(solution)/shard_map/mix/pallas_call | solution.py:691
Async XLA Ops:
  1.7 24.3 %collective-permute-start = (s32[1,16384]{1,0:T(1,128)}, s32[1,16384]{1,0:T(1,128)S(1)}, u32[]{:S(2)}, u32[]{:S(2)}) collective-permute-start(s32[1,16384]{1,0:T(1,128)} %cells.1), channel_id=1, source_target_pairs={{0,24},{8,16},{16,8},{24,0},{1,25},{9,17},{17,9},{25,1},{2,26},{10... | collective-permute-start | bytes 196616 | tf_op jit(solution)/shard_map/ppermute | solution.py:713
  4.2 22.0 %collective-permute-start.1 = (f32[2,16512]{1,0:T(2,128)S(1)}, f32[2,16512]{1,0:T(2,128)S(1)}, u32[]{:S(2)}, u32[]{:S(2)}) collective-permute-start(f32[2,16512]{1,0:T(2,128)S(1)} %get-tuple-element.31), channel_id=1, source_target_pairs={{0,24},{8,16},{16,8},{24,0},{1,25},{9,17},{17,9},{25,1},{2,26},{10... | collective-permute-start | bytes 396296 | tf_op jit(solution)/shard_map/ppermute | solution.py:713
  23.5 36.8 %collective-permute-start.2 = (f32[1032,128]{1,0:T(8,128)S(1)}, f32[1032,128]{1,0:T(8,128)S(1)}, u32[]{:S(2)}, u32[]{:S(2)}) collective-permute-start(f32[1032,128]{1,0:T(8,128)S(1)} %get-tuple-element.38), channel_id=1, source_target_pairs={{0,8},{8,0},{16,24},{24,16},{1,9},{9,1},{17,25},{25,17},{2,10},{10... | collective-permute-start | bytes 1585160 | tf_op jit(solution)/shard_map/ppermute | solution.py:713
  24.2 36.0 %collective-permute-start.3 = (f32[1032,128]{1,0:T(8,128)S(1)}, f32[1032,128]{1,0:T(8,128)S(1)}, u32[]{:S(2)}, u32[]{:S(2)}) collective-permute-start(f32[1032,128]{1,0:T(8,128)S(1)} %get-tuple-element.39), channel_id=1, source_target_pairs={{0,16},{8,24},{16,0},{24,8},{1,17},{9,25},{17,1},{25,9},{2,18},{10... | collective-permute-start | bytes 1585160 | tf_op jit(solution)/shard_map/ppermute | solution.py:713
  25.9 16.4 %collective-permute-start.4 = (f32[2,128,512]{2,1,0:T(8,128)S(1)}, f32[2,128,512]{2,1,0:T(8,128)S(1)}, u32[]{:S(2)}, u32[]{:S(2)}) collective-permute-start(f32[2,128,512]{2,1,0:T(8,128)S(1)} %get-tuple-element.42), channel_id=1, source_target_pairs={{0,8},{8,0},{16,24},{24,16},{1,9},{9,1},{17,25},{25,17},{2,10},{10... | collective-permute-start | bytes 1572872 | tf_op jit(solution)/shard_map/ppermute | solution.py:713
  26.0 24.3 %collective-permute-start.5 = (f32[2,128,512]{2,1,0:T(8,128)S(1)}, f32[2,128,512]{2,1,0:T(8,128)S(1)}, u32[]{:S(2)}, u32[]{:S(2)}) collective-permute-start(f32[2,128,512]{2,1,0:T(8,128)S(1)} %get-tuple-element.43), channel_id=1, source_target_pairs={{0,16},{8,24},{16,0},{24,8},{1,17},{9,25},{17,1},{25,9},{2,18},{10... | collective-permute-start | bytes 1572872 | tf_op jit(solution)/shard_map/ppermute | solution.py:713
  26.3 34.0 %collective-permute-start.6 = (f32[2,128,512]{2,1,0:T(8,128)S(1)}, f32[2,128,512]{2,1,0:T(8,128)S(1)}, u32[]{:S(2)}, u32[]{:S(2)}) collective-permute-start(f32[2,128,512]{2,1,0:T(8,128)S(1)} %get-tuple-element.44), channel_id=1, source_target_pairs={{0,24},{8,16},{16,8},{24,0},{1,25},{9,17},{17,9},{25,1},{2,26},{10... | collective-permute-start | bytes 1572872 | tf_op jit(solution)/shard_map/ppermute | solution.py:713
  60.3 30.1 %copy-start = (f32[64,64]{1,0:T(8,128)S(1)}, f32[64,64]{1,0:T(8,128)}, u32[]{:S(2)}) copy-start(f32[64,64]{1,0:T(8,128)} %vertical.1) | copy-start | bytes 49156
